TPU v7x, 256 devices: a whole 4x4x8 slice. The times are simulated.
256 devices in a mesh: row: 16 (over z, y_hi), col: 16 (over y_lo, x, core).
Axes of the slice: x: 4, y: 4 (y_hi: 2, y_lo: 2; y = y_hi * 2 + y_lo), z: 8, core: 2. Of those that a mesh axis runs over, the one named last changes fastest.
Arguments:
- inputs: bfloat16 [512, 8192], P('col', 'row'), may hold values from -6 to 6
- cotangent: bfloat16 [512, 8192], P('col', 'row'), may hold values from -1.59375 to 1.59375
- weight_in: bfloat16 [8192, 32768], P('row', 'col'), may hold values from -0.125 to 0.125
- weight_out: bfloat16 [32768, 8192], P('col', 'row'), may hold values from -0.0625 to 0.0625
- mask_in: int32 [64, 256], P('row', 'col'), may hold values 0 or 1
- mask_out: int32 [256, 64], P('col', 'row'), may hold values 0 or 1
Outputs:
- grad_inputs: float32 [512, 8192], P('col', 'row')
- grad_weight_in: float32 [8192, 32768], P('row', 'col')
- grad_weight_out: float32 [32768, 8192], P('col', 'row')
All inputs are finite; a program needn't handle non-finite values. No bound on the sum of `mask_in` or of `mask_out` on one device may be relied on, other than what follows from the above.
Results may differ from a plain program's by a relative error of at most 0.0029.
Values may be sent and summed in bfloat16 or wider, within the bound.
No kernel may reach another device: no remote copies, remote signals or barrier semaphores. Data moves between devices by JAX's collectives and lax.ppermute only.
A program may use at most 128 MiB of HBM per device.

v0:
```python
import jax
import jax.numpy as jnp
from jax import lax
from jax.sharding import PartitionSpec as P

BLOCK = 128


def spread(weight, mask):
    rows, cols = mask.shape
    blocks = weight.reshape(rows, BLOCK, cols, BLOCK) * mask.astype(weight.dtype)[:, None, :, None]
    return blocks.reshape(weight.shape)


def shards(inputs, cotangent, weight_in, weight_out, mask_in, mask_out):
    sparse_in = spread(weight_in, mask_in)
    sparse_out = spread(weight_out, mask_out)
    inputs_all, cotangent_all = (
        lax.all_gather(inputs, "col", axis=0, tiled=True),
        lax.all_gather(cotangent, "col", axis=0, tiled=True),
    )
    hidden_width = sparse_in.shape[1]
    first = jnp.dot(inputs_all, sparse_in, preferred_element_type=jnp.float32)
    second = lax.dot_general(
        cotangent_all, sparse_out, (((1,), (1,)), ((), ())), preferred_element_type=jnp.float32
    )
    summed = lax.psum_scatter(
        jnp.concatenate([first, second], axis=1), "row", scatter_dimension=0, tiled=True
    )
    pre = summed[:, :hidden_width]
    grad_act = summed[:, hidden_width:]
    sig = jax.nn.sigmoid(pre)
    act = (pre * sig).astype(jnp.bfloat16)
    activate_grad_pre = (grad_act * sig * (1.0 + pre * (1.0 - sig))).astype(jnp.bfloat16)
    act_share = act
    stacked = jnp.concatenate([act_share, activate_grad_pre], axis=1)
    joined = lax.all_gather(stacked, "row", axis=0, tiled=True)
    act = joined[:, :hidden_width]
    grad_pre = joined[:, hidden_width:]
    grad_inputs = lax.psum_scatter(
        lax.dot_general(
            grad_pre, sparse_in, (((1,), (1,)), ((), ())), preferred_element_type=jnp.float32
        ),
        "col",
        scatter_dimension=0,
        tiled=True,
    )
    grad_weight_in = lax.dot_general(
        inputs_all, grad_pre, (((0,), (0,)), ((), ())), preferred_element_type=jnp.float32
    )
    grad_weight_out = lax.dot_general(
        act, cotangent_all, (((0,), (0,)), ((), ())), preferred_element_type=jnp.float32
    )
    return (grad_inputs, spread(grad_weight_in, mask_in), spread(grad_weight_out, mask_out))


def solution(mesh):
    return jax.shard_map(
        shards,
        mesh=mesh,
        in_specs=(
            P("col", "row"),
            P("col", "row"),
            P("row", "col"),
            P("col", "row"),
            P("row", "col"),
            P("col", "row"),
        ),
        out_specs=(P("col", "row"), P("row", "col"), P("col", "row")),
        check_vma=False,
    )
```

profile of v0, /device:TPU:1, one launch (start us, length us, event | category | flops | bytes accessed | tf_op | source)
XLA Modules:
  0.0 460.7 jit_solution(2468672127989224259)
XLA Ops:
  7.2 0.0 reduce-scatter.7.cloned.1.call-start
  7.2 0.8 fusion.8
  8.0 22.7 %all_gather.9 = bf16[512,512]{1,0:T(8,128)(2,1)S(1)} all-gather(bf16[32,512]{1,0:T(8,128)(2,1)} %param.6), channel_id=1, replica_groups=mesh['row'=16,'col'=16] {'col'}, dimensions={0}, use_global_device_ids=true | all-gather | bytes 557056 | tf_op jit(solution)/shard_map/all_gather | solution.py:19
  30.7 0.8 fusion.7
  31.4 0.1 copy.19
  31.5 0.0 copy-start.3
  31.5 18.1 %all_gather.10 = bf16[512,512]{1,0:T(8,128)(2,1)S(1)} all-gather(bf16[32,512]{1,0:T(8,128)(2,1)} %param.7), channel_id=1, replica_groups=mesh['row'=16,'col'=16] {'col'}, dimensions={0}, use_global_device_ids=true | all-gather | bytes 557056 | tf_op jit(solution)/shard_map/all_gather | solution.py:20
  49.6 0.3 mul.56
  49.9 0.0 copy-done.3
  49.9 0.0 copy-start.2
  50.0 1.5 convolution_bitcast_fusion.1
  51.4 0.6 mul.59
  52.0 0.0 copy-done.2
  52.1 1.3 convolution_bitcast_fusion
  53.4 4.2 pad_maximum_fusion
  57.6 9.0 %copy.25 = f32[512,4096]{1,0:T(8,128)} copy(f32[512,4096]{0,1:T(8,128)} %pad_maximum_fusion) | data formatting | bytes 16777216
  66.6 0.0 reduce-scatter.7.cloned.1.call-update
  66.6 0.0 all-gather.2.cloned.1.call-start
  66.6 219.9 %reduce-scatter.7.cloned.1.call-done = f32[32,4096]{1,0:T(8,128)} async-done(((f32[512,4096]{1,0:T(8,128)}), f32[32,4096]{1,0:T(8,128)}) %reduce-scatter.7.cloned.1.call-update) | async-done | bytes 524304 | tf_op jit(solution)/shard_map/reduce_scatter | solution.py:27
  286.6 1.1 multiply_convert_fusion
  287.7 0.7 pad_maximum_fusion.1
  288.4 0.0 all-gather.2.cloned.1.call-update
  288.5 0.0 reduce-scatter.5.cloned.1.call-start
  288.5 100.5 %all-gather.2.cloned.1.call-done = bf16[512,4096]{1,0:T(8,128)(2,1)} async-done(((bf16[32,4096]{1,0:T(8,128)(2,1)}), bf16[512,4096]{1,0:T(8,128)(2,1)}) %all-gather.2.cloned.1.call-update) | async-done | bytes 4194320 | tf_op jit(solution)/shard_map/all_gather | solution.py:37
  389.0 4.5 fusion.3
  393.5 0.0 reduce-scatter.5.cloned.1.call-update
  393.5 0.1 copy.22
  393.6 0.1 copy.23
  393.7 0.0 copy-start
  393.7 0.6 mul.66
  394.3 1.6 copy-done
  395.9 3.3 bitcast_multiply_fusion.1
  399.2 5.3 %copy.24 = f32[512,2048]{1,0:T(8,128)} copy(f32[512,2048]{0,1:T(8,128)} %bitcast_multiply_fusion.1) | data formatting | bytes 8388608
  404.5 0.0 copy-start.1
  404.5 0.6 mul.69
  405.2 1.6 copy-done.1
  406.8 3.3 bitcast_multiply_fusion
  410.1 44.2 %reduce-scatter.5.cloned.1.call-done = f32[32,512]{1,0:T(8,128)} async-done(((f32[512,512]{1,0:T(8,128)}), f32[32,512]{1,0:T(8,128)}) %reduce-scatter.5.cloned.1.call-update) | async-done | bytes 65552 | tf_op jit(solution)/shard_map/reduce_scatter | solution.py:40
Async XLA Ops:
  7.2 279.4 %reduce-scatter.7.cloned.1.call-start = ((), (), s32[]{:S(2)}) async-start(), calls=%async_computation.4 | async-start | bytes 8912896 | tf_op jit(solution)/shard_map/reduce_scatter | solution.py:27
  31.5 18.4 %copy-start.3 = (bf16[512,2048]{1,0:T(8,128)(2,1)S(1)}, bf16[512,2048]{1,0:T(8,128)(2,1)}, u32[]{:S(2)}) copy-start(bf16[512,2048]{1,0:T(8,128)(2,1)} %param.8) | copy-start | bytes 6291460
  49.9 2.1 copy-start.2
  66.6 322.4 %all-gather.2.cloned.1.call-start = ((), (), s32[]{:S(2)}) async-start(), calls=%async_computation.2 | async-start | bytes 4456448 | tf_op jit(solution)/shard_map/all_gather | solution.py:37
  288.5 165.8 %reduce-scatter.5.cloned.1.call-start = ((), (), s32[]{:S(2)}) async-start(), calls=%async_computation.3 | async-start | bytes 1114112 | tf_op jit(solution)/shard_map/reduce_scatter | solution.py:40
  393.7 2.2 copy-start
  404.5 2.2 copy-start.1
Sparse Core Ops, SparseCore 0:
  66.7 219.8 reduce-scatter.6
  289.7 99.2 all-gather.1
  393.6 60.5 reduce-scatter.4
where the time goes:
time: 463 us; the launch traced here: 461 us
  waiting for transfers between devices  365 us (79%)
  blocking collectives  40.8 us (9%)
  local copies, waits for them, and re-layouts  19.9 us (4%)
  matrix products  13.9 us (3%)
  between operations  13.8 us (3%)
  other arithmetic  7.61 us (2%)
    reduce_scatter x1, waiting for transfers between devices, shards(): lax.psum_scatter(jnp.concatenate([first, second], axis=1), 'row', scatter...  220 us
    all_gather x1, waiting for transfers between devices, shards(): joined = lax.all_gather(stacked, 'row', axis=0, tiled=True)  100 us
    reduce_scatter x1, waiting for transfers between devices, shards(): lax.psum_scatter(lax.dot_general(grad_pre, sparse_in, (((1,), (1,)), ((),...  44.2 us
    all_gather x1, blocking collectives, shards(): lax.all_gather(inputs, 'col', axis=0, tiled=True)  22.7 us
    all_gather x1, blocking collectives, shards(): lax.all_gather(cotangent, 'col', axis=0, tiled=True)  18.1 us
    unnamed x10, local copies, waits for them, and re-layouts  17.5 us
  transfers between devices with their start and end apart: 3, of which 3 were waited for; matrix products, arithmetic and copies ran while one was open for 3% of the time, Pallas kernels for 0%

commit v1 on v0

v1 whole, which is shorter than its diff:
```python
import jax
import jax.numpy as jnp
from jax import lax
from jax.experimental import pallas as pl
from jax.experimental.pallas import tpu as pltpu
from jax.sharding import PartitionSpec as P

BLOCK = 128
F16 = jnp.float16
BF16 = jnp.bfloat16
F32 = jnp.float32
PRE_SCALE = 8.0
ACT_SCALE = 64.0


def spread(weight, mask):
    rows, cols = mask.shape
    blocks = weight.reshape(rows, BLOCK, cols, BLOCK) * mask.astype(weight.dtype)[:, None, :, None]
    return blocks.reshape(weight.shape)


def ring(shift, rows):
    return [(r, (r + 2 * shift) % rows) for r in range(rows)]


def send(value, shift, rows):
    return lax.ppermute(value, "row", ring(shift, rows))


def swap(value, rows):
    return lax.ppermute(value, "row", [(r, r ^ 1) for r in range(rows)])


def together(*values):
    return lax.optimization_barrier(values)


def chunk_of(stack, index):
    return lax.dynamic_index_in_dim(stack, index % stack.shape[0], 0, keepdims=False)


def gather_kernel(place, *refs):
    depth = len(refs) - 4
    chunks, (weight, stack, pieces, sems) = refs[:depth], refs[depth:]
    z, core = place[0], place[1]
    copies = [
        pltpu.make_async_copy(chunks[d], stack.at[lax.rem(z + d, depth)], sems.at[d])
        for d in range(depth)
    ]
    for copy in copies:
        copy.start()
    for copy in copies:
        copy.wait()
    cols, share, width = pieces.shape
    per_half = depth // 2
    for half in range(2):
        rows = stack[half * per_half : (half + 1) * per_half]
        rows = rows.reshape(per_half * rows.shape[1], rows.shape[2])
        product = lax.dot_general(
            rows, weight[...], (((1,), (1,)), ((), ())), preferred_element_type=F32
        )
        product = product.astype(BF16).reshape(cols // 2, share, width)
        side = core if half == 0 else 1 - core
        for k in range(cols // 2):
            pieces[2 * k + side] = product[k]


def gather_and_multiply(chunks, weight, place, cols):
    depth = len(chunks)
    chunk, hidden = chunks[0].shape
    features = weight.shape[0]
    tokens = depth * chunk
    whole = lambda shape: pl.BlockSpec(shape, lambda i, p: (0,) * len(shape))
    stack, pieces = pl.pallas_call(
        gather_kernel,
        out_shape=(
            jax.ShapeDtypeStruct((depth, chunk, hidden), BF16),
            jax.ShapeDtypeStruct((cols, tokens // cols, features), BF16),
        ),
        grid_spec=pltpu.PrefetchScalarGridSpec(
            num_scalar_prefetch=1,
            grid=(1,),
            in_specs=[pl.BlockSpec(memory_space=pl.ANY)] * depth + [whole(weight.shape)],
            out_specs=(whole((depth, chunk, hidden)), whole((cols, tokens // cols, features))),
            scratch_shapes=[pltpu.SemaphoreType.DMA((depth,))],
        ),
        cost_estimate=pl.CostEstimate(
            flops=2 * tokens * hidden * features, bytes_accessed=8 * tokens * hidden, transcendentals=0
        ),
    )(place, *chunks, weight)
    return stack.reshape(tokens, hidden), pieces


def weight_in_kernel(mask, x, grad, out):
    tile = pl.program_id(0)
    product = lax.dot_general(
        x[...], grad[...], (((0,), (0,)), ((), ())), preferred_element_type=F32
    )
    for i in range(out.shape[0] // BLOCK):
        for j in range(out.shape[1] // BLOCK):
            keep = mask[i, tile * (out.shape[1] // BLOCK) + j].astype(F32)
            at = (slice(i * BLOCK, (i + 1) * BLOCK), slice(j * BLOCK, (j + 1) * BLOCK))
            out[at] = product[at] * keep


def grad_of_weight_in(x, grad, mask, width=512):
    tokens, features = x.shape
    hidden = grad.shape[1]
    return pl.pallas_call(
        weight_in_kernel,
        out_shape=jax.ShapeDtypeStruct((features, hidden), F32),
        grid=(hidden // width,),
        in_specs=[
            pl.BlockSpec(memory_space=pltpu.SMEM),
            pl.BlockSpec((tokens, features), lambda i: (0, 0)),
            pl.BlockSpec((tokens, width), lambda i: (0, i)),
        ],
        out_specs=pl.BlockSpec((features, width), lambda i: (0, i)),
        cost_estimate=pl.CostEstimate(
            flops=2 * tokens * hidden * features, bytes_accessed=8 * features * hidden, transcendentals=0
        ),
    )(mask, x, grad)


def weight_out_kernel(place, *refs):
    depth = len(refs) - 5
    chunks, (mask, cot, out, stack, sems) = refs[:depth], refs[depth:]
    tile = pl.program_id(0)
    z = place[0]

    @pl.when(tile == 0)
    def _():
        copies = [
            pltpu.make_async_copy(chunks[d], stack.at[lax.rem(z + d, depth)], sems.at[d])
            for d in range(depth)
        ]
        for copy in copies:
            copy.start()
        for copy in copies:
            copy.wait()

    height = out.shape[0]
    act = stack[:, :, pl.ds(pl.multiple_of(tile * height, BLOCK), height)]
    act = act.reshape(depth * act.shape[1], height)
    product = lax.dot_general(
        act, cot[...], (((0,), (0,)), ((), ())), preferred_element_type=F32
    )
    for i in range(height // BLOCK):
        for j in range(out.shape[1] // BLOCK):
            keep = mask[tile * (height // BLOCK) + i, j].astype(F32)
            at = (slice(i * BLOCK, (i + 1) * BLOCK), slice(j * BLOCK, (j + 1) * BLOCK))
            out[at] = product[at] * keep


def grad_of_weight_out(chunks, cot, mask, place, height=512):
    depth = len(chunks)
    chunk, hidden = chunks[0].shape
    tokens, features = cot.shape
    return pl.pallas_call(
        weight_out_kernel,
        out_shape=jax.ShapeDtypeStruct((hidden, features), F32),
        grid_spec=pltpu.PrefetchScalarGridSpec(
            num_scalar_prefetch=1,
            grid=(hidden // height,),
            in_specs=[pl.BlockSpec(memory_space=pl.ANY)] * depth
            + [
                pl.BlockSpec(memory_space=pltpu.SMEM),
                pl.BlockSpec((tokens, features), lambda i, p: (0, 0)),
            ],
            out_specs=pl.BlockSpec((height, features), lambda i, p: (i, 0)),
            scratch_shapes=[
                pltpu.VMEM((depth, chunk, hidden), BF16),
                pltpu.SemaphoreType.DMA((depth,)),
            ],
        ),
        cost_estimate=pl.CostEstimate(
            flops=2 * tokens * hidden * features, bytes_accessed=8 * features * hidden, transcendentals=0
        ),
    )(place, *chunks, mask, cot)


def shards(rows, cols, inputs, cotangent, weight_in, weight_out, mask_in, mask_out):
    share, width = inputs.shape
    chips = cols // 2
    tokens = share * cols
    depth = rows // 2
    far = depth // 2
    same_core = [[2 * k + i for k in range(chips)] for i in range(2)]
    other_core = [(c, c ^ 1) for c in range(cols)]
    z = lax.axis_index("row") // 2
    place = jnp.stack([z, lax.axis_index("col") % 2]).astype(jnp.int32)

    both = jnp.concatenate([inputs, cotangent], axis=1)
    both = jnp.broadcast_to(both[None], (chips, share, 2 * width))
    mine = lax.all_to_all(both, "col", 0, 0, axis_index_groups=same_core)
    both = jnp.concatenate([mine, lax.ppermute(mine, "col", other_core)], axis=0)
    both = both.reshape(tokens, 2 * width)
    inputs_all, cotangent_all = both[:, :width], both[:, width:]
    sparse_in, sparse_out = together(spread(weight_in, mask_in), spread(weight_out, mask_out))
    pre_part = jnp.dot(inputs_all, sparse_in, preferred_element_type=F32)
    act_part = lax.dot_general(
        cotangent_all, sparse_out, (((1,), (1,)), ((), ())), preferred_element_type=F32
    )
    pre_part = pre_part.reshape(depth, tokens // depth, -1)
    act_part = act_part.reshape(depth, tokens // depth, -1)
    inputs_all, cotangent_all = together(inputs_all, cotangent_all)

    def p(d):
        return chunk_of(pre_part, z + d) * PRE_SCALE

    def g(d):
        return chunk_of(act_part, z + d + depth) * ACT_SCALE

    pu, pd = p(far).astype(F16), p(depth - far + 1).astype(F16)
    gu, gd = g(far - 1).astype(F16), g(-far).astype(F16)
    for step in range(1, far):
        pu, pd = together(send(pu, 1, rows), send(pd, -1, rows))
        pu = (p(far - step) + pu.astype(F32)).astype(F16)
        if step < far - 1:
            pd = (p(depth - far + 1 + step) + pd.astype(F32)).astype(F16)
        gu, gd = together(send(gu, 1, rows), send(gd, -1, rows))
        if step < far - 1:
            gu = (g(far - 1 - step) + gu.astype(F32)).astype(F16)
        gd = (g(-far + step) + gd.astype(F32)).astype(F16)
    pu = send(pu, 1, rows)
    gd = send(gd, -1, rows)
    pre = (p(0) + pu.astype(F32) + pd.astype(F32)).astype(F16)
    pre = (pre.astype(F32) + swap(pre, rows).astype(F32)) * (1.0 / PRE_SCALE)
    grad_act = (g(0) + gu.astype(F32) + gd.astype(F32)).astype(F16)
    grad_act = (grad_act.astype(F32) + swap(grad_act, rows).astype(F32)) * (1.0 / ACT_SCALE)
    sig = jax.nn.sigmoid(pre)
    act = (pre * sig).astype(BF16)
    grad_pre = (grad_act * sig * (1.0 + pre * (1.0 - sig))).astype(BF16)

    acts, grads = {0: act}, {0: grad_pre}
    au = ad = act
    gu = gd = grad_pre
    for step in range(1, far + 1):
        au = acts[depth - step] = send(au, 1, rows)
        if step < far:
            ad = acts[step] = send(ad, -1, rows)
            gu = grads[depth - step] = send(gu, 1, rows)
        gd = grads[step] = send(gd, -1, rows)
    acts = [acts[d] for d in range(depth)]
    grads = [grads[d] for d in range(depth)]

    grad_pre, pieces = gather_and_multiply(grads, sparse_in, place, cols)
    pieces = lax.all_to_all(pieces, "col", 0, 0)
    grad_inputs = jnp.sum(pieces.astype(F32), axis=0)
    grad_weight_in = grad_of_weight_in(inputs_all, grad_pre, mask_in)
    grad_weight_out = grad_of_weight_out(acts, cotangent_all, mask_out, place)
    return (grad_inputs, grad_weight_in, grad_weight_out)


def solution(mesh):
    rows, cols = mesh.shape["row"], mesh.shape["col"]
    return jax.shard_map(
        lambda *args: shards(rows, cols, *args),
        mesh=mesh,
        in_specs=(
            P("col", "row"),
            P("col", "row"),
            P("row", "col"),
            P("col", "row"),
            P("row", "col"),
            P("col", "row"),
        ),
        out_specs=(P("col", "row"), P("row", "col"), P("col", "row")),
        check_vma=False,
    )
```

time: 463 us -> 152 us (0.33)
  waiting for transfers between devices: 365 us -> 57.9 us
  starting transfers between devices: 0.12 us -> 58.1 us
  blocking collectives: 40.8 us -> 0 us
  Pallas kernels: 0 us -> 17.9 us
  local copies, waits for them, and re-layouts: 19.9 us -> 5.34 us
  between operations: 13.8 us -> 1.02 us
  matrix products: 13.9 us -> 2.54 us
    reduce_scatter x2 -> x0, waiting for transfers between devices: 264 us -> none  [the longest x1 220 us: shards(): lax.psum_scatter(jnp.concatenate([first, second], axis=1), 'row', scatter...]
    all_gather x1 -> x0, waiting for transfers between devices: 100 us -> none  [shards(): joined = lax.all_gather(stacked, 'row', axis=0, tiled=True)]
    ppermute x0 -> x31, waiting for transfers between devices: none -> 50 us  [the longest x28 44.8 us: send(): return lax.ppermute(value, 'row', ring(shift, rows))]
    ppermute x0 -> x31, starting transfers between devices: none -> 40.9 us  [the longest x28 34.6 us: send(): return lax.ppermute(value, 'row', ring(shift, rows))]
    all_gather x2 -> x0, blocking collectives: 40.8 us -> none  [the longest x1 22.7 us: shards(): lax.all_gather(inputs, 'col', axis=0, tiled=True)]
    pallas_call x0 -> x3, Pallas kernels: none -> 17.9 us  [the longest x1 6.81 us: grad_of_weight_out(): pl.pallas_call(weight_out_kernel, out_shape=jax.ShapeDtypeStruct((hidden,...]
    all_to_all x0 -> x2, starting transfers between devices: none -> 17.2 us  [the longest x1 11.4 us: shards(): pieces = lax.all_to_all(pieces, 'col', 0, 0)]
    unnamed x10 -> x37, local copies, waits for them, and re-layouts: 17.5 us -> 2.39 us
  transfers between devices with their start and end apart: 3 -> 33, of which waited for: 3 -> 23; matrix products, arithmetic and copies ran while one was open for 3% -> 5% of each run, Pallas kernels for 0% -> 12%
where the time goes in v1:
time: 152 us; the launch traced here: 151 us
  starting transfers between devices  58.1 us (38%)
  waiting for transfers between devices  57.9 us (38%)
  Pallas kernels  17.9 us (12%)
  other arithmetic  8.15 us (5%)
  local copies, waits for them, and re-layouts  5.34 us (4%)
  matrix products  2.54 us (2%)
    ppermute x28, waiting for transfers between devices, send(): return lax.ppermute(value, 'row', ring(shift, rows))  44.8 us
    ppermute x28, starting transfers between devices, send(): return lax.ppermute(value, 'row', ring(shift, rows))  34.6 us
    all_to_all x1, starting transfers between devices, shards(): pieces = lax.all_to_all(pieces, 'col', 0, 0)  11.4 us
    all_to_all x1, waiting for transfers between devices, shards(): mine = lax.all_to_all(both, 'col', 0, 0, axis_index_groups=same_core)  7.84 us
    pallas_call x1, Pallas kernels, grad_of_weight_out(): pl.pallas_call(weight_out_kernel, out_shape=jax.ShapeDtypeStruct((hidden,...  6.81 us
    pallas_call x1, Pallas kernels, gather_and_multiply(): pl.pallas_call(gather_kernel, out_shape=(jax.ShapeDtypeStruct((depth, chu...  5.92 us
    all_to_all x1, starting transfers between devices, shards(): mine = lax.all_to_all(both, 'col', 0, 0, axis_index_groups=same_core)  5.86 us
    ppermute x2, starting transfers between devices, swap(): return lax.ppermute(value, 'row', [(r, r ^ 1) for r in range(rows)])  5.41 us
  transfers between devices with their start and end apart: 33, of which 23 were waited for; matrix products, arithmetic and copies ran while one was open for 5% of the time, Pallas kernels for 12%

profile of v1, /device:TPU:1, one launch (start us, length us, event | category | flops | bytes accessed | tf_op | source)
XLA Modules:
  0.0 150.9 jit_solution(17428074770988769844)
XLA Ops:
  0.7 0.9 pad_maximum_fusion.1
  1.6 0.9 broadcast_in_dim.2
  2.4 5.9 %all-to-all-start = ((bf16[8,32,1024]{2,1,0:T(8,128)(2,1)}), bf16[8,32,1024]{2,1,0:T(8,128)(2,1)S(1)}, u32[]{:S(2)}, u32[]{:S(2)}) async-start(bf16[8,32,1024]{2,1,0:T(8,128)(2,1)} %broadcast_in_dim.2), calls=%async_computation | async-start | bytes 1048576 | tf_op jit(solution)/shard_map/all_to_all | solution.py:195
  8.4 0.6 mul.137
  9.1 1.6 %bitcast_multiply_fusion = bf16[2048,512]{1,0:T(8,128)(2,1)} fusion(bf16[2048,512]{1,0:T(8,128)(2,1)S(1)} %copy-done.2, bf16[256,8,4,128]{3,2,1,0:T(4,128)(2,1)S(1)} %bitcast.89), kind=kLoop, calls=%fused_computation | loop fusion | flops 1048576 | bytes 6291456 | tf_op jit(solution)/shard_map/mul | solution.py:18
  10.7 7.8 %all-to-all-done = bf16[8,32,1024]{2,1,0:T(8,128)(2,1)S(1)} async-done(((bf16[8,32,1024]{2,1,0:T(8,128)(2,1)}), bf16[8,32,1024]{2,1,0:T(8,128)(2,1)S(1)}, u32[]{:S(2)}, u32[]{:S(2)}) %all-to-all-start) | async-done | bytes 524320 | tf_op jit(solution)/shard_map/all_to_all | solution.py:195
  18.5 0.8 collective-permute-start
  19.4 0.3 mul.134
  19.7 0.6 copy-done.3
  20.3 0.5 bitcast_multiply_fusion.1.refs_8_
  21.0 2.1 %pad_maximum_fusion = bf16[16,32,1024]{2,1,0:T(8,128)(2,1)S(1)} fusion(bf16[8,32,1024]{2,1,0:T(8,128)(2,1)} %collective-permute-done, bf16[8,32,1024]{2,1,0:T(8,128)(2,1)} %copy-done.4), kind=kLoop, calls=%fused_computation.2 | loop fusion | flops 524288 | bytes 2097152 | tf_op jit(solution)/shard_map/concatenate | solution.py:196
  23.1 0.3 copy-done.1
  23.4 1.3 fusion.20
  24.8 5.7 %collective-permute-start.2 = (f16[64,2048]{1,0:T(8,128)(2,1)S(1)}, f16[64,2048]{1,0:T(8,128)(2,1)S(1)}, u32[]{:S(2)}, u32[]{:S(2)}) collective-permute-start(f16[64,2048]{1,0:T(8,128)(2,1)S(1)} %get-tuple-element.49), channel_id=1, source_target_pairs={{0,224},{16,240},{32,0},{48,16},{64,32},{80,48},{96,64},{112,80},{... | collective-permute-start | bytes 786440 | tf_op jit(solution)/shard_map/ppermute | solution.py:27
  30.5 1.3 fusion.18
  31.9 2.7 %collective-permute-start.10 = (f16[64,2048]{1,0:T(8,128)(2,1)S(1)}, f16[64,2048]{1,0:T(8,128)(2,1)S(1)}, u32[]{:S(2)}, u32[]{:S(2)}) collective-permute-start(f16[64,2048]{1,0:T(8,128)(2,1)S(1)} %get-tuple-element.43), channel_id=1, source_target_pairs={{0,224},{16,240},{32,0},{48,16},{64,32},{80,48},{96,64},{112,80},{... | collective-permute-start | bytes 786440 | tf_op jit(solution)/shard_map/ppermute | solution.py:27
  34.6 0.6 collective-permute-done.2
  35.3 3.1 %collective-permute-done.1 = f16[64,2048]{1,0:T(8,128)(2,1)S(1)} collective-permute-done((f16[64,2048]{1,0:T(8,128)(2,1)S(1)}, f16[64,2048]{1,0:T(8,128)(2,1)S(1)}, u32[]{:S(2)}, u32[]{:S(2)}) %collective-permute-start.1) | collective-permute-done | bytes 262176 | tf_op jit(solution)/shard_map/ppermute | solution.py:27
  38.5 0.4 collective-permute-start.4
  38.9 1.2 collective-permute-start.3
  40.1 0.8 collective-permute-done.10
  40.9 3.3 %collective-permute-done.9 = f16[64,2048]{1,0:T(8,128)(2,1)S(1)} collective-permute-done((f16[64,2048]{1,0:T(8,128)(2,1)S(1)}, f16[64,2048]{1,0:T(8,128)(2,1)S(1)}, u32[]{:S(2)}, u32[]{:S(2)}) %collective-permute-start.9) | collective-permute-done | bytes 262176 | tf_op jit(solution)/shard_map/ppermute | solution.py:27
  44.2 0.2 fusion.1
  44.6 1.4 collective-permute-start.11
  45.9 0.6 collective-permute-done.4
  46.5 3.3 %collective-permute-done.3 = f16[64,2048]{1,0:T(8,128)(2,1)S(1)} collective-permute-done((f16[64,2048]{1,0:T(8,128)(2,1)S(1)}, f16[64,2048]{1,0:T(8,128)(2,1)S(1)}, u32[]{:S(2)}, u32[]{:S(2)}) %collective-permute-start.3) | collective-permute-done | bytes 262176 | tf_op jit(solution)/shard_map/ppermute | solution.py:27
  49.8 0.2 fusion.8
  50.0 0.3 collective-permute-start.6
  50.4 1.4 collective-permute-start.5
  51.8 0.4 collective-permute-done.12
  52.1 3.3 %collective-permute-done.11 = f16[64,2048]{1,0:T(8,128)(2,1)S(1)} collective-permute-done((f16[64,2048]{1,0:T(8,128)(2,1)S(1)}, f16[64,2048]{1,0:T(8,128)(2,1)S(1)}, u32[]{:S(2)}, u32[]{:S(2)}) %collective-permute-start.11) | collective-permute-done | bytes 262176 | tf_op jit(solution)/shard_map/ppermute | solution.py:27
  55.8 1.4 collective-permute-start.13
  57.2 0.6 collective-permute-done.6
  57.7 3.3 %collective-permute-done.5 = f16[64,2048]{1,0:T(8,128)(2,1)S(1)} collective-permute-done((f16[64,2048]{1,0:T(8,128)(2,1)S(1)}, f16[64,2048]{1,0:T(8,128)(2,1)S(1)}, u32[]{:S(2)}, u32[]{:S(2)}) %collective-permute-start.5) | collective-permute-done | bytes 262176 | tf_op jit(solution)/shard_map/ppermute | solution.py:27
  61.3 2.0 %collective-permute-done.14 = f16[64,2048]{1,0:T(8,128)(2,1)S(1)} collective-permute-done((f16[64,2048]{1,0:T(8,128)(2,1)S(1)}, f16[64,2048]{1,0:T(8,128)(2,1)S(1)}, u32[]{:S(2)}, u32[]{:S(2)}) %collective-permute-start.14) | collective-permute-done | bytes 262176 | tf_op jit(solution)/shard_map/ppermute | solution.py:27
  63.3 3.3 %collective-permute-done.13 = f16[64,2048]{1,0:T(8,128)(2,1)S(1)} collective-permute-done((f16[64,2048]{1,0:T(8,128)(2,1)S(1)}, f16[64,2048]{1,0:T(8,128)(2,1)S(1)}, u32[]{:S(2)}, u32[]{:S(2)}) %collective-permute-start.13) | collective-permute-done | bytes 262176 | tf_op jit(solution)/shard_map/ppermute | solution.py:27
  66.9 2.1 %collective-permute-done.7 = f16[64,2048]{1,0:T(8,128)(2,1)S(1)} collective-permute-done((f16[64,2048]{1,0:T(8,128)(2,1)S(1)}, f16[64,2048]{1,0:T(8,128)(2,1)S(1)}, u32[]{:S(2)}, u32[]{:S(2)}) %collective-permute-start.7) | collective-permute-done | bytes 262176 | tf_op jit(solution)/shard_map/ppermute | solution.py:27
  69.1 2.7 %collective-permute-start.8 = (f16[64,2048]{1,0:T(8,128)(2,1)S(1)}, f16[64,2048]{1,0:T(8,128)(2,1)S(1)}, u32[]{:S(2)}, u32[]{:S(2)}) collective-permute-start(f16[64,2048]{1,0:T(8,128)(2,1)S(1)} %fusion.13), channel_id=1, source_target_pairs={{0,16},{16,0},{32,48},{48,32},{64,80},{80,64},{96,112},{112,96},{1... | collective-permute-start | bytes 786440 | tf_op jit(solution)/shard_map/ppermute | solution.py:31
  71.8 2.2 %collective-permute-done.15 = f16[64,2048]{1,0:T(8,128)(2,1)S(1)} collective-permute-done((f16[64,2048]{1,0:T(8,128)(2,1)S(1)}, f16[64,2048]{1,0:T(8,128)(2,1)S(1)}, u32[]{:S(2)}, u32[]{:S(2)}) %collective-permute-start.15) | collective-permute-done | bytes 262176 | tf_op jit(solution)/shard_map/ppermute | solution.py:27
  74.2 2.7 %collective-permute-start.16 = (f16[64,2048]{1,0:T(8,128)(2,1)S(1)}, f16[64,2048]{1,0:T(8,128)(2,1)S(1)}, u32[]{:S(2)}, u32[]{:S(2)}) collective-permute-start(f16[64,2048]{1,0:T(8,128)(2,1)S(1)} %fusion.6), channel_id=1, source_target_pairs={{0,16},{16,0},{32,48},{48,32},{64,80},{80,64},{96,112},{112,96},{1... | collective-permute-start | bytes 786440 | tf_op jit(solution)/shard_map/ppermute | solution.py:31
  76.9 5.0 %collective-permute-done.16 = f16[64,2048]{1,0:T(8,128)(2,1)S(1)} collective-permute-done((f16[64,2048]{1,0:T(8,128)(2,1)S(1)}, f16[64,2048]{1,0:T(8,128)(2,1)S(1)}, u32[]{:S(2)}, u32[]{:S(2)}) %collective-permute-start.16) | collective-permute-done | bytes 262176 | tf_op jit(solution)/shard_map/ppermute | solution.py:31
  81.9 0.4 multiply_convert_fusion
  82.3 3.9 %collective-permute-start.17 = (bf16[64,2048]{1,0:T(8,128)(2,1)S(1)}, bf16[64,2048]{1,0:T(8,128)(2,1)S(1)}, u32[]{:S(2)}, u32[]{:S(2)}) collective-permute-start(bf16[64,2048]{1,0:T(8,128)(2,1)S(1)} %get-tuple-element.54.refs_0_), channel_id=1, source_target_pairs={{0,224},{16,240},{32,0},{48,16},{64,32},{80,48},{96,64},{112,80},{... | collective-permute-start | bytes 786440 | tf_op jit(solution)/shard_map/ppermute | solution.py:27
  86.2 3.3 %collective-permute-done.17.refs_1_ = bf16[64,2048]{1,0:T(8,128)(2,1)S(1)} collective-permute-done((bf16[64,2048]{1,0:T(8,128)(2,1)S(1)}, bf16[64,2048]{1,0:T(8,128)(2,1)S(1)}, u32[]{:S(2)}, u32[]{:S(2)}) %collective-permute-start.17) | collective-permute-done | bytes 262176 | tf_op jit(solution)/shard_map/ppermute | solution.py:27
  89.5 3.1 %collective-permute-start.18 = (bf16[64,2048]{1,0:T(8,128)(2,1)S(1)}, bf16[64,2048]{1,0:T(8,128)(2,1)S(1)}, u32[]{:S(2)}, u32[]{:S(2)}) collective-permute-start(bf16[64,2048]{1,0:T(8,128)(2,1)S(1)} %collective-permute-done.17.refs_1_), channel_id=1, source_target_pairs={{0,224},{16,240},{32,0},{48,16},{64,32},{80,48},{96,64},{112,80},{... | collective-permute-start | bytes 786440 | tf_op jit(solution)/shard_map/ppermute | solution.py:27
  92.8 3.2 %collective-permute-done.18.refs_2_ = bf16[64,2048]{1,0:T(8,128)(2,1)S(1)} collective-permute-done((bf16[64,2048]{1,0:T(8,128)(2,1)S(1)}, bf16[64,2048]{1,0:T(8,128)(2,1)S(1)}, u32[]{:S(2)}, u32[]{:S(2)}) %collective-permute-start.18) | collective-permute-done | bytes 262176 | tf_op jit(solution)/shard_map/ppermute | solution.py:27
  96.0 3.1 %collective-permute-start.19 = (bf16[64,2048]{1,0:T(8,128)(2,1)S(1)}, bf16[64,2048]{1,0:T(8,128)(2,1)}, u32[]{:S(2)}, u32[]{:S(2)}) collective-permute-start(bf16[64,2048]{1,0:T(8,128)(2,1)S(1)} %collective-permute-done.18.refs_2_), channel_id=1, source_target_pairs={{0,224},{16,240},{32,0},{48,16},{64,32},{80,48},{96,64},{112,80},{... | collective-permute-start | bytes 786440 | tf_op jit(solution)/shard_map/ppermute | solution.py:27
  99.1 1.4 collective-permute-start.28
  100.6 2.6 %collective-permute-done.22.refs_6_ = bf16[64,2048]{1,0:T(8,128)(2,1)} collective-permute-done((bf16[64,2048]{1,0:T(8,128)(2,1)S(1)}, bf16[64,2048]{1,0:T(8,128)(2,1)}, u32[]{:S(2)}, u32[]{:S(2)}) %collective-permute-start.22) | collective-permute-done | bytes 262176 | tf_op jit(solution)/shard_map/ppermute | solution.py:27
  103.2 3.1 %collective-permute-start.20 = (bf16[64,2048]{1,0:T(8,128)(2,1)}, bf16[64,2048]{1,0:T(8,128)(2,1)}, u32[]{:S(2)}, u32[]{:S(2)}) collective-permute-start(bf16[64,2048]{1,0:T(8,128)(2,1)} %collective-permute-done.19.refs_3_), channel_id=1, source_target_pairs={{0,224},{16,240},{32,0},{48,16},{64,32},{80,48},{96,64},{112,80},{... | collective-permute-start | bytes 786440 | tf_op jit(solution)/shard_map/ppermute | solution.py:27
  106.3 3.3 %collective-permute-start.25 = (bf16[64,2048]{1,0:T(8,128)(2,1)S(1)}, bf16[64,2048]{1,0:T(8,128)(2,1)S(1)}, u32[]{:S(2)}, u32[]{:S(2)}) collective-permute-start(bf16[64,2048]{1,0:T(8,128)(2,1)S(1)} %collective-permute-done.24.refs_1_), channel_id=1, source_target_pairs={{0,224},{16,240},{32,0},{48,16},{64,32},{80,48},{96,64},{112,80},{... | collective-permute-start | bytes 786440 | tf_op jit(solution)/shard_map/ppermute | solution.py:27
  109.6 0.6 pad_add_fusion.place
  110.2 4.4 %collective-permute-done.23.refs_5_ = bf16[64,2048]{1,0:T(8,128)(2,1)} collective-permute-done((bf16[64,2048]{1,0:T(8,128)(2,1)}, bf16[64,2048]{1,0:T(8,128)(2,1)}, u32[]{:S(2)}, u32[]{:S(2)}) %collective-permute-start.23) | collective-permute-done | bytes 262176 | tf_op jit(solution)/shard_map/ppermute | solution.py:27
  114.7 5.9 %shard_map.85 = (bf16[8,64,2048]{2,1,0:T(8,128)(2,1)}, bf16[16,32,512]{2,1,0:T(8,128)(2,1)}) custom-call(s32[2]{0:T(128)} %pad_add_fusion.place, bf16[64,2048]{1,0:T(8,128)(2,1)} %copy-done.6, bf16[64,2048]{1,0:T(8,128)(2,1)} %copy-done.10, bf16[64,2048]{1,0:T(8,128)(2,1)} %copy-done.12, bf16[64,2048]{1,0:T(8,128)(2,1)} %collective-permute-done.19.refs_3_, ...), custom_call_target="tpu_custom_call" | custom-call | flops 1073741824 | bytes 8388608 | tf_op jit(solution)/shard_map/pallas_call | solution.py:74
  120.6 11.4 %all-to-all-start.1 = ((bf16[16,32,512]{2,1,0:T(8,128)(2,1)}), bf16[16,32,512]{2,1,0:T(8,128)(2,1)S(1)}, u32[]{:S(2)}, u32[]{:S(2)}) async-start(bf16[16,32,512]{2,1,0:T(8,128)(2,1)} %get-tuple-element.35), calls=%async_computation.1 | async-start | bytes 1048576 | tf_op jit(solution)/shard_map/all_to_all | solution.py:248
  132.0 0.7 copy.10.refs_8_
  132.7 1.2 collective-permute-start.26
  133.9 0.3 collective-permute-start.30
  134.2 1.1 fusion.22
  135.3 5.2 %shard_map.86 = f32[512,2048]{1,0:T(8,128)} custom-call(s32[4,16]{1,0:T(4,128)} %mask.1, bf16[512,512]{1,0:T(8,128)(2,1)} %get-tuple-element.36.x, bf16[512,2048]{1,0:T(8,128)(2,1)} %bitcast.91), custom_call_target="tpu_custom_call" | custom-call | flops 1073741824 | bytes 8388608 | tf_op jit(solution)/shard_map/pallas_call | solution.py:109
  140.6 2.1 %collective-permute-done.30.refs_4_ = bf16[64,2048]{1,0:T(8,128)(2,1)S(1)} collective-permute-done((bf16[64,2048]{1,0:T(8,128)(2,1)}, bf16[64,2048]{1,0:T(8,128)(2,1)S(1)}, u32[]{:S(2)}, u32[]{:S(2)}) %collective-permute-start.30) | collective-permute-done | bytes 262176 | tf_op jit(solution)/shard_map/ppermute | solution.py:27
  142.7 0.7 copy-done.15
  143.4 6.8 %shard_map.87 = f32[2048,512]{1,0:T(8,128)} custom-call(s32[2]{0:T(128)} %pad_add_fusion.place, bf16[64,2048]{1,0:T(8,128)(2,1)} %copy-done.5, bf16[64,2048]{1,0:T(8,128)(2,1)} %copy-done.8, bf16[64,2048]{1,0:T(8,128)(2,1)} %copy-done.13, bf16[64,2048]{1,0:T(8,128)(2,1)} %copy-done.14, bf16[64,2048]{1,0:T(8,128)(2,1)} %copy-done.15, ...), custom_call_target="tpu_custom_call" | custom-call | flops 1073741824 | bytes 8388608 | tf_op jit(solution)/shard_map/pallas_call | solution.py:159
  150.2 0.7 convert_reduce_fusion
  (68 shorter events, 2.2 us)
Async XLA Ops:
  0.6 7.7 %copy-start.16 = (s32[4,16]{1,0:T(4,128)S(1)}, s32[4,16]{1,0:T(4,128)}, u32[]{:S(2)}) copy-start(s32[4,16]{1,0:T(4,128)} %mask.1) | copy-start | bytes 772
  0.6 7.7 %copy-start.17 = (s32[16,4]{0,1:T(4,128)S(1)}, s32[16,4]{0,1:T(4,128)}, u32[]{:S(2)}) copy-start(s32[16,4]{0,1:T(4,128)} %param.11) | copy-start | bytes 772
  0.7 8.4 %copy-start.2 = (bf16[2048,512]{1,0:T(8,128)(2,1)S(1)}, bf16[2048,512]{1,0:T(8,128)(2,1)}, u32[]{:S(2)}) copy-start(bf16[2048,512]{1,0:T(8,128)(2,1)} %param.9) | copy-start | bytes 6291460
  2.4 16.1 %all-to-all-start = ((bf16[8,32,1024]{2,1,0:T(8,128)(2,1)}), bf16[8,32,1024]{2,1,0:T(8,128)(2,1)S(1)}, u32[]{:S(2)}, u32[]{:S(2)}) async-start(bf16[8,32,1024]{2,1,0:T(8,128)(2,1)} %broadcast_in_dim.2), calls=%async_computation | async-start | bytes 1048576 | tf_op jit(solution)/shard_map/all_to_all | solution.py:195
  18.5 2.3 %copy-start.4 = (bf16[8,32,1024]{2,1,0:T(8,128)(2,1)}, bf16[8,32,1024]{2,1,0:T(8,128)(2,1)S(1)}, u32[]{:S(2)}) copy-start(bf16[8,32,1024]{2,1,0:T(8,128)(2,1)S(1)} %all-to-all-done) | copy-start | bytes 1572868
  18.5 1.8 %copy-start.3 = (bf16[512,2048]{1,0:T(8,128)(2,1)S(1)}, bf16[512,2048]{1,0:T(8,128)(2,1)}, u32[]{:S(2)}) copy-start(bf16[512,2048]{1,0:T(8,128)(2,1)} %param.8) | copy-start | bytes 6291460
  18.5 2.5 %collective-permute-start = (bf16[8,32,1024]{2,1,0:T(8,128)(2,1)S(1)}, bf16[8,32,1024]{2,1,0:T(8,128)(2,1)}, u32[]{:S(2)}, u32[]{:S(2)}) collective-permute-start(bf16[8,32,1024]{2,1,0:T(8,128)(2,1)S(1)} %all-to-all-done), channel_id=1, source_target_pairs={{0,1},{1,0},{2,3},{3,2},{4,5},{5,4},{6,7},{7,6},{8,9},{9,8},{10,11... | collective-permute-start | bytes 1572872 | tf_op jit(solution)/shard_map/ppermute | solution.py:196
  20.7 9.7 %copy-start = (bf16[512,2048]{1,0:T(8,128)(2,1)}, bf16[512,2048]{1,0:T(8,128)(2,1)S(1)}, u32[]{:S(2)}) copy-start(bf16[512,2048]{1,0:T(8,128)(2,1)S(1)} %bitcast_multiply_fusion.1.refs_8_) | copy-start | bytes 6291460
  20.8 2.6 %copy-start.1 = (bf16[2048,512]{1,0:T(8,128)(2,1)S(1)}, bf16[2048,512]{1,0:T(8,128)(2,1)}, u32[]{:S(2)}) copy-start(bf16[2048,512]{1,0:T(8,128)(2,1)} %bitcast_multiply_fusion) | copy-start | bytes 6291460
  24.8 10.4 %collective-permute-start.2 = (f16[64,2048]{1,0:T(8,128)(2,1)S(1)}, f16[64,2048]{1,0:T(8,128)(2,1)S(1)}, u32[]{:S(2)}, u32[]{:S(2)}) collective-permute-start(f16[64,2048]{1,0:T(8,128)(2,1)S(1)} %get-tuple-element.49), channel_id=1, source_target_pairs={{0,224},{16,240},{32,0},{48,16},{64,32},{80,48},{96,64},{112,80},{... | collective-permute-start | bytes 786440 | tf_op jit(solution)/shard_map/ppermute | solution.py:27
  30.5 7.9 %collective-permute-start.1 = (f16[64,2048]{1,0:T(8,128)(2,1)S(1)}, f16[64,2048]{1,0:T(8,128)(2,1)S(1)}, u32[]{:S(2)}, u32[]{:S(2)}) collective-permute-start(f16[64,2048]{1,0:T(8,128)(2,1)S(1)} %get-tuple-element.50), channel_id=1, source_target_pairs={{0,32},{16,48},{32,64},{48,80},{64,96},{80,112},{96,128},{112,144}... | collective-permute-start | bytes 786440 | tf_op jit(solution)/shard_map/ppermute | solution.py:27
  31.9 9.0 %collective-permute-start.10 = (f16[64,2048]{1,0:T(8,128)(2,1)S(1)}, f16[64,2048]{1,0:T(8,128)(2,1)S(1)}, u32[]{:S(2)}, u32[]{:S(2)}) collective-permute-start(f16[64,2048]{1,0:T(8,128)(2,1)S(1)} %get-tuple-element.43), channel_id=1, source_target_pairs={{0,224},{16,240},{32,0},{48,16},{64,32},{80,48},{96,64},{112,80},{... | collective-permute-start | bytes 786440 | tf_op jit(solution)/shard_map/ppermute | solution.py:27
  34.6 9.6 %collective-permute-start.9 = (f16[64,2048]{1,0:T(8,128)(2,1)S(1)}, f16[64,2048]{1,0:T(8,128)(2,1)S(1)}, u32[]{:S(2)}, u32[]{:S(2)}) collective-permute-start(f16[64,2048]{1,0:T(8,128)(2,1)S(1)} %get-tuple-element.44), channel_id=1, source_target_pairs={{0,32},{16,48},{32,64},{48,80},{64,96},{80,112},{96,128},{112,144}... | collective-permute-start | bytes 786440 | tf_op jit(solution)/shard_map/ppermute | solution.py:27
  38.5 8.0 %collective-permute-start.4 = (f16[64,2048]{1,0:T(8,128)(2,1)S(1)}, f16[64,2048]{1,0:T(8,128)(2,1)S(1)}, u32[]{:S(2)}, u32[]{:S(2)}) collective-permute-start(f16[64,2048]{1,0:T(8,128)(2,1)S(1)} %get-tuple-element.47), channel_id=1, source_target_pairs={{0,224},{16,240},{32,0},{48,16},{64,32},{80,48},{96,64},{112,80},{... | collective-permute-start | bytes 786440 | tf_op jit(solution)/shard_map/ppermute | solution.py:27
  38.9 10.9 %collective-permute-start.3 = (f16[64,2048]{1,0:T(8,128)(2,1)S(1)}, f16[64,2048]{1,0:T(8,128)(2,1)S(1)}, u32[]{:S(2)}, u32[]{:S(2)}) collective-permute-start(f16[64,2048]{1,0:T(8,128)(2,1)S(1)} %get-tuple-element.48), channel_id=1, source_target_pairs={{0,32},{16,48},{32,64},{48,80},{64,96},{80,112},{96,128},{112,144}... | collective-permute-start | bytes 786440 | tf_op jit(solution)/shard_map/ppermute | solution.py:27
  44.4 7.7 %collective-permute-start.12 = (f16[64,2048]{1,0:T(8,128)(2,1)S(1)}, f16[64,2048]{1,0:T(8,128)(2,1)S(1)}, u32[]{:S(2)}, u32[]{:S(2)}) collective-permute-start(f16[64,2048]{1,0:T(8,128)(2,1)S(1)} %get-tuple-element.41), channel_id=1, source_target_pairs={{0,224},{16,240},{32,0},{48,16},{64,32},{80,48},{96,64},{112,80},{... | collective-permute-start | bytes 786440 | tf_op jit(solution)/shard_map/ppermute | solution.py:27
  44.6 10.9 %collective-permute-start.11 = (f16[64,2048]{1,0:T(8,128)(2,1)S(1)}, f16[64,2048]{1,0:T(8,128)(2,1)S(1)}, u32[]{:S(2)}, u32[]{:S(2)}) collective-permute-start(f16[64,2048]{1,0:T(8,128)(2,1)S(1)} %get-tuple-element.42), channel_id=1, source_target_pairs={{0,32},{16,48},{32,64},{48,80},{64,96},{80,112},{96,128},{112,144}... | collective-permute-start | bytes 786440 | tf_op jit(solution)/shard_map/ppermute | solution.py:27
  50.0 7.7 %collective-permute-start.6 = (f16[64,2048]{1,0:T(8,128)(2,1)S(1)}, f16[64,2048]{1,0:T(8,128)(2,1)S(1)}, u32[]{:S(2)}, u32[]{:S(2)}) collective-permute-start(f16[64,2048]{1,0:T(8,128)(2,1)S(1)} %get-tuple-element.45), channel_id=1, source_target_pairs={{0,224},{16,240},{32,0},{48,16},{64,32},{80,48},{96,64},{112,80},{... | collective-permute-start | bytes 786440 | tf_op jit(solution)/shard_map/ppermute | solution.py:27
  50.4 10.7 %collective-permute-start.5 = (f16[64,2048]{1,0:T(8,128)(2,1)S(1)}, f16[64,2048]{1,0:T(8,128)(2,1)S(1)}, u32[]{:S(2)}, u32[]{:S(2)}) collective-permute-start(f16[64,2048]{1,0:T(8,128)(2,1)S(1)} %get-tuple-element.46), channel_id=1, source_target_pairs={{0,32},{16,48},{32,64},{48,80},{64,96},{80,112},{96,128},{112,144}... | collective-permute-start | bytes 786440 | tf_op jit(solution)/shard_map/ppermute | solution.py:27
  55.6 7.7 %collective-permute-start.14 = (f16[64,2048]{1,0:T(8,128)(2,1)S(1)}, f16[64,2048]{1,0:T(8,128)(2,1)S(1)}, u32[]{:S(2)}, u32[]{:S(2)}) collective-permute-start(f16[64,2048]{1,0:T(8,128)(2,1)S(1)} %get-tuple-element.39), channel_id=1, source_target_pairs={{0,224},{16,240},{32,0},{48,16},{64,32},{80,48},{96,64},{112,80},{... | collective-permute-start | bytes 786440 | tf_op jit(solution)/shard_map/ppermute | solution.py:27
  55.8 10.9 %collective-permute-start.13 = (f16[64,2048]{1,0:T(8,128)(2,1)S(1)}, f16[64,2048]{1,0:T(8,128)(2,1)S(1)}, u32[]{:S(2)}, u32[]{:S(2)}) collective-permute-start(f16[64,2048]{1,0:T(8,128)(2,1)S(1)} %get-tuple-element.40), channel_id=1, source_target_pairs={{0,32},{16,48},{32,64},{48,80},{64,96},{80,112},{96,128},{112,144}... | collective-permute-start | bytes 786440 | tf_op jit(solution)/shard_map/ppermute | solution.py:27
  61.2 7.8 %collective-permute-start.7 = (f16[64,2048]{1,0:T(8,128)(2,1)S(1)}, f16[64,2048]{1,0:T(8,128)(2,1)S(1)}, u32[]{:S(2)}, u32[]{:S(2)}) collective-permute-start(f16[64,2048]{1,0:T(8,128)(2,1)S(1)} %fusion.7), channel_id=1, source_target_pairs={{0,224},{16,240},{32,0},{48,16},{64,32},{80,48},{96,64},{112,80},{... | collective-permute-start | bytes 786440 | tf_op jit(solution)/shard_map/ppermute | solution.py:27
  66.8 7.3 %collective-permute-start.15 = (f16[64,2048]{1,0:T(8,128)(2,1)S(1)}, f16[64,2048]{1,0:T(8,128)(2,1)S(1)}, u32[]{:S(2)}, u32[]{:S(2)}) collective-permute-start(f16[64,2048]{1,0:T(8,128)(2,1)S(1)} %fusion.4), channel_id=1, source_target_pairs={{0,32},{16,48},{32,64},{48,80},{64,96},{80,112},{96,128},{112,144}... | collective-permute-start | bytes 786440 | tf_op jit(solution)/shard_map/ppermute | solution.py:27
  69.1 7.8 %collective-permute-start.8 = (f16[64,2048]{1,0:T(8,128)(2,1)S(1)}, f16[64,2048]{1,0:T(8,128)(2,1)S(1)}, u32[]{:S(2)}, u32[]{:S(2)}) collective-permute-start(f16[64,2048]{1,0:T(8,128)(2,1)S(1)} %fusion.13), channel_id=1, source_target_pairs={{0,16},{16,0},{32,48},{48,32},{64,80},{80,64},{96,112},{112,96},{1... | collective-permute-start | bytes 786440 | tf_op jit(solution)/shard_map/ppermute | solution.py:31
  74.2 7.7 %collective-permute-start.16 = (f16[64,2048]{1,0:T(8,128)(2,1)S(1)}, f16[64,2048]{1,0:T(8,128)(2,1)S(1)}, u32[]{:S(2)}, u32[]{:S(2)}) collective-permute-start(f16[64,2048]{1,0:T(8,128)(2,1)S(1)} %fusion.6), channel_id=1, source_target_pairs={{0,16},{16,0},{32,48},{48,32},{64,80},{80,64},{96,112},{112,96},{1... | collective-permute-start | bytes 786440 | tf_op jit(solution)/shard_map/ppermute | solution.py:31
  82.3 32.4 %copy-start.6 = (bf16[64,2048]{1,0:T(8,128)(2,1)}, bf16[64,2048]{1,0:T(8,128)(2,1)S(1)}, u32[]{:S(2)}) copy-start(bf16[64,2048]{1,0:T(8,128)(2,1)S(1)} %get-tuple-element.54.refs_0_) | copy-start | bytes 786436
  82.3 38.3 %copy-start.5 = (bf16[64,2048]{1,0:T(8,128)(2,1)}, bf16[64,2048]{1,0:T(8,128)(2,1)S(1)}, u32[]{:S(2)}) copy-start(bf16[64,2048]{1,0:T(8,128)(2,1)S(1)} %get-tuple-element.53.refs_0_) | copy-start | bytes 786436
  82.3 7.3 %collective-permute-start.17 = (bf16[64,2048]{1,0:T(8,128)(2,1)S(1)}, bf16[64,2048]{1,0:T(8,128)(2,1)S(1)}, u32[]{:S(2)}, u32[]{:S(2)}) collective-permute-start(bf16[64,2048]{1,0:T(8,128)(2,1)S(1)} %get-tuple-element.54.refs_0_), channel_id=1, source_target_pairs={{0,224},{16,240},{32,0},{48,16},{64,32},{80,48},{96,64},{112,80},{... | collective-permute-start | bytes 786440 | tf_op jit(solution)/shard_map/ppermute | solution.py:27
  86.2 6.4 %collective-permute-start.21 = (bf16[64,2048]{1,0:T(8,128)(2,1)S(1)}, bf16[64,2048]{1,0:T(8,128)(2,1)S(1)}, u32[]{:S(2)}, u32[]{:S(2)}) collective-permute-start(bf16[64,2048]{1,0:T(8,128)(2,1)S(1)} %get-tuple-element.54.refs_0_), channel_id=1, source_target_pairs={{0,32},{16,48},{32,64},{48,80},{64,96},{80,112},{96,128},{112,144}... | collective-permute-start | bytes 786440 | tf_op jit(solution)/shard_map/ppermute | solution.py:27
  89.5 25.1 %copy-start.10 = (bf16[64,2048]{1,0:T(8,128)(2,1)}, bf16[64,2048]{1,0:T(8,128)(2,1)S(1)}, u32[]{:S(2)}) copy-start(bf16[64,2048]{1,0:T(8,128)(2,1)S(1)} %collective-permute-done.17.refs_1_) | copy-start | bytes 786436
  89.5 6.4 %collective-permute-start.18 = (bf16[64,2048]{1,0:T(8,128)(2,1)S(1)}, bf16[64,2048]{1,0:T(8,128)(2,1)S(1)}, u32[]{:S(2)}, u32[]{:S(2)}) collective-permute-start(bf16[64,2048]{1,0:T(8,128)(2,1)S(1)} %collective-permute-done.17.refs_1_), channel_id=1, source_target_pairs={{0,224},{16,240},{32,0},{48,16},{64,32},{80,48},{96,64},{112,80},{... | collective-permute-start | bytes 786440 | tf_op jit(solution)/shard_map/ppermute | solution.py:27
  92.7 6.5 %collective-permute-start.27 = (bf16[64,2048]{1,0:T(8,128)(2,1)S(1)}, bf16[64,2048]{1,0:T(8,128)(2,1)S(1)}, u32[]{:S(2)}, u32[]{:S(2)}) collective-permute-start(bf16[64,2048]{1,0:T(8,128)(2,1)S(1)} %get-tuple-element.53.refs_0_), channel_id=1, source_target_pairs={{0,32},{16,48},{32,64},{48,80},{64,96},{80,112},{96,128},{112,144}... | collective-permute-start | bytes 786440 | tf_op jit(solution)/shard_map/ppermute | solution.py:27
  92.7 22.0 %copy-start.11 = (bf16[64,2048]{1,0:T(8,128)(2,1)}, bf16[64,2048]{1,0:T(8,128)(2,1)S(1)}, u32[]{:S(2)}) copy-start(bf16[64,2048]{1,0:T(8,128)(2,1)S(1)} %collective-permute-done.21.refs_7_) | copy-start | bytes 786436
  92.7 10.5 %collective-permute-start.22 = (bf16[64,2048]{1,0:T(8,128)(2,1)S(1)}, bf16[64,2048]{1,0:T(8,128)(2,1)}, u32[]{:S(2)}, u32[]{:S(2)}) collective-permute-start(bf16[64,2048]{1,0:T(8,128)(2,1)S(1)} %collective-permute-done.21.refs_7_), channel_id=1, source_target_pairs={{0,32},{16,48},{32,64},{48,80},{64,96},{80,112},{96,128},{112,144}... | collective-permute-start | bytes 786440 | tf_op jit(solution)/shard_map/ppermute | solution.py:27
  96.0 18.7 %copy-start.12 = (bf16[64,2048]{1,0:T(8,128)(2,1)}, bf16[64,2048]{1,0:T(8,128)(2,1)S(1)}, u32[]{:S(2)}) copy-start(bf16[64,2048]{1,0:T(8,128)(2,1)S(1)} %collective-permute-done.18.refs_2_) | copy-start | bytes 786436
  96.0 7.2 %collective-permute-start.19 = (bf16[64,2048]{1,0:T(8,128)(2,1)S(1)}, bf16[64,2048]{1,0:T(8,128)(2,1)}, u32[]{:S(2)}, u32[]{:S(2)}) collective-permute-start(bf16[64,2048]{1,0:T(8,128)(2,1)S(1)} %collective-permute-done.18.refs_2_), channel_id=1, source_target_pairs={{0,224},{16,240},{32,0},{48,16},{64,32},{80,48},{96,64},{112,80},{... | collective-permute-start | bytes 786440 | tf_op jit(solution)/shard_map/ppermute | solution.py:27
  99.1 7.2 %collective-permute-start.24 = (bf16[64,2048]{1,0:T(8,128)(2,1)S(1)}, bf16[64,2048]{1,0:T(8,128)(2,1)S(1)}, u32[]{:S(2)}, u32[]{:S(2)}) collective-permute-start(bf16[64,2048]{1,0:T(8,128)(2,1)S(1)} %get-tuple-element.53.refs_0_), channel_id=1, source_target_pairs={{0,224},{16,240},{32,0},{48,16},{64,32},{80,48},{96,64},{112,80},{... | collective-permute-start | bytes 786440 | tf_op jit(solution)/shard_map/ppermute | solution.py:27
  99.1 21.5 %copy-start.7 = (bf16[64,2048]{1,0:T(8,128)(2,1)}, bf16[64,2048]{1,0:T(8,128)(2,1)S(1)}, u32[]{:S(2)}) copy-start(bf16[64,2048]{1,0:T(8,128)(2,1)S(1)} %collective-permute-done.27.refs_7_) | copy-start | bytes 786436
  99.1 10.4 %collective-permute-start.28 = (bf16[64,2048]{1,0:T(8,128)(2,1)S(1)}, bf16[64,2048]{1,0:T(8,128)(2,1)S(1)}, u32[]{:S(2)}, u32[]{:S(2)}) collective-permute-start(bf16[64,2048]{1,0:T(8,128)(2,1)S(1)} %collective-permute-done.27.refs_7_), channel_id=1, source_target_pairs={{0,32},{16,48},{32,64},{48,80},{64,96},{80,112},{96,128},{112,144}... | collective-permute-start | bytes 786440 | tf_op jit(solution)/shard_map/ppermute | solution.py:27
  103.2 11.4 %collective-permute-start.23 = (bf16[64,2048]{1,0:T(8,128)(2,1)}, bf16[64,2048]{1,0:T(8,128)(2,1)}, u32[]{:S(2)}, u32[]{:S(2)}) collective-permute-start(bf16[64,2048]{1,0:T(8,128)(2,1)} %collective-permute-done.22.refs_6_), channel_id=1, source_target_pairs={{0,32},{16,48},{32,64},{48,80},{64,96},{80,112},{96,128},{112,144}... | collective-permute-start | bytes 786440 | tf_op jit(solution)/shard_map/ppermute | solution.py:27
  103.2 11.4 %collective-permute-start.20 = (bf16[64,2048]{1,0:T(8,128)(2,1)}, bf16[64,2048]{1,0:T(8,128)(2,1)}, u32[]{:S(2)}, u32[]{:S(2)}) collective-permute-start(bf16[64,2048]{1,0:T(8,128)(2,1)} %collective-permute-done.19.refs_3_), channel_id=1, source_target_pairs={{0,224},{16,240},{32,0},{48,16},{64,32},{80,48},{96,64},{112,80},{... | collective-permute-start | bytes 786440 | tf_op jit(solution)/shard_map/ppermute | solution.py:27
  106.3 14.3 %copy-start.8 = (bf16[64,2048]{1,0:T(8,128)(2,1)}, bf16[64,2048]{1,0:T(8,128)(2,1)S(1)}, u32[]{:S(2)}) copy-start(bf16[64,2048]{1,0:T(8,128)(2,1)S(1)} %collective-permute-done.24.refs_1_) | copy-start | bytes 786436
  106.3 26.4 %collective-permute-start.25 = (bf16[64,2048]{1,0:T(8,128)(2,1)S(1)}, bf16[64,2048]{1,0:T(8,128)(2,1)S(1)}, u32[]{:S(2)}, u32[]{:S(2)}) collective-permute-start(bf16[64,2048]{1,0:T(8,128)(2,1)S(1)} %collective-permute-done.24.refs_1_), channel_id=1, source_target_pairs={{0,224},{16,240},{32,0},{48,16},{64,32},{80,48},{96,64},{112,80},{... | collective-permute-start | bytes 786440 | tf_op jit(solution)/shard_map/ppermute | solution.py:27
  109.6 11.0 %copy-start.9 = (bf16[64,2048]{1,0:T(8,128)(2,1)}, bf16[64,2048]{1,0:T(8,128)(2,1)S(1)}, u32[]{:S(2)}) copy-start(bf16[64,2048]{1,0:T(8,128)(2,1)S(1)} %collective-permute-done.28.refs_6_) | copy-start | bytes 786436
  109.6 24.3 %collective-permute-start.29 = (bf16[64,2048]{1,0:T(8,128)(2,1)S(1)}, bf16[64,2048]{1,0:T(8,128)(2,1)}, u32[]{:S(2)}, u32[]{:S(2)}) collective-permute-start(bf16[64,2048]{1,0:T(8,128)(2,1)S(1)} %collective-permute-done.28.refs_6_), channel_id=1, source_target_pairs={{0,32},{16,48},{32,64},{48,80},{64,96},{80,112},{96,128},{112,144}... | collective-permute-start | bytes 786440 | tf_op jit(solution)/shard_map/ppermute | solution.py:27
  120.6 29.6 %all-to-all-start.1 = ((bf16[16,32,512]{2,1,0:T(8,128)(2,1)}), bf16[16,32,512]{2,1,0:T(8,128)(2,1)S(1)}, u32[]{:S(2)}, u32[]{:S(2)}) async-start(bf16[16,32,512]{2,1,0:T(8,128)(2,1)} %get-tuple-element.35), calls=%async_computation.1 | async-start | bytes 1048576 | tf_op jit(solution)/shard_map/all_to_all | solution.py:248
  132.7 7.7 %copy-start.13 = (bf16[64,2048]{1,0:T(8,128)(2,1)}, bf16[64,2048]{1,0:T(8,128)(2,1)S(1)}, u32[]{:S(2)}) copy-start(bf16[64,2048]{1,0:T(8,128)(2,1)S(1)} %collective-permute-done.25.refs_2_) | copy-start | bytes 786436
  132.7 7.9 %collective-permute-start.26 = (bf16[64,2048]{1,0:T(8,128)(2,1)S(1)}, bf16[64,2048]{1,0:T(8,128)(2,1)S(1)}, u32[]{:S(2)}, u32[]{:S(2)}) collective-permute-start(bf16[64,2048]{1,0:T(8,128)(2,1)S(1)} %collective-permute-done.25.refs_2_), channel_id=1, source_target_pairs={{0,224},{16,240},{32,0},{48,16},{64,32},{80,48},{96,64},{112,80},{... | collective-permute-start | bytes 786440 | tf_op jit(solution)/shard_map/ppermute | solution.py:27
  133.9 8.8 %collective-permute-start.30 = (bf16[64,2048]{1,0:T(8,128)(2,1)}, bf16[64,2048]{1,0:T(8,128)(2,1)S(1)}, u32[]{:S(2)}, u32[]{:S(2)}) collective-permute-start(bf16[64,2048]{1,0:T(8,128)(2,1)} %collective-permute-done.29.refs_5_), channel_id=1, source_target_pairs={{0,32},{16,48},{32,64},{48,80},{64,96},{80,112},{96,128},{112,144}... | collective-permute-start | bytes 786440 | tf_op jit(solution)/shard_map/ppermute | solution.py:27
  140.6 2.1 %copy-start.14 = (bf16[64,2048]{1,0:T(8,128)(2,1)}, bf16[64,2048]{1,0:T(8,128)(2,1)S(1)}, u32[]{:S(2)}) copy-start(bf16[64,2048]{1,0:T(8,128)(2,1)S(1)} %collective-permute-done.26.refs_3_) | copy-start | bytes 786436
  142.7 0.7 copy-start.15

commit v2 on v0

v2 whole, which is shorter than its diff:
```python
import jax
import jax.numpy as jnp
from jax import lax
from jax.experimental import pallas as pl
from jax.experimental.pallas import tpu as pltpu
from jax.sharding import PartitionSpec as P

BLOCK = 128
F16 = jnp.float16
BF16 = jnp.bfloat16
F32 = jnp.float32
PRE_SCALE = 8.0
ACT_SCALE = 64.0


def spread(weight, mask):
    rows, cols = mask.shape
    blocks = weight.reshape(rows, BLOCK, cols, BLOCK) * mask.astype(weight.dtype)[:, None, :, None]
    return blocks.reshape(weight.shape)


def ring(shift, rows):
    return [(r, (r + 2 * shift) % rows) for r in range(rows)]


def send(value, shift, rows):
    return lax.ppermute(value, "row", ring(shift, rows))


def swap(value, rows):
    return lax.ppermute(value, "row", [(r, r ^ 1) for r in range(rows)])


def together(*values):
    return lax.optimization_barrier(values)


def chunk_of(stack, index):
    return lax.dynamic_index_in_dim(stack, index % stack.shape[0], 0, keepdims=False)


def weight_in_kernel(mask, x, grad, out):
    tile = pl.program_id(0)
    product = lax.dot_general(
        x[...], grad[...], (((0,), (0,)), ((), ())), preferred_element_type=F32
    )
    for i in range(out.shape[0] // BLOCK):
        for j in range(out.shape[1] // BLOCK):
            keep = mask[i, tile * (out.shape[1] // BLOCK) + j].astype(F32)
            at = (slice(i * BLOCK, (i + 1) * BLOCK), slice(j * BLOCK, (j + 1) * BLOCK))
            out[at] = product[at] * keep


def grad_of_weight_in(x, grad, mask, width=1024):
    tokens, features = x.shape
    hidden = grad.shape[1]
    return pl.pallas_call(
        weight_in_kernel,
        out_shape=jax.ShapeDtypeStruct((features, hidden), F32),
        grid=(hidden // width,),
        in_specs=[
            pl.BlockSpec(memory_space=pltpu.SMEM),
            pl.BlockSpec((tokens, features), lambda i: (0, 0)),
            pl.BlockSpec((tokens, width), lambda i: (0, i)),
        ],
        out_specs=pl.BlockSpec((features, width), lambda i: (0, i)),
        cost_estimate=pl.CostEstimate(
            flops=2 * tokens * hidden * features, bytes_accessed=8 * features * hidden, transcendentals=0
        ),
    )(mask, x, grad)


def shards(rows, cols, inputs, cotangent, weight_in, weight_out, mask_in, mask_out):
    share, width = inputs.shape
    chips = cols // 2
    tokens = share * cols
    depth = rows // 2
    far = depth // 2
    same_core = [[2 * k + i for k in range(chips)] for i in range(2)]
    other_core = [(c, c ^ 1) for c in range(cols)]
    z = lax.axis_index("row") // 2
    first_core = lax.axis_index("col") % 2 == 0

    mine = jnp.concatenate([inputs, cotangent], axis=1)
    mine = jnp.broadcast_to(mine[None], (chips, share, 2 * width))
    mine = lax.all_to_all(mine, "col", 0, 0, axis_index_groups=same_core)
    other = lax.ppermute(mine, "col", other_core)
    both = jnp.stack(
        [jnp.where(first_core, mine, other), jnp.where(first_core, other, mine)], axis=1
    )
    both = both.reshape(tokens, 2 * width)
    inputs_all, cotangent_all = both[:, :width], both[:, width:]
    sparse_in, sparse_out = together(spread(weight_in, mask_in), spread(weight_out, mask_out))
    pre_part = jnp.dot(inputs_all, sparse_in, preferred_element_type=F32)
    act_part = lax.dot_general(
        cotangent_all, sparse_out, (((1,), (1,)), ((), ())), preferred_element_type=F32
    )
    pre_part = pre_part.reshape(depth, tokens // depth, -1)
    act_part = act_part.reshape(depth, tokens // depth, -1)
    inputs_all, cotangent_all = together(inputs_all, cotangent_all)

    def p(d):
        return chunk_of(pre_part, z + d) * PRE_SCALE

    def g(d):
        return chunk_of(act_part, z + d + depth) * ACT_SCALE

    pu, pd = p(far).astype(F16), p(depth - far + 1).astype(F16)
    gu, gd = g(far - 1).astype(F16), g(-far).astype(F16)
    for step in range(1, far):
        pu, pd = together(send(pu, 1, rows), send(pd, -1, rows))
        pu = (p(far - step) + pu.astype(F32)).astype(F16)
        if step < far - 1:
            pd = (p(depth - far + 1 + step) + pd.astype(F32)).astype(F16)
        gu, gd, _ = together(send(gu, 1, rows), send(gd, -1, rows), pu)
        if step < far - 1:
            gu = (g(far - 1 - step) + gu.astype(F32)).astype(F16)
        gd = (g(-far + step) + gd.astype(F32)).astype(F16)
    pu = send(pu, 1, rows)
    gd = send(gd, -1, rows)
    pre = (p(0) + pu.astype(F32) + pd.astype(F32)).astype(F16)
    pre = (pre.astype(F32) + swap(pre, rows).astype(F32)) * (1.0 / PRE_SCALE)
    grad_act = (g(0) + gu.astype(F32) + gd.astype(F32)).astype(F16)
    grad_act = (grad_act.astype(F32) + swap(grad_act, rows).astype(F32)) * (1.0 / ACT_SCALE)
    sig = jax.nn.sigmoid(pre)
    act, slope = together((pre * sig).astype(BF16), sig * (1.0 + pre * (1.0 - sig)))
    au, ad = send(act, 1, rows), send(act, -1, rows)
    au, ad = together(au, ad)
    grad_pre = (grad_act * slope).astype(BF16)

    acts, grads = {0: act, depth - 1: au, 1: ad}, {0: grad_pre}
    gu = gd = grad_pre
    for step in range(1, far):
        gu, gd = together(send(gu, 1, rows), send(gd, -1, rows))
        grads[depth - step], grads[step] = gu, gd
        au = acts[depth - step - 1] = send(au, 1, rows)
        if step < far - 1:
            ad = acts[step + 1] = send(ad, -1, rows)
            au, ad = together(au, ad)
    grads[far] = send(gd, -1, rows)

    chunk = tokens // depth
    gathered = jnp.zeros((depth, chunk, grad_pre.shape[1]), BF16)
    for d in [0] + [d for k in range(1, far) for d in (k, depth - k)] + [far]:
        gathered = lax.dynamic_update_index_in_dim(gathered, grads[d], (z + d) % depth, 0)
    (gathered,) = together(gathered.reshape(tokens, -1))
    partial = lax.dot_general(
        gathered, sparse_in, (((1,), (1,)), ((), ())), preferred_element_type=F32
    )
    pieces = partial.astype(BF16).reshape(cols, share, width)
    pieces = lax.all_to_all(pieces, "col", 0, 0)
    grad_inputs = jnp.sum(pieces.astype(F32), axis=0)
    grad_weight_in = grad_of_weight_in(inputs_all, gathered, mask_in)
    turned = cotangent_all.reshape(depth, chunk, width)
    turned = lax.dynamic_slice_in_dim(jnp.concatenate([turned, turned]), z, depth, axis=0)
    act, turned = together(
        jnp.concatenate([acts[d] for d in range(depth)], axis=0), turned.reshape(tokens, width)
    )
    grad_weight_out = lax.dot_general(
        act, turned, (((0,), (0,)), ((), ())), preferred_element_type=F32
    )
    return (grad_inputs, grad_weight_in, spread(grad_weight_out, mask_out))


def solution(mesh):
    rows, cols = mesh.shape["row"], mesh.shape["col"]
    return jax.shard_map(
        lambda *args: shards(rows, cols, *args),
        mesh=mesh,
        in_specs=(
            P("col", "row"),
            P("col", "row"),
            P("row", "col"),
            P("col", "row"),
            P("row", "col"),
            P("col", "row"),
        ),
        out_specs=(P("col", "row"), P("row", "col"), P("col", "row")),
        check_vma=False,
    )
```

time: 463 us -> 147 us (0.32)
  waiting for transfers between devices: 365 us -> 67.3 us
  starting transfers between devices: 0.12 us -> 51.2 us
  blocking collectives: 40.8 us -> 0 us
  between operations: 13.8 us -> 1.06 us
  local copies, waits for them, and re-layouts: 19.9 us -> 8.42 us
  matrix products: 13.9 us -> 7.98 us
    reduce_scatter x2 -> x0, waiting for transfers between devices: 264 us -> none  [the longest x1 220 us: shards(): lax.psum_scatter(jnp.concatenate([first, second], axis=1), 'row', scatter...]
    all_gather x1 -> x0, waiting for transfers between devices: 100 us -> none  [shards(): joined = lax.all_gather(stacked, 'row', axis=0, tiled=True)]
    ppermute x0 -> x31, waiting for transfers between devices: none -> 59.5 us  [the longest x28 51.4 us: send(): return lax.ppermute(value, 'row', ring(shift, rows))]
    all_gather x2 -> x0, blocking collectives: 40.8 us -> none  [the longest x1 22.7 us: shards(): lax.all_gather(inputs, 'col', axis=0, tiled=True)]
    ppermute x0 -> x31, starting transfers between devices: none -> 34.5 us  [the longest x28 30.2 us: send(): return lax.ppermute(value, 'row', ring(shift, rows))]
    all_to_all x0 -> x2, starting transfers between devices: none -> 16.7 us  [the longest x1 10.8 us: shards(): pieces = lax.all_to_all(pieces, 'col', 0, 0)]
    unnamed x10 -> x25, local copies, waits for them, and re-layouts: 17.5 us -> 4.56 us
    all_to_all x0 -> x2, waiting for transfers between devices: none -> 7.76 us  [the longest x1 7.76 us: shards(): mine = lax.all_to_all(mine, 'col', 0, 0, axis_index_groups=same_core)]
  transfers between devices with their start and end apart: 3 -> 33, of which waited for: 3 -> 27; matrix products, arithmetic and copies ran while one was open for 3% -> 10% of each run, Pallas kernels for 0% -> 3%
where the time goes in v2:
time: 147 us; the launch traced here: 146 us
  waiting for transfers between devices  67.3 us (46%)
  starting transfers between devices  51.2 us (35%)
  local copies, waits for them, and re-layouts  8.42 us (6%)
  matrix products  7.98 us (5%)
  other arithmetic  5.69 us (4%)
  Pallas kernels  4.36 us (3%)
    ppermute x28, waiting for transfers between devices, send(): return lax.ppermute(value, 'row', ring(shift, rows))  51.4 us
    ppermute x28, starting transfers between devices, send(): return lax.ppermute(value, 'row', ring(shift, rows))  30.2 us
    all_to_all x1, starting transfers between devices, shards(): pieces = lax.all_to_all(pieces, 'col', 0, 0)  10.8 us
    ppermute x2, waiting for transfers between devices, swap(): return lax.ppermute(value, 'row', [(r, r ^ 1) for r in range(rows)])  7.84 us
    all_to_all x1, waiting for transfers between devices, shards(): mine = lax.all_to_all(mine, 'col', 0, 0, axis_index_groups=same_core)  7.76 us
    all_to_all x1, starting transfers between devices, shards(): mine = lax.all_to_all(mine, 'col', 0, 0, axis_index_groups=same_core)  5.86 us
    unnamed x25, local copies, waits for them, and re-layouts  4.56 us
    pallas_call x1, Pallas kernels, grad_of_weight_in(): pl.pallas_call(weight_in_kernel, out_shape=jax.ShapeDtypeStruct((features...  4.36 us
  transfers between devices with their start and end apart: 33, of which 27 were waited for; matrix products, arithmetic and copies ran while one was open for 10% of the time, Pallas kernels for 3%

profile of v2, /device:TPU:1, one launch (start us, length us, event | category | flops | bytes accessed | tf_op | source)
XLA Modules:
  0.0 146.0 jit_solution(16046439583063300203)
XLA Ops:
  0.7 0.8 pad_maximum_fusion.1
  1.4 0.9 broadcast_in_dim.38
  2.3 5.9 %all-to-all-start = ((bf16[8,32,1024]{2,1,0:T(8,128)(2,1)}), bf16[8,32,1024]{2,1,0:T(8,128)(2,1)S(1)}, u32[]{:S(2)}, u32[]{:S(2)}) async-start(bf16[8,32,1024]{2,1,0:T(8,128)(2,1)} %broadcast_in_dim.38), calls=%async_computation | async-start | bytes 1048576 | tf_op jit(solution)/shard_map/all_to_all | solution.py:86
  8.4 0.6 mul.148
  9.0 1.6 %bitcast_multiply_fusion.1 = bf16[2048,512]{1,0:T(8,128)(2,1)} fusion(bf16[2048,512]{1,0:T(8,128)(2,1)S(1)} %copy-done.4, bf16[256,8,4,128]{3,2,1,0:T(4,128)(2,1)S(1)} %bitcast.121), kind=kLoop, calls=%fused_computation.1 | loop fusion | flops 1048576 | bytes 6291456 | tf_op jit(solution)/shard_map/mul | solution.py:18
  10.6 7.8 %all-to-all-done = bf16[8,32,1024]{2,1,0:T(8,128)(2,1)S(1)} async-done(((bf16[8,32,1024]{2,1,0:T(8,128)(2,1)}), bf16[8,32,1024]{2,1,0:T(8,128)(2,1)S(1)}, u32[]{:S(2)}, u32[]{:S(2)}) %all-to-all-start) | async-done | bytes 524320 | tf_op jit(solution)/shard_map/all_to_all | solution.py:86
  18.4 0.8 collective-permute-start
  19.2 0.3 mul.145
  19.5 0.4 copy-done.5
  19.9 0.5 bitcast_multiply_fusion.2
  20.9 1.1 copy-done
  22.1 1.3 fusion.21
  23.4 1.3 fusion.19
  24.7 5.7 %collective-permute-start.4 = (f16[64,2048]{1,0:T(8,128)(2,1)S(1)}, f16[64,2048]{1,0:T(8,128)(2,1)S(1)}, u32[]{:S(2)}, u32[]{:S(2)}) collective-permute-start(f16[64,2048]{1,0:T(8,128)(2,1)S(1)} %get-tuple-element.77), channel_id=1, source_target_pairs={{0,224},{16,240},{32,0},{48,16},{64,32},{80,48},{96,64},{112,80},{... | collective-permute-start | bytes 786440 | tf_op jit(solution)/shard_map/ppermute | solution.py:27
  30.4 0.9 fusion.23
  31.4 2.7 %collective-permute-start.2 = (f16[64,2048]{1,0:T(8,128)(2,1)S(1)}, f16[64,2048]{1,0:T(8,128)(2,1)S(1)}, u32[]{:S(2)}, u32[]{:S(2)}) collective-permute-start(f16[64,2048]{1,0:T(8,128)(2,1)S(1)} %get-tuple-element.71), channel_id=1, source_target_pairs={{0,224},{16,240},{32,0},{48,16},{64,32},{80,48},{96,64},{112,80},{... | collective-permute-start | bytes 786440 | tf_op jit(solution)/shard_map/ppermute | solution.py:27
  34.1 1.1 collective-permute-done.4
  35.2 3.1 %collective-permute-done.3 = f16[64,2048]{1,0:T(8,128)(2,1)S(1)} collective-permute-done((f16[64,2048]{1,0:T(8,128)(2,1)S(1)}, f16[64,2048]{1,0:T(8,128)(2,1)S(1)}, u32[]{:S(2)}, u32[]{:S(2)}) %collective-permute-start.3) | collective-permute-done | bytes 262176 | tf_op jit(solution)/shard_map/ppermute | solution.py:27
  38.6 2.2 %collective-permute-done.2 = f16[64,2048]{1,0:T(8,128)(2,1)S(1)} collective-permute-done((f16[64,2048]{1,0:T(8,128)(2,1)S(1)}, f16[64,2048]{1,0:T(8,128)(2,1)S(1)}, u32[]{:S(2)}, u32[]{:S(2)}) %collective-permute-start.2) | collective-permute-done | bytes 262176 | tf_op jit(solution)/shard_map/ppermute | solution.py:27
  40.8 3.1 %collective-permute-done.1 = f16[64,2048]{1,0:T(8,128)(2,1)S(1)} collective-permute-done((f16[64,2048]{1,0:T(8,128)(2,1)S(1)}, f16[64,2048]{1,0:T(8,128)(2,1)S(1)}, u32[]{:S(2)}, u32[]{:S(2)}) %collective-permute-start.1) | collective-permute-done | bytes 262176 | tf_op jit(solution)/shard_map/ppermute | solution.py:27
  43.9 0.3 collective-permute-start.8
  44.5 1.5 collective-permute-start.5
  45.9 3.5 %collective-permute-done.8 = f16[64,2048]{1,0:T(8,128)(2,1)S(1)} collective-permute-done((f16[64,2048]{1,0:T(8,128)(2,1)S(1)}, f16[64,2048]{1,0:T(8,128)(2,1)S(1)}, u32[]{:S(2)}, u32[]{:S(2)}) %collective-permute-start.8) | collective-permute-done | bytes 262176 | tf_op jit(solution)/shard_map/ppermute | solution.py:27
  49.7 0.3 collective-permute-start.11
  49.9 3.6 %collective-permute-done.6 = f16[64,2048]{1,0:T(8,128)(2,1)S(1)} collective-permute-done((f16[64,2048]{1,0:T(8,128)(2,1)S(1)}, f16[64,2048]{1,0:T(8,128)(2,1)S(1)}, u32[]{:S(2)}, u32[]{:S(2)}) %collective-permute-start.6) | collective-permute-done | bytes 262176 | tf_op jit(solution)/shard_map/ppermute | solution.py:27
  53.6 1.2 collective-permute-done.5
  54.8 0.9 collective-permute-start.12
  56.0 1.5 collective-permute-start.9
  57.4 3.2 %collective-permute-done.12 = f16[64,2048]{1,0:T(8,128)(2,1)S(1)} collective-permute-done((f16[64,2048]{1,0:T(8,128)(2,1)S(1)}, f16[64,2048]{1,0:T(8,128)(2,1)S(1)}, u32[]{:S(2)}, u32[]{:S(2)}) %collective-permute-start.12) | collective-permute-done | bytes 262176 | tf_op jit(solution)/shard_map/ppermute | solution.py:27
  60.8 3.7 %collective-permute-done.10 = f16[64,2048]{1,0:T(8,128)(2,1)S(1)} collective-permute-done((f16[64,2048]{1,0:T(8,128)(2,1)S(1)}, f16[64,2048]{1,0:T(8,128)(2,1)S(1)}, u32[]{:S(2)}, u32[]{:S(2)}) %collective-permute-start.10) | collective-permute-done | bytes 262176 | tf_op jit(solution)/shard_map/ppermute | solution.py:27
  64.5 0.8 collective-permute-done.9
  65.5 1.0 collective-permute-start.13
  66.5 4.5 %collective-permute-done.15 = f16[64,2048]{1,0:T(8,128)(2,1)S(1)} collective-permute-done((f16[64,2048]{1,0:T(8,128)(2,1)S(1)}, f16[64,2048]{1,0:T(8,128)(2,1)S(1)}, u32[]{:S(2)}, u32[]{:S(2)}) %collective-permute-start.15) | collective-permute-done | bytes 262176 | tf_op jit(solution)/shard_map/ppermute | solution.py:27
  71.1 2.7 %collective-permute-start.16 = (f16[64,2048]{1,0:T(8,128)(2,1)S(1)}, f16[64,2048]{1,0:T(8,128)(2,1)S(1)}, u32[]{:S(2)}, u32[]{:S(2)}) collective-permute-start(f16[64,2048]{1,0:T(8,128)(2,1)S(1)} %fusion.2), channel_id=1, source_target_pairs={{0,16},{16,0},{32,48},{48,32},{64,80},{80,64},{96,112},{112,96},{1... | collective-permute-start | bytes 786440 | tf_op jit(solution)/shard_map/ppermute | solution.py:31
  74.0 0.8 collective-permute-start.14
  74.7 3.2 %collective-permute-done.16 = f16[64,2048]{1,0:T(8,128)(2,1)S(1)} collective-permute-done((f16[64,2048]{1,0:T(8,128)(2,1)S(1)}, f16[64,2048]{1,0:T(8,128)(2,1)S(1)}, u32[]{:S(2)}, u32[]{:S(2)}) %collective-permute-start.16) | collective-permute-done | bytes 262176 | tf_op jit(solution)/shard_map/ppermute | solution.py:31
  78.2 4.6 %collective-permute-done.14 = f16[64,2048]{1,0:T(8,128)(2,1)S(1)} collective-permute-done((f16[64,2048]{1,0:T(8,128)(2,1)S(1)}, f16[64,2048]{1,0:T(8,128)(2,1)S(1)}, u32[]{:S(2)}, u32[]{:S(2)}) %collective-permute-start.14) | collective-permute-done | bytes 262176 | tf_op jit(solution)/shard_map/ppermute | solution.py:31
  83.3 2.7 %collective-permute-start.18 = (bf16[64,2048]{1,0:T(8,128)(2,1)S(1)}, bf16[64,2048]{1,0:T(8,128)(2,1)S(1)}, u32[]{:S(2)}, u32[]{:S(2)}) collective-permute-start(bf16[64,2048]{1,0:T(8,128)(2,1)S(1)} %get-tuple-element.66), channel_id=1, source_target_pairs={{0,224},{16,240},{32,0},{48,16},{64,32},{80,48},{96,64},{112,80},{... | collective-permute-start | bytes 786440 | tf_op jit(solution)/shard_map/ppermute | solution.py:27
  86.2 1.5 collective-permute-start.24
  87.7 2.0 %collective-permute-done.17 = bf16[64,2048]{1,0:T(8,128)(2,1)S(1)} collective-permute-done((bf16[64,2048]{1,0:T(8,128)(2,1)S(1)}, bf16[64,2048]{1,0:T(8,128)(2,1)S(1)}, u32[]{:S(2)}, u32[]{:S(2)}) %collective-permute-start.17) | collective-permute-done | bytes 262176 | tf_op jit(solution)/shard_map/ppermute | solution.py:27
  89.7 2.7 %collective-permute-start.20 = (bf16[64,2048]{1,0:T(8,128)(2,1)S(1)}, bf16[64,2048]{1,0:T(8,128)(2,1)S(1)}, u32[]{:S(2)}, u32[]{:S(2)}) collective-permute-start(bf16[64,2048]{1,0:T(8,128)(2,1)S(1)} %collective-permute-done.18), channel_id=1, source_target_pairs={{0,224},{16,240},{32,0},{48,16},{64,32},{80,48},{96,64},{112,80},{... | collective-permute-start | bytes 786440 | tf_op jit(solution)/shard_map/ppermute | solution.py:27
  92.6 1.5 %collective-permute-done.24 = bf16[64,2048]{1,0:T(8,128)(2,1)S(1)} collective-permute-done((bf16[64,2048]{1,0:T(8,128)(2,1)S(1)}, bf16[64,2048]{1,0:T(8,128)(2,1)S(1)}, u32[]{:S(2)}, u32[]{:S(2)}) %collective-permute-start.24) | collective-permute-done | bytes 262176 | tf_op jit(solution)/shard_map/ppermute | solution.py:27
  94.1 1.9 %collective-permute-start.26 = (bf16[64,2048]{1,0:T(8,128)(2,1)S(1)}, bf16[64,2048]{1,0:T(8,128)(2,1)S(1)}, u32[]{:S(2)}, u32[]{:S(2)}) collective-permute-start(bf16[64,2048]{1,0:T(8,128)(2,1)S(1)} %collective-permute-done.25), channel_id=1, source_target_pairs={{0,224},{16,240},{32,0},{48,16},{64,32},{80,48},{96,64},{112,80},{... | collective-permute-start | bytes 786440 | tf_op jit(solution)/shard_map/ppermute | solution.py:27
  96.1 2.5 %collective-permute-done.20 = bf16[64,2048]{1,0:T(8,128)(2,1)S(1)} collective-permute-done((bf16[64,2048]{1,0:T(8,128)(2,1)S(1)}, bf16[64,2048]{1,0:T(8,128)(2,1)S(1)}, u32[]{:S(2)}, u32[]{:S(2)}) %collective-permute-start.20) | collective-permute-done | bytes 262176 | tf_op jit(solution)/shard_map/ppermute | solution.py:27
  98.6 2.6 %collective-permute-done.19 = bf16[64,2048]{1,0:T(8,128)(2,1)S(1)} collective-permute-done((bf16[64,2048]{1,0:T(8,128)(2,1)S(1)}, bf16[64,2048]{1,0:T(8,128)(2,1)S(1)}, u32[]{:S(2)}, u32[]{:S(2)}) %collective-permute-start.19) | collective-permute-done | bytes 262176 | tf_op jit(solution)/shard_map/ppermute | solution.py:27
  101.2 0.8 collective-permute-start.22
  102.0 0.7 collective-permute-start.21
  102.8 1.4 collective-permute-done.26
  104.2 3.4 %collective-permute-start.28 = (bf16[64,2048]{1,0:T(8,128)(2,1)S(1)}, bf16[64,2048]{1,0:T(8,128)(2,1)S(1)}, u32[]{:S(2)}, u32[]{:S(2)}) collective-permute-start(bf16[64,2048]{1,0:T(8,128)(2,1)S(1)} %collective-permute-done.26), channel_id=1, source_target_pairs={{0,224},{16,240},{32,0},{48,16},{64,32},{80,48},{96,64},{112,80},{... | collective-permute-start | bytes 786440 | tf_op jit(solution)/shard_map/ppermute | solution.py:27
  107.6 2.2 %collective-permute-done.22 = bf16[64,2048]{1,0:T(8,128)(2,1)S(1)} collective-permute-done((bf16[64,2048]{1,0:T(8,128)(2,1)S(1)}, bf16[64,2048]{1,0:T(8,128)(2,1)S(1)}, u32[]{:S(2)}, u32[]{:S(2)}) %collective-permute-start.22) | collective-permute-done | bytes 262176 | tf_op jit(solution)/shard_map/ppermute | solution.py:27
  109.8 1.2 collective-permute-done.21
  111.0 2.2 %collective-permute-start.23 = (bf16[64,2048]{1,0:T(8,128)(2,1)S(1)}, bf16[64,2048]{1,0:T(8,128)(2,1)S(1)}, u32[]{:S(2)}, u32[]{:S(2)}) collective-permute-start(bf16[64,2048]{1,0:T(8,128)(2,1)S(1)} %collective-permute-done.22), channel_id=1, source_target_pairs={{0,224},{16,240},{32,0},{48,16},{64,32},{80,48},{96,64},{112,80},{... | collective-permute-start | bytes 786440 | tf_op jit(solution)/shard_map/ppermute | solution.py:27
  113.2 2.2 %collective-permute-done.28 = bf16[64,2048]{1,0:T(8,128)(2,1)S(1)} collective-permute-done((bf16[64,2048]{1,0:T(8,128)(2,1)S(1)}, bf16[64,2048]{1,0:T(8,128)(2,1)S(1)}, u32[]{:S(2)}, u32[]{:S(2)}) %collective-permute-start.28) | collective-permute-done | bytes 262176 | tf_op jit(solution)/shard_map/ppermute | solution.py:27
  115.4 1.0 collective-permute-done.29
  116.5 4.5 %collective-permute-done.23 = bf16[64,2048]{1,0:T(8,128)(2,1)S(1)} collective-permute-done((bf16[64,2048]{1,0:T(8,128)(2,1)S(1)}, bf16[64,2048]{1,0:T(8,128)(2,1)S(1)}, u32[]{:S(2)}, u32[]{:S(2)}) %collective-permute-start.23) | collective-permute-done | bytes 262176 | tf_op jit(solution)/shard_map/ppermute | solution.py:27
  121.1 2.1 %convolution_convert_fusion = bf16[512,512]{1,0:T(8,128)(2,1)} fusion(bf16[512,2048]{1,0:T(8,128)(2,1)S(1)} %bitcast.123, bf16[512,2048]{1,0:T(8,128)(2,1)S(1)} %bitcast_multiply_fusion.2), kind=kOutput, calls=%fused_computation.3 | convolution fusion | flops 1074003968 | bytes 4718592 | tf_op jit(solution)/shard_map/dot_general | solution.py:147
  123.2 10.8 %all-to-all-start.1 = ((bf16[16,32,512]{2,1,0:T(8,128)(2,1)}), bf16[16,32,512]{2,1,0:T(8,128)(2,1)S(1)}, u32[]{:S(2)}, u32[]{:S(2)}) async-start(bf16[16,32,512]{2,1,0:T(8,128)(2,1)} %bitcast.127), calls=%async_computation.1 | async-start | bytes 1048576 | tf_op jit(solution)/shard_map/all_to_all | solution.py:151
  134.0 4.4 %shard_map.85 = f32[512,2048]{1,0:T(8,128)} custom-call(s32[4,16]{1,0:T(4,128)} %mask.1, bf16[512,512]{1,0:T(8,128)(2,1)} %get-tuple-element.55.x, bf16[512,2048]{1,0:T(8,128)(2,1)} %bitcast.124), custom_call_target="tpu_custom_call" | custom-call | flops 1073741824 | bytes 8388608 | tf_op jit(solution)/shard_map/pallas_call | solution.py:57
  138.4 1.0 constant_dynamic-update-slice_fusion.3
  139.4 1.0 constant_dynamic-update-slice_fusion.2
  140.4 1.0 constant_dynamic-update-slice_fusion.1
  141.4 0.6 mul.187
  142.0 3.3 %bitcast_multiply_fusion = f32[2048,512]{1,0:T(8,128)} fusion(f32[256,8,4,128]{3,2,1,0:T(4,128)S(1)} %bitcast.107, bf16[512,2048]{1,0:T(8,128)(2,1)S(1)} %constant_dynamic-update-slice_fusion, bf16[512,512]{1,0:T(8,128)(2,1)S(1)} %bitcast.125), kind=kOutput, calls=%fused_computation | convolution fusion | flops 1074790400 | bytes 11010048 | tf_op jit(solution)/shard_map/dot_general | solution.py:159
  145.3 0.7 convert_reduce_fusion
  (69 shorter events, 3.9 us)
Async XLA Ops:
  0.6 7.5 %copy-start.7 = (s32[4,16]{1,0:T(4,128)S(1)}, s32[4,16]{1,0:T(4,128)}, u32[]{:S(2)}) copy-start(s32[4,16]{1,0:T(4,128)} %mask.1) | copy-start | bytes 772
  0.6 7.5 %copy-start.8 = (s32[16,4]{0,1:T(4,128)S(1)}, s32[16,4]{0,1:T(4,128)}, u32[]{:S(2)}) copy-start(s32[16,4]{0,1:T(4,128)} %param.11) | copy-start | bytes 772
  1.4 7.6 %copy-start.4 = (bf16[2048,512]{1,0:T(8,128)(2,1)S(1)}, bf16[2048,512]{1,0:T(8,128)(2,1)}, u32[]{:S(2)}) copy-start(bf16[2048,512]{1,0:T(8,128)(2,1)} %param.9) | copy-start | bytes 6291460
  2.3 16.1 %all-to-all-start = ((bf16[8,32,1024]{2,1,0:T(8,128)(2,1)}), bf16[8,32,1024]{2,1,0:T(8,128)(2,1)S(1)}, u32[]{:S(2)}, u32[]{:S(2)}) async-start(bf16[8,32,1024]{2,1,0:T(8,128)(2,1)} %broadcast_in_dim.38), calls=%async_computation | async-start | bytes 1048576 | tf_op jit(solution)/shard_map/all_to_all | solution.py:86
  18.4 1.6 %copy-start.5 = (bf16[512,2048]{1,0:T(8,128)(2,1)S(1)}, bf16[512,2048]{1,0:T(8,128)(2,1)}, u32[]{:S(2)}) copy-start(bf16[512,2048]{1,0:T(8,128)(2,1)} %param.8) | copy-start | bytes 6291460
  18.4 2.4 %collective-permute-start = (bf16[8,32,1024]{2,1,0:T(8,128)(2,1)S(1)}, bf16[8,32,1024]{2,1,0:T(8,128)(2,1)S(1)}, u32[]{:S(2)}, u32[]{:S(2)}) collective-permute-start(bf16[8,32,1024]{2,1,0:T(8,128)(2,1)S(1)} %all-to-all-done), channel_id=1, source_target_pairs={{0,1},{1,0},{2,3},{3,2},{4,5},{5,4},{6,7},{7,6},{8,9},{9,8},{10,11... | collective-permute-start | bytes 1572872 | tf_op jit(solution)/shard_map/ppermute | solution.py:87
  20.5 1.6 %copy-start = (bf16[2048,512]{1,0:T(8,128)(2,1)S(1)}, bf16[2048,512]{1,0:T(8,128)(2,1)}, u32[]{:S(2)}) copy-start(bf16[2048,512]{1,0:T(8,128)(2,1)} %bitcast_multiply_fusion.1) | copy-start | bytes 6291460
  24.7 10.4 %collective-permute-start.4 = (f16[64,2048]{1,0:T(8,128)(2,1)S(1)}, f16[64,2048]{1,0:T(8,128)(2,1)S(1)}, u32[]{:S(2)}, u32[]{:S(2)}) collective-permute-start(f16[64,2048]{1,0:T(8,128)(2,1)S(1)} %get-tuple-element.77), channel_id=1, source_target_pairs={{0,224},{16,240},{32,0},{48,16},{64,32},{80,48},{96,64},{112,80},{... | collective-permute-start | bytes 786440 | tf_op jit(solution)/shard_map/ppermute | solution.py:27
  30.4 7.9 %collective-permute-start.3 = (f16[64,2048]{1,0:T(8,128)(2,1)S(1)}, f16[64,2048]{1,0:T(8,128)(2,1)S(1)}, u32[]{:S(2)}, u32[]{:S(2)}) collective-permute-start(f16[64,2048]{1,0:T(8,128)(2,1)S(1)} %get-tuple-element.78), channel_id=1, source_target_pairs={{0,32},{16,48},{32,64},{48,80},{64,96},{80,112},{96,128},{112,144}... | collective-permute-start | bytes 786440 | tf_op jit(solution)/shard_map/ppermute | solution.py:27
  31.4 9.4 %collective-permute-start.2 = (f16[64,2048]{1,0:T(8,128)(2,1)S(1)}, f16[64,2048]{1,0:T(8,128)(2,1)S(1)}, u32[]{:S(2)}, u32[]{:S(2)}) collective-permute-start(f16[64,2048]{1,0:T(8,128)(2,1)S(1)} %get-tuple-element.71), channel_id=1, source_target_pairs={{0,224},{16,240},{32,0},{48,16},{64,32},{80,48},{96,64},{112,80},{... | collective-permute-start | bytes 786440 | tf_op jit(solution)/shard_map/ppermute | solution.py:27
  34.1 9.8 %collective-permute-start.1 = (f16[64,2048]{1,0:T(8,128)(2,1)S(1)}, f16[64,2048]{1,0:T(8,128)(2,1)S(1)}, u32[]{:S(2)}, u32[]{:S(2)}) collective-permute-start(f16[64,2048]{1,0:T(8,128)(2,1)S(1)} %get-tuple-element.72), channel_id=1, source_target_pairs={{0,32},{16,48},{32,64},{48,80},{64,96},{80,112},{96,128},{112,144}... | collective-permute-start | bytes 786440 | tf_op jit(solution)/shard_map/ppermute | solution.py:27
  38.5 11.0 %collective-permute-start.7 = (f16[64,2048]{1,0:T(8,128)(2,1)S(1)}, f16[64,2048]{1,0:T(8,128)(2,1)S(1)}, u32[]{:S(2)}, u32[]{:S(2)}) collective-permute-start(f16[64,2048]{1,0:T(8,128)(2,1)S(1)} %get-tuple-element.76), channel_id=1, source_target_pairs={{0,32},{16,48},{32,64},{48,80},{64,96},{80,112},{96,128},{112,144}... | collective-permute-start | bytes 786440 | tf_op jit(solution)/shard_map/ppermute | solution.py:27
  43.9 5.5 %collective-permute-start.8 = (f16[64,2048]{1,0:T(8,128)(2,1)S(1)}, f16[64,2048]{1,0:T(8,128)(2,1)S(1)}, u32[]{:S(2)}, u32[]{:S(2)}) collective-permute-start(f16[64,2048]{1,0:T(8,128)(2,1)S(1)} %get-tuple-element.75), channel_id=1, source_target_pairs={{0,224},{16,240},{32,0},{48,16},{64,32},{80,48},{96,64},{112,80},{... | collective-permute-start | bytes 786440 | tf_op jit(solution)/shard_map/ppermute | solution.py:27
  44.4 9.2 %collective-permute-start.6 = (f16[64,2048]{1,0:T(8,128)(2,1)S(1)}, f16[64,2048]{1,0:T(8,128)(2,1)S(1)}, u32[]{:S(2)}, u32[]{:S(2)}) collective-permute-start(f16[64,2048]{1,0:T(8,128)(2,1)S(1)} %get-tuple-element.69), channel_id=1, source_target_pairs={{0,224},{16,240},{32,0},{48,16},{64,32},{80,48},{96,64},{112,80},{... | collective-permute-start | bytes 786440 | tf_op jit(solution)/shard_map/ppermute | solution.py:27
  44.5 10.3 %collective-permute-start.5 = (f16[64,2048]{1,0:T(8,128)(2,1)S(1)}, f16[64,2048]{1,0:T(8,128)(2,1)S(1)}, u32[]{:S(2)}, u32[]{:S(2)}) collective-permute-start(f16[64,2048]{1,0:T(8,128)(2,1)S(1)} %get-tuple-element.70), channel_id=1, source_target_pairs={{0,32},{16,48},{32,64},{48,80},{64,96},{80,112},{96,128},{112,144}... | collective-permute-start | bytes 786440 | tf_op jit(solution)/shard_map/ppermute | solution.py:27
  49.7 11.0 %collective-permute-start.11 = (f16[64,2048]{1,0:T(8,128)(2,1)S(1)}, f16[64,2048]{1,0:T(8,128)(2,1)S(1)}, u32[]{:S(2)}, u32[]{:S(2)}) collective-permute-start(f16[64,2048]{1,0:T(8,128)(2,1)S(1)} %get-tuple-element.74), channel_id=1, source_target_pairs={{0,32},{16,48},{32,64},{48,80},{64,96},{80,112},{96,128},{112,144}... | collective-permute-start | bytes 786440 | tf_op jit(solution)/shard_map/ppermute | solution.py:27
  54.8 5.8 %collective-permute-start.12 = (f16[64,2048]{1,0:T(8,128)(2,1)S(1)}, f16[64,2048]{1,0:T(8,128)(2,1)S(1)}, u32[]{:S(2)}, u32[]{:S(2)}) collective-permute-start(f16[64,2048]{1,0:T(8,128)(2,1)S(1)} %get-tuple-element.73), channel_id=1, source_target_pairs={{0,224},{16,240},{32,0},{48,16},{64,32},{80,48},{96,64},{112,80},{... | collective-permute-start | bytes 786440 | tf_op jit(solution)/shard_map/ppermute | solution.py:27
  55.9 8.6 %collective-permute-start.10 = (f16[64,2048]{1,0:T(8,128)(2,1)S(1)}, f16[64,2048]{1,0:T(8,128)(2,1)S(1)}, u32[]{:S(2)}, u32[]{:S(2)}) collective-permute-start(f16[64,2048]{1,0:T(8,128)(2,1)S(1)} %get-tuple-element.67), channel_id=1, source_target_pairs={{0,224},{16,240},{32,0},{48,16},{64,32},{80,48},{96,64},{112,80},{... | collective-permute-start | bytes 786440 | tf_op jit(solution)/shard_map/ppermute | solution.py:27
  56.0 9.4 %collective-permute-start.9 = (f16[64,2048]{1,0:T(8,128)(2,1)S(1)}, f16[64,2048]{1,0:T(8,128)(2,1)S(1)}, u32[]{:S(2)}, u32[]{:S(2)}) collective-permute-start(f16[64,2048]{1,0:T(8,128)(2,1)S(1)} %get-tuple-element.68), channel_id=1, source_target_pairs={{0,32},{16,48},{32,64},{48,80},{64,96},{80,112},{96,128},{112,144}... | collective-permute-start | bytes 786440 | tf_op jit(solution)/shard_map/ppermute | solution.py:27
  60.7 10.3 %collective-permute-start.15 = (f16[64,2048]{1,0:T(8,128)(2,1)S(1)}, f16[64,2048]{1,0:T(8,128)(2,1)S(1)}, u32[]{:S(2)}, u32[]{:S(2)}) collective-permute-start(f16[64,2048]{1,0:T(8,128)(2,1)S(1)} %fusion.5), channel_id=1, source_target_pairs={{0,32},{16,48},{32,64},{48,80},{64,96},{80,112},{96,128},{112,144}... | collective-permute-start | bytes 786440 | tf_op jit(solution)/shard_map/ppermute | solution.py:27
  65.5 8.4 %collective-permute-start.13 = (f16[64,2048]{1,0:T(8,128)(2,1)S(1)}, f16[64,2048]{1,0:T(8,128)(2,1)S(1)}, u32[]{:S(2)}, u32[]{:S(2)}) collective-permute-start(f16[64,2048]{1,0:T(8,128)(2,1)S(1)} %fusion.3), channel_id=1, source_target_pairs={{0,224},{16,240},{32,0},{48,16},{64,32},{80,48},{96,64},{112,80},{... | collective-permute-start | bytes 786440 | tf_op jit(solution)/shard_map/ppermute | solution.py:27
  71.1 6.8 %collective-permute-start.16 = (f16[64,2048]{1,0:T(8,128)(2,1)S(1)}, f16[64,2048]{1,0:T(8,128)(2,1)S(1)}, u32[]{:S(2)}, u32[]{:S(2)}) collective-permute-start(f16[64,2048]{1,0:T(8,128)(2,1)S(1)} %fusion.2), channel_id=1, source_target_pairs={{0,16},{16,0},{32,48},{48,32},{64,80},{80,64},{96,112},{112,96},{1... | collective-permute-start | bytes 786440 | tf_op jit(solution)/shard_map/ppermute | solution.py:31
  74.0 8.9 %collective-permute-start.14 = (f16[64,2048]{1,0:T(8,128)(2,1)S(1)}, f16[64,2048]{1,0:T(8,128)(2,1)S(1)}, u32[]{:S(2)}, u32[]{:S(2)}) collective-permute-start(f16[64,2048]{1,0:T(8,128)(2,1)S(1)} %fusion.14), channel_id=1, source_target_pairs={{0,16},{16,0},{32,48},{48,32},{64,80},{80,64},{96,112},{112,96},{1... | collective-permute-start | bytes 786440 | tf_op jit(solution)/shard_map/ppermute | solution.py:31
  83.2 6.5 %collective-permute-start.17 = (bf16[64,2048]{1,0:T(8,128)(2,1)S(1)}, bf16[64,2048]{1,0:T(8,128)(2,1)S(1)}, u32[]{:S(2)}, u32[]{:S(2)}) collective-permute-start(bf16[64,2048]{1,0:T(8,128)(2,1)S(1)} %get-tuple-element.66), channel_id=1, source_target_pairs={{0,32},{16,48},{32,64},{48,80},{64,96},{80,112},{96,128},{112,144}... | collective-permute-start | bytes 786440 | tf_op jit(solution)/shard_map/ppermute | solution.py:27
  83.3 6.4 %collective-permute-start.18 = (bf16[64,2048]{1,0:T(8,128)(2,1)S(1)}, bf16[64,2048]{1,0:T(8,128)(2,1)S(1)}, u32[]{:S(2)}, u32[]{:S(2)}) collective-permute-start(bf16[64,2048]{1,0:T(8,128)(2,1)S(1)} %get-tuple-element.66), channel_id=1, source_target_pairs={{0,224},{16,240},{32,0},{48,16},{64,32},{80,48},{96,64},{112,80},{... | collective-permute-start | bytes 786440 | tf_op jit(solution)/shard_map/ppermute | solution.py:27
  86.1 6.5 %collective-permute-start.25 = (bf16[64,2048]{1,0:T(8,128)(2,1)S(1)}, bf16[64,2048]{1,0:T(8,128)(2,1)S(1)}, u32[]{:S(2)}, u32[]{:S(2)}) collective-permute-start(bf16[64,2048]{1,0:T(8,128)(2,1)S(1)} %get-tuple-element.56), channel_id=1, source_target_pairs={{0,224},{16,240},{32,0},{48,16},{64,32},{80,48},{96,64},{112,80},{... | collective-permute-start | bytes 786440 | tf_op jit(solution)/shard_map/ppermute | solution.py:27
  86.2 7.9 %collective-permute-start.24 = (bf16[64,2048]{1,0:T(8,128)(2,1)S(1)}, bf16[64,2048]{1,0:T(8,128)(2,1)S(1)}, u32[]{:S(2)}, u32[]{:S(2)}) collective-permute-start(bf16[64,2048]{1,0:T(8,128)(2,1)S(1)} %get-tuple-element.56), channel_id=1, source_target_pairs={{0,32},{16,48},{32,64},{48,80},{64,96},{80,112},{96,128},{112,144}... | collective-permute-start | bytes 786440 | tf_op jit(solution)/shard_map/ppermute | solution.py:27
  89.7 8.9 %collective-permute-start.20 = (bf16[64,2048]{1,0:T(8,128)(2,1)S(1)}, bf16[64,2048]{1,0:T(8,128)(2,1)S(1)}, u32[]{:S(2)}, u32[]{:S(2)}) collective-permute-start(bf16[64,2048]{1,0:T(8,128)(2,1)S(1)} %collective-permute-done.18), channel_id=1, source_target_pairs={{0,224},{16,240},{32,0},{48,16},{64,32},{80,48},{96,64},{112,80},{... | collective-permute-start | bytes 786440 | tf_op jit(solution)/shard_map/ppermute | solution.py:27
  92.4 8.8 %collective-permute-start.19 = (bf16[64,2048]{1,0:T(8,128)(2,1)S(1)}, bf16[64,2048]{1,0:T(8,128)(2,1)S(1)}, u32[]{:S(2)}, u32[]{:S(2)}) collective-permute-start(bf16[64,2048]{1,0:T(8,128)(2,1)S(1)} %collective-permute-done.17), channel_id=1, source_target_pairs={{0,32},{16,48},{32,64},{48,80},{64,96},{80,112},{96,128},{112,144}... | collective-permute-start | bytes 786440 | tf_op jit(solution)/shard_map/ppermute | solution.py:27
  94.1 10.1 %collective-permute-start.26 = (bf16[64,2048]{1,0:T(8,128)(2,1)S(1)}, bf16[64,2048]{1,0:T(8,128)(2,1)S(1)}, u32[]{:S(2)}, u32[]{:S(2)}) collective-permute-start(bf16[64,2048]{1,0:T(8,128)(2,1)S(1)} %collective-permute-done.25), channel_id=1, source_target_pairs={{0,224},{16,240},{32,0},{48,16},{64,32},{80,48},{96,64},{112,80},{... | collective-permute-start | bytes 786440 | tf_op jit(solution)/shard_map/ppermute | solution.py:27
  96.0 8.1 %collective-permute-start.27 = (bf16[64,2048]{1,0:T(8,128)(2,1)S(1)}, bf16[64,2048]{1,0:T(8,128)(2,1)S(1)}, u32[]{:S(2)}, u32[]{:S(2)}) collective-permute-start(bf16[64,2048]{1,0:T(8,128)(2,1)S(1)} %collective-permute-done.24), channel_id=1, source_target_pairs={{0,32},{16,48},{32,64},{48,80},{64,96},{80,112},{96,128},{112,144}... | collective-permute-start | bytes 786440 | tf_op jit(solution)/shard_map/ppermute | solution.py:27
  101.2 8.6 %collective-permute-start.22 = (bf16[64,2048]{1,0:T(8,128)(2,1)S(1)}, bf16[64,2048]{1,0:T(8,128)(2,1)S(1)}, u32[]{:S(2)}, u32[]{:S(2)}) collective-permute-start(bf16[64,2048]{1,0:T(8,128)(2,1)S(1)} %collective-permute-done.20), channel_id=1, source_target_pairs={{0,224},{16,240},{32,0},{48,16},{64,32},{80,48},{96,64},{112,80},{... | collective-permute-start | bytes 786440 | tf_op jit(solution)/shard_map/ppermute | solution.py:27
  102.0 9.0 %collective-permute-start.21 = (bf16[64,2048]{1,0:T(8,128)(2,1)S(1)}, bf16[64,2048]{1,0:T(8,128)(2,1)S(1)}, u32[]{:S(2)}, u32[]{:S(2)}) collective-permute-start(bf16[64,2048]{1,0:T(8,128)(2,1)S(1)} %collective-permute-done.19), channel_id=1, source_target_pairs={{0,32},{16,48},{32,64},{48,80},{64,96},{80,112},{96,128},{112,144}... | collective-permute-start | bytes 786440 | tf_op jit(solution)/shard_map/ppermute | solution.py:27
  104.2 16.9 %copy-start.6 = (bf16[64,2048]{1,0:T(8,128)(2,1)}, bf16[64,2048]{1,0:T(8,128)(2,1)S(1)}, u32[]{:S(2)}) copy-start(bf16[64,2048]{1,0:T(8,128)(2,1)S(1)} %collective-permute-done.27) | copy-start | bytes 786436
  104.2 11.2 %collective-permute-start.28 = (bf16[64,2048]{1,0:T(8,128)(2,1)S(1)}, bf16[64,2048]{1,0:T(8,128)(2,1)S(1)}, u32[]{:S(2)}, u32[]{:S(2)}) collective-permute-start(bf16[64,2048]{1,0:T(8,128)(2,1)S(1)} %collective-permute-done.26), channel_id=1, source_target_pairs={{0,224},{16,240},{32,0},{48,16},{64,32},{80,48},{96,64},{112,80},{... | collective-permute-start | bytes 786440 | tf_op jit(solution)/shard_map/ppermute | solution.py:27
  107.6 8.8 %collective-permute-start.29 = (bf16[64,2048]{1,0:T(8,128)(2,1)S(1)}, bf16[64,2048]{1,0:T(8,128)(2,1)}, u32[]{:S(2)}, u32[]{:S(2)}) collective-permute-start(bf16[64,2048]{1,0:T(8,128)(2,1)S(1)} %collective-permute-done.27), channel_id=1, source_target_pairs={{0,32},{16,48},{32,64},{48,80},{64,96},{80,112},{96,128},{112,144}... | collective-permute-start | bytes 786440 | tf_op jit(solution)/shard_map/ppermute | solution.py:27
  111.0 10.0 %collective-permute-start.23 = (bf16[64,2048]{1,0:T(8,128)(2,1)S(1)}, bf16[64,2048]{1,0:T(8,128)(2,1)S(1)}, u32[]{:S(2)}, u32[]{:S(2)}) collective-permute-start(bf16[64,2048]{1,0:T(8,128)(2,1)S(1)} %collective-permute-done.22), channel_id=1, source_target_pairs={{0,224},{16,240},{32,0},{48,16},{64,32},{80,48},{96,64},{112,80},{... | collective-permute-start | bytes 786440 | tf_op jit(solution)/shard_map/ppermute | solution.py:27
  116.4 22.0 %collective-permute-start.30 = (bf16[64,2048]{1,0:T(8,128)(2,1)}, bf16[64,2048]{1,0:T(8,128)(2,1)}, u32[]{:S(2)}, u32[]{:S(2)}) collective-permute-start(bf16[64,2048]{1,0:T(8,128)(2,1)} %collective-permute-done.29), channel_id=1, source_target_pairs={{0,32},{16,48},{32,64},{48,80},{64,96},{80,112},{96,128},{112,144}... | collective-permute-start | bytes 786440 | tf_op jit(solution)/shard_map/ppermute | solution.py:27
  116.5 4.6 %copy-start.2 = (bf16[512,2048]{1,0:T(8,128)(2,1)}, bf16[512,2048]{1,0:T(8,128)(2,1)S(1)}, u32[]{:S(2)}) copy-start(bf16[512,2048]{1,0:T(8,128)(2,1)S(1)} %constant_dynamic-update-slice_fusion.4) | copy-start | bytes 6291460
  121.1 2.1 %copy-start.1 = (bf16[8,64,2048]{2,1,0:T(8,128)(2,1)}, bf16[8,64,2048]{2,1,0:T(8,128)(2,1)S(1)}, u32[]{:S(2)}) copy-start(bf16[8,64,2048]{2,1,0:T(8,128)(2,1)S(1)} %bitcast_dynamic-update-slice_fusion) | copy-start | bytes 6291460
  123.2 22.1 %all-to-all-start.1 = ((bf16[16,32,512]{2,1,0:T(8,128)(2,1)}), bf16[16,32,512]{2,1,0:T(8,128)(2,1)S(1)}, u32[]{:S(2)}, u32[]{:S(2)}) async-start(bf16[16,32,512]{2,1,0:T(8,128)(2,1)} %bitcast.127), calls=%async_computation.1 | async-start | bytes 1048576 | tf_op jit(solution)/shard_map/all_to_all | solution.py:151
  134.0 4.4 %copy-start.3 = (bf16[512,2048]{1,0:T(8,128)(2,1)S(1)}, bf16[512,2048]{1,0:T(8,128)(2,1)}, u32[]{:S(2)}) copy-start(bf16[512,2048]{1,0:T(8,128)(2,1)} %copy-done.2) | copy-start | bytes 6291460

commit v3 on v2

--- a/solution.py
+++ b/solution.py
@@ -90,7 +90,8 @@
     )
     both = both.reshape(tokens, 2 * width)
     inputs_all, cotangent_all = both[:, :width], both[:, width:]
-    sparse_in, sparse_out = together(spread(weight_in, mask_in), spread(weight_out, mask_out))
+    (sparse_in,) = together(spread(weight_in, mask_in))
+    (sparse_out,) = together(spread(weight_out, mask_out))
     pre_part = jnp.dot(inputs_all, sparse_in, preferred_element_type=F32)
     act_part = lax.dot_general(
         cotangent_all, sparse_out, (((1,), (1,)), ((), ())), preferred_element_type=F32
@@ -153,9 +154,10 @@
     grad_weight_in = grad_of_weight_in(inputs_all, gathered, mask_in)
     turned = cotangent_all.reshape(depth, chunk, width)
     turned = lax.dynamic_slice_in_dim(jnp.concatenate([turned, turned]), z, depth, axis=0)
-    act, turned = together(
-        jnp.concatenate([acts[d] for d in range(depth)], axis=0), turned.reshape(tokens, width)
-    )
+    act = jnp.zeros((depth, chunk, act.shape[1]), BF16)
+    for d in [0] + [d for k in range(1, far) for d in (k, depth - k)] + [far]:
+        act = lax.dynamic_update_index_in_dim(act, acts[d], d, 0)
+    act, turned = together(act.reshape(tokens, -1), turned.reshape(tokens, width))
     grad_weight_out = lax.dot_general(
         act, turned, (((0,), (0,)), ((), ())), preferred_element_type=F32
     )

time: 147 us -> 143 us (0.973)
  starting transfers between devices: 51.2 us -> 48 us
  local copies, waits for them, and re-layouts: 8.42 us -> 6.42 us
  waiting for transfers between devices: 67.3 us -> 69 us
    unnamed x25 -> x16, local copies, waits for them, and re-layouts: 4.56 us -> 1.24 us
    ppermute x28, starting transfers between devices: 30.2 us -> 28.3 us  [send(): return lax.ppermute(value, 'row', ring(shift, rows))]
where the time goes in v3:
time: 143 us; the launch traced here: 142 us
  waiting for transfers between devices  69 us (48%)
  starting transfers between devices  48 us (34%)
  matrix products  7.96 us (6%)
  local copies, waits for them, and re-layouts  6.42 us (4%)
  other arithmetic  5.65 us (4%)
  Pallas kernels  4.21 us (3%)
    ppermute x28, waiting for transfers between devices, send(): return lax.ppermute(value, 'row', ring(shift, rows))  52.5 us
    ppermute x28, starting transfers between devices, send(): return lax.ppermute(value, 'row', ring(shift, rows))  28.3 us
    all_to_all x1, starting transfers between devices, shards(): pieces = lax.all_to_all(pieces, 'col', 0, 0)  9.44 us
    all_to_all x1, waiting for transfers between devices, shards(): mine = lax.all_to_all(mine, 'col', 0, 0, axis_index_groups=same_core)  7.76 us
    ppermute x2, waiting for transfers between devices, swap(): return lax.ppermute(value, 'row', [(r, r ^ 1) for r in range(rows)])  7.69 us
    all_to_all x1, starting transfers between devices, shards(): mine = lax.all_to_all(mine, 'col', 0, 0, axis_index_groups=same_core)  5.86 us
    pallas_call x1, Pallas kernels, grad_of_weight_in(): pl.pallas_call(weight_in_kernel, out_shape=jax.ShapeDtypeStruct((features...  4.21 us
    ppermute x2, starting transfers between devices, swap(): return lax.ppermute(value, 'row', [(r, r ^ 1) for r in range(rows)])  3.53 us
  transfers between devices with their start and end apart: 33, of which 27 were waited for; matrix products, arithmetic and copies ran while one was open for 10% of the time, Pallas kernels for 3%

profile of v3, /device:TPU:1, one launch (start us, length us, event | category | flops | bytes accessed | tf_op | source)
XLA Modules:
  0.0 142.2 jit_solution(4711140559143218493)
XLA Ops:
  0.7 0.8 pad_maximum_fusion.1
  1.4 0.9 broadcast_in_dim.59
  2.3 5.9 %all-to-all-start = ((bf16[8,32,1024]{2,1,0:T(8,128)(2,1)}), bf16[8,32,1024]{2,1,0:T(8,128)(2,1)S(1)}, u32[]{:S(2)}, u32[]{:S(2)}) async-start(bf16[8,32,1024]{2,1,0:T(8,128)(2,1)} %broadcast_in_dim.59), calls=%async_computation | async-start | bytes 1048576 | tf_op jit(solution)/shard_map/all_to_all | solution.py:86
  8.4 0.6 mul.145
  9.0 1.6 %bitcast_multiply_fusion.2 = bf16[2048,512]{1,0:T(8,128)(2,1)} fusion(bf16[2048,512]{1,0:T(8,128)(2,1)S(1)} %copy-done.4, bf16[256,8,4,128]{3,2,1,0:T(4,128)(2,1)S(1)} %bitcast.138), kind=kLoop, calls=%fused_computation.2 | loop fusion | flops 1048576 | bytes 6291456 | tf_op jit(solution)/shard_map/mul | solution.py:18
  10.6 7.8 %all-to-all-done = bf16[8,32,1024]{2,1,0:T(8,128)(2,1)S(1)} async-done(((bf16[8,32,1024]{2,1,0:T(8,128)(2,1)}), bf16[8,32,1024]{2,1,0:T(8,128)(2,1)S(1)}, u32[]{:S(2)}, u32[]{:S(2)}) %all-to-all-start) | async-done | bytes 524320 | tf_op jit(solution)/shard_map/all_to_all | solution.py:86
  18.4 0.8 collective-permute-start
  19.2 0.3 mul.156
  19.5 0.4 copy-done.5
  19.9 0.5 bitcast_multiply_fusion.1
  20.5 0.3 collective-permute-done
  20.9 0.8 copy-done
  21.7 1.3 fusion.19
  23.1 5.7 %collective-permute-start.4 = (f16[64,2048]{1,0:T(8,128)(2,1)S(1)}, f16[64,2048]{1,0:T(8,128)(2,1)S(1)}, u32[]{:S(2)}, u32[]{:S(2)}) collective-permute-start(f16[64,2048]{1,0:T(8,128)(2,1)S(1)} %get-tuple-element.73), channel_id=1, source_target_pairs={{0,224},{16,240},{32,0},{48,16},{64,32},{80,48},{96,64},{112,80},{... | collective-permute-start | bytes 786440 | tf_op jit(solution)/shard_map/ppermute | solution.py:27
  28.8 1.3 fusion.21
  30.2 2.7 %collective-permute-start.2 = (f16[64,2048]{1,0:T(8,128)(2,1)S(1)}, f16[64,2048]{1,0:T(8,128)(2,1)S(1)}, u32[]{:S(2)}, u32[]{:S(2)}) collective-permute-start(f16[64,2048]{1,0:T(8,128)(2,1)S(1)} %get-tuple-element.67), channel_id=1, source_target_pairs={{0,224},{16,240},{32,0},{48,16},{64,32},{80,48},{96,64},{112,80},{... | collective-permute-start | bytes 786440 | tf_op jit(solution)/shard_map/ppermute | solution.py:27
  32.9 0.6 collective-permute-done.4
  33.5 3.1 %collective-permute-done.3 = f16[64,2048]{1,0:T(8,128)(2,1)S(1)} collective-permute-done((f16[64,2048]{1,0:T(8,128)(2,1)S(1)}, f16[64,2048]{1,0:T(8,128)(2,1)S(1)}, u32[]{:S(2)}, u32[]{:S(2)}) %collective-permute-start.3) | collective-permute-done | bytes 262176 | tf_op jit(solution)/shard_map/ppermute | solution.py:27
  36.9 2.3 %collective-permute-done.2 = f16[64,2048]{1,0:T(8,128)(2,1)S(1)} collective-permute-done((f16[64,2048]{1,0:T(8,128)(2,1)S(1)}, f16[64,2048]{1,0:T(8,128)(2,1)S(1)}, u32[]{:S(2)}, u32[]{:S(2)}) %collective-permute-start.2) | collective-permute-done | bytes 262176 | tf_op jit(solution)/shard_map/ppermute | solution.py:27
  39.2 3.4 %collective-permute-done.1 = f16[64,2048]{1,0:T(8,128)(2,1)S(1)} collective-permute-done((f16[64,2048]{1,0:T(8,128)(2,1)S(1)}, f16[64,2048]{1,0:T(8,128)(2,1)S(1)}, u32[]{:S(2)}, u32[]{:S(2)}) %collective-permute-start.1) | collective-permute-done | bytes 262176 | tf_op jit(solution)/shard_map/ppermute | solution.py:27
  42.8 1.5 %collective-permute-start.5 = (f16[64,2048]{1,0:T(8,128)(2,1)S(1)}, f16[64,2048]{1,0:T(8,128)(2,1)S(1)}, u32[]{:S(2)}, u32[]{:S(2)}) collective-permute-start(f16[64,2048]{1,0:T(8,128)(2,1)S(1)} %get-tuple-element.66), channel_id=1, source_target_pairs={{0,32},{16,48},{32,64},{48,80},{64,96},{80,112},{96,128},{112,144}... | collective-permute-start | bytes 786440 | tf_op jit(solution)/shard_map/ppermute | solution.py:27
  44.3 3.7 %collective-permute-done.8 = f16[64,2048]{1,0:T(8,128)(2,1)S(1)} collective-permute-done((f16[64,2048]{1,0:T(8,128)(2,1)S(1)}, f16[64,2048]{1,0:T(8,128)(2,1)S(1)}, u32[]{:S(2)}, u32[]{:S(2)}) %collective-permute-start.8) | collective-permute-done | bytes 262176 | tf_op jit(solution)/shard_map/ppermute | solution.py:27
  48.3 0.3 collective-permute-start.11
  48.6 4.1 %collective-permute-done.6 = f16[64,2048]{1,0:T(8,128)(2,1)S(1)} collective-permute-done((f16[64,2048]{1,0:T(8,128)(2,1)S(1)}, f16[64,2048]{1,0:T(8,128)(2,1)S(1)}, u32[]{:S(2)}, u32[]{:S(2)}) %collective-permute-start.6) | collective-permute-done | bytes 262176 | tf_op jit(solution)/shard_map/ppermute | solution.py:27
  52.7 0.5 collective-permute-done.5
  53.2 1.1 collective-permute-start.12
  54.6 1.5 %collective-permute-start.9 = (f16[64,2048]{1,0:T(8,128)(2,1)S(1)}, f16[64,2048]{1,0:T(8,128)(2,1)S(1)}, u32[]{:S(2)}, u32[]{:S(2)}) collective-permute-start(f16[64,2048]{1,0:T(8,128)(2,1)S(1)} %get-tuple-element.64), channel_id=1, source_target_pairs={{0,32},{16,48},{32,64},{48,80},{64,96},{80,112},{96,128},{112,144}... | collective-permute-start | bytes 786440 | tf_op jit(solution)/shard_map/ppermute | solution.py:27
  56.0 3.2 %collective-permute-done.12 = f16[64,2048]{1,0:T(8,128)(2,1)S(1)} collective-permute-done((f16[64,2048]{1,0:T(8,128)(2,1)S(1)}, f16[64,2048]{1,0:T(8,128)(2,1)S(1)}, u32[]{:S(2)}, u32[]{:S(2)}) %collective-permute-start.12) | collective-permute-done | bytes 262176 | tf_op jit(solution)/shard_map/ppermute | solution.py:27
  59.5 4.0 %collective-permute-done.10 = f16[64,2048]{1,0:T(8,128)(2,1)S(1)} collective-permute-done((f16[64,2048]{1,0:T(8,128)(2,1)S(1)}, f16[64,2048]{1,0:T(8,128)(2,1)S(1)}, u32[]{:S(2)}, u32[]{:S(2)}) %collective-permute-start.10) | collective-permute-done | bytes 262176 | tf_op jit(solution)/shard_map/ppermute | solution.py:27
  63.4 0.5 collective-permute-done.9
  64.0 1.3 collective-permute-start.13
  65.3 4.2 %collective-permute-done.15 = f16[64,2048]{1,0:T(8,128)(2,1)S(1)} collective-permute-done((f16[64,2048]{1,0:T(8,128)(2,1)S(1)}, f16[64,2048]{1,0:T(8,128)(2,1)S(1)}, u32[]{:S(2)}, u32[]{:S(2)}) %collective-permute-start.15) | collective-permute-done | bytes 262176 | tf_op jit(solution)/shard_map/ppermute | solution.py:27
  69.7 2.7 %collective-permute-start.16 = (f16[64,2048]{1,0:T(8,128)(2,1)S(1)}, f16[64,2048]{1,0:T(8,128)(2,1)S(1)}, u32[]{:S(2)}, u32[]{:S(2)}) collective-permute-start(f16[64,2048]{1,0:T(8,128)(2,1)S(1)} %fusion.2), channel_id=1, source_target_pairs={{0,16},{16,0},{32,48},{48,32},{64,80},{80,64},{96,112},{112,96},{1... | collective-permute-start | bytes 786440 | tf_op jit(solution)/shard_map/ppermute | solution.py:31
  72.5 0.8 collective-permute-start.14
  73.3 3.1 %collective-permute-done.16 = f16[64,2048]{1,0:T(8,128)(2,1)S(1)} collective-permute-done((f16[64,2048]{1,0:T(8,128)(2,1)S(1)}, f16[64,2048]{1,0:T(8,128)(2,1)S(1)}, u32[]{:S(2)}, u32[]{:S(2)}) %collective-permute-start.16) | collective-permute-done | bytes 262176 | tf_op jit(solution)/shard_map/ppermute | solution.py:31
  76.5 0.3 add_multiply_fusion
  76.7 4.5 %collective-permute-done.14 = f16[64,2048]{1,0:T(8,128)(2,1)S(1)} collective-permute-done((f16[64,2048]{1,0:T(8,128)(2,1)S(1)}, f16[64,2048]{1,0:T(8,128)(2,1)S(1)}, u32[]{:S(2)}, u32[]{:S(2)}) %collective-permute-start.14) | collective-permute-done | bytes 262176 | tf_op jit(solution)/shard_map/ppermute | solution.py:31
  81.3 0.2 broadcast.53
  81.8 2.7 %collective-permute-start.18 = (bf16[64,2048]{1,0:T(8,128)(2,1)S(1)}, bf16[64,2048]{1,0:T(8,128)(2,1)S(1)}, u32[]{:S(2)}, u32[]{:S(2)}) collective-permute-start(bf16[64,2048]{1,0:T(8,128)(2,1)S(1)} %get-tuple-element.62), channel_id=1, source_target_pairs={{0,224},{16,240},{32,0},{48,16},{64,32},{80,48},{96,64},{112,80},{... | collective-permute-start | bytes 786440 | tf_op jit(solution)/shard_map/ppermute | solution.py:27
  84.4 0.9 fusion.23
  85.6 1.5 %collective-permute-start.24 = (bf16[64,2048]{1,0:T(8,128)(2,1)S(1)}, bf16[64,2048]{1,0:T(8,128)(2,1)S(1)}, u32[]{:S(2)}, u32[]{:S(2)}) collective-permute-start(bf16[64,2048]{1,0:T(8,128)(2,1)S(1)} %get-tuple-element.52), channel_id=1, source_target_pairs={{0,32},{16,48},{32,64},{48,80},{64,96},{80,112},{96,128},{112,144}... | collective-permute-start | bytes 786440 | tf_op jit(solution)/shard_map/ppermute | solution.py:27
  87.1 0.2 dynamic_update_slice.58
  87.3 0.9 collective-permute-done.17
  88.2 2.7 %collective-permute-start.20 = (bf16[64,2048]{1,0:T(8,128)(2,1)S(1)}, bf16[64,2048]{1,0:T(8,128)(2,1)S(1)}, u32[]{:S(2)}, u32[]{:S(2)}) collective-permute-start(bf16[64,2048]{1,0:T(8,128)(2,1)S(1)} %collective-permute-done.18), channel_id=1, source_target_pairs={{0,224},{16,240},{32,0},{48,16},{64,32},{80,48},{96,64},{112,80},{... | collective-permute-start | bytes 786440 | tf_op jit(solution)/shard_map/ppermute | solution.py:27
  91.0 1.9 %collective-permute-done.25 = bf16[64,2048]{1,0:T(8,128)(2,1)S(1)} collective-permute-done((bf16[64,2048]{1,0:T(8,128)(2,1)S(1)}, bf16[64,2048]{1,0:T(8,128)(2,1)S(1)}, u32[]{:S(2)}, u32[]{:S(2)}) %collective-permute-start.25) | collective-permute-done | bytes 262176 | tf_op jit(solution)/shard_map/ppermute | solution.py:27
  92.9 1.5 %collective-permute-done.24 = bf16[64,2048]{1,0:T(8,128)(2,1)S(1)} collective-permute-done((bf16[64,2048]{1,0:T(8,128)(2,1)S(1)}, bf16[64,2048]{1,0:T(8,128)(2,1)S(1)}, u32[]{:S(2)}, u32[]{:S(2)}) %collective-permute-start.24) | collective-permute-done | bytes 262176 | tf_op jit(solution)/shard_map/ppermute | solution.py:27
  94.4 1.4 collective-permute-start.27
  95.9 2.6 %collective-permute-done.20 = bf16[64,2048]{1,0:T(8,128)(2,1)S(1)} collective-permute-done((bf16[64,2048]{1,0:T(8,128)(2,1)S(1)}, bf16[64,2048]{1,0:T(8,128)(2,1)S(1)}, u32[]{:S(2)}, u32[]{:S(2)}) %collective-permute-start.20) | collective-permute-done | bytes 262176 | tf_op jit(solution)/shard_map/ppermute | solution.py:27
  98.5 2.1 %collective-permute-done.19 = bf16[64,2048]{1,0:T(8,128)(2,1)S(1)} collective-permute-done((bf16[64,2048]{1,0:T(8,128)(2,1)S(1)}, bf16[64,2048]{1,0:T(8,128)(2,1)S(1)}, u32[]{:S(2)}, u32[]{:S(2)}) %collective-permute-start.19) | collective-permute-done | bytes 262176 | tf_op jit(solution)/shard_map/ppermute | solution.py:27
  100.6 1.5 %collective-permute-start.21 = (bf16[64,2048]{1,0:T(8,128)(2,1)S(1)}, bf16[64,2048]{1,0:T(8,128)(2,1)S(1)}, u32[]{:S(2)}, u32[]{:S(2)}) collective-permute-start(bf16[64,2048]{1,0:T(8,128)(2,1)S(1)} %collective-permute-done.19), channel_id=1, source_target_pairs={{0,32},{16,48},{32,64},{48,80},{64,96},{80,112},{96,128},{112,144}... | collective-permute-start | bytes 786440 | tf_op jit(solution)/shard_map/ppermute | solution.py:27
  102.2 1.9 %collective-permute-done.26 = bf16[64,2048]{1,0:T(8,128)(2,1)S(1)} collective-permute-done((bf16[64,2048]{1,0:T(8,128)(2,1)S(1)}, bf16[64,2048]{1,0:T(8,128)(2,1)S(1)}, u32[]{:S(2)}, u32[]{:S(2)}) %collective-permute-start.26) | collective-permute-done | bytes 262176 | tf_op jit(solution)/shard_map/ppermute | solution.py:27
  104.1 1.9 %collective-permute-start.28 = (bf16[64,2048]{1,0:T(8,128)(2,1)S(1)}, bf16[64,2048]{1,0:T(8,128)(2,1)S(1)}, u32[]{:S(2)}, u32[]{:S(2)}) collective-permute-start(bf16[64,2048]{1,0:T(8,128)(2,1)S(1)} %collective-permute-done.26), channel_id=1, source_target_pairs={{0,224},{16,240},{32,0},{48,16},{64,32},{80,48},{96,64},{112,80},{... | collective-permute-start | bytes 786440 | tf_op jit(solution)/shard_map/ppermute | solution.py:27
  106.1 3.6 %collective-permute-done.22 = bf16[64,2048]{1,0:T(8,128)(2,1)S(1)} collective-permute-done((bf16[64,2048]{1,0:T(8,128)(2,1)S(1)}, bf16[64,2048]{1,0:T(8,128)(2,1)S(1)}, u32[]{:S(2)}, u32[]{:S(2)}) %collective-permute-start.22) | collective-permute-done | bytes 262176 | tf_op jit(solution)/shard_map/ppermute | solution.py:27
  109.7 1.9 %collective-permute-start.23 = (bf16[64,2048]{1,0:T(8,128)(2,1)S(1)}, bf16[64,2048]{1,0:T(8,128)(2,1)S(1)}, u32[]{:S(2)}, u32[]{:S(2)}) collective-permute-start(bf16[64,2048]{1,0:T(8,128)(2,1)S(1)} %collective-permute-done.22), channel_id=1, source_target_pairs={{0,224},{16,240},{32,0},{48,16},{64,32},{80,48},{96,64},{112,80},{... | collective-permute-start | bytes 786440 | tf_op jit(solution)/shard_map/ppermute | solution.py:27
  111.7 3.0 %collective-permute-done.28 = bf16[64,2048]{1,0:T(8,128)(2,1)S(1)} collective-permute-done((bf16[64,2048]{1,0:T(8,128)(2,1)S(1)}, bf16[64,2048]{1,0:T(8,128)(2,1)S(1)}, u32[]{:S(2)}, u32[]{:S(2)}) %collective-permute-start.28) | collective-permute-done | bytes 262176 | tf_op jit(solution)/shard_map/ppermute | solution.py:27
  114.9 5.2 %collective-permute-done.23 = bf16[64,2048]{1,0:T(8,128)(2,1)S(1)} collective-permute-done((bf16[64,2048]{1,0:T(8,128)(2,1)S(1)}, bf16[64,2048]{1,0:T(8,128)(2,1)S(1)}, u32[]{:S(2)}, u32[]{:S(2)}) %collective-permute-start.23) | collective-permute-done | bytes 262176 | tf_op jit(solution)/shard_map/ppermute | solution.py:27
  120.1 2.1 %convolution_convert_fusion = bf16[512,512]{1,0:T(8,128)(2,1)} fusion(bf16[512,2048]{1,0:T(8,128)(2,1)S(1)} %bitcast.140, bf16[512,2048]{1,0:T(8,128)(2,1)S(1)} %copy-done.1), kind=kOutput, calls=%fused_computation.3 | convolution fusion | flops 1074003968 | bytes 4718592 | tf_op jit(solution)/shard_map/dot_general | solution.py:148
  122.2 9.4 %all-to-all-start.1 = ((bf16[16,32,512]{2,1,0:T(8,128)(2,1)}), bf16[16,32,512]{2,1,0:T(8,128)(2,1)S(1)}, u32[]{:S(2)}, u32[]{:S(2)}) async-start(bf16[16,32,512]{2,1,0:T(8,128)(2,1)} %bitcast.145), calls=%async_computation.1 | async-start | bytes 1048576 | tf_op jit(solution)/shard_map/all_to_all | solution.py:152
  131.7 4.2 %shard_map.85 = f32[512,2048]{1,0:T(8,128)} custom-call(s32[4,16]{1,0:T(4,128)} %mask.1, bf16[512,512]{1,0:T(8,128)(2,1)} %get-tuple-element.51.x, bf16[512,2048]{1,0:T(8,128)(2,1)} %bitcast.141), custom_call_target="tpu_custom_call" | custom-call | flops 1073741824 | bytes 8388608 | tf_op jit(solution)/shard_map/pallas_call | solution.py:57
  135.9 1.0 bitcast_dynamic-update-slice_fusion
  136.8 0.6 mul.187
  137.4 3.3 %bitcast_multiply_fusion = f32[2048,512]{1,0:T(8,128)} fusion(f32[256,8,4,128]{3,2,1,0:T(4,128)S(1)} %bitcast.123, bf16[512,2048]{1,0:T(8,128)(2,1)S(1)} %bitcast.134, bf16[512,512]{1,0:T(8,128)(2,1)S(1)} %bitcast.142), kind=kOutput, calls=%fused_computation | convolution fusion | flops 1074790400 | bytes 11010048 | tf_op jit(solution)/shard_map/dot_general | solution.py:161
  140.8 0.8 all-to-all-done.1
  141.5 0.7 convert_reduce_fusion
  (67 shorter events, 3.2 us)
Async XLA Ops:
  0.6 7.5 %copy-start.6 = (s32[4,16]{1,0:T(4,128)S(1)}, s32[4,16]{1,0:T(4,128)}, u32[]{:S(2)}) copy-start(s32[4,16]{1,0:T(4,128)} %mask.1) | copy-start | bytes 772
  0.6 7.5 %copy-start.7 = (s32[16,4]{0,1:T(4,128)S(1)}, s32[16,4]{0,1:T(4,128)}, u32[]{:S(2)}) copy-start(s32[16,4]{0,1:T(4,128)} %param.11) | copy-start | bytes 772
  1.4 7.6 %copy-start.4 = (bf16[2048,512]{1,0:T(8,128)(2,1)S(1)}, bf16[2048,512]{1,0:T(8,128)(2,1)}, u32[]{:S(2)}) copy-start(bf16[2048,512]{1,0:T(8,128)(2,1)} %param.9) | copy-start | bytes 6291460
  2.3 16.1 %all-to-all-start = ((bf16[8,32,1024]{2,1,0:T(8,128)(2,1)}), bf16[8,32,1024]{2,1,0:T(8,128)(2,1)S(1)}, u32[]{:S(2)}, u32[]{:S(2)}) async-start(bf16[8,32,1024]{2,1,0:T(8,128)(2,1)} %broadcast_in_dim.59), calls=%async_computation | async-start | bytes 1048576 | tf_op jit(solution)/shard_map/all_to_all | solution.py:86
  18.4 1.6 %copy-start.5 = (bf16[512,2048]{1,0:T(8,128)(2,1)S(1)}, bf16[512,2048]{1,0:T(8,128)(2,1)}, u32[]{:S(2)}) copy-start(bf16[512,2048]{1,0:T(8,128)(2,1)} %param.8) | copy-start | bytes 6291460
  18.4 2.4 %collective-permute-start = (bf16[8,32,1024]{2,1,0:T(8,128)(2,1)S(1)}, bf16[8,32,1024]{2,1,0:T(8,128)(2,1)S(1)}, u32[]{:S(2)}, u32[]{:S(2)}) collective-permute-start(bf16[8,32,1024]{2,1,0:T(8,128)(2,1)S(1)} %all-to-all-done), channel_id=1, source_target_pairs={{0,1},{1,0},{2,3},{3,2},{4,5},{5,4},{6,7},{7,6},{8,9},{9,8},{10,11... | collective-permute-start | bytes 1572872 | tf_op jit(solution)/shard_map/ppermute | solution.py:87
  20.4 1.3 copy-start
  21.7 7.0 %copy-start.2 = (bf16[2048,512]{1,0:T(8,128)(2,1)S(1)}, bf16[2048,512]{1,0:T(8,128)(2,1)}, u32[]{:S(2)}) copy-start(bf16[2048,512]{1,0:T(8,128)(2,1)} %bitcast_multiply_fusion.2) | copy-start | bytes 6291460
  23.1 10.4 %collective-permute-start.4 = (f16[64,2048]{1,0:T(8,128)(2,1)S(1)}, f16[64,2048]{1,0:T(8,128)(2,1)S(1)}, u32[]{:S(2)}, u32[]{:S(2)}) collective-permute-start(f16[64,2048]{1,0:T(8,128)(2,1)S(1)} %get-tuple-element.73), channel_id=1, source_target_pairs={{0,224},{16,240},{32,0},{48,16},{64,32},{80,48},{96,64},{112,80},{... | collective-permute-start | bytes 786440 | tf_op jit(solution)/shard_map/ppermute | solution.py:27
  28.8 7.9 %collective-permute-start.3 = (f16[64,2048]{1,0:T(8,128)(2,1)S(1)}, f16[64,2048]{1,0:T(8,128)(2,1)S(1)}, u32[]{:S(2)}, u32[]{:S(2)}) collective-permute-start(f16[64,2048]{1,0:T(8,128)(2,1)S(1)} %get-tuple-element.74), channel_id=1, source_target_pairs={{0,32},{16,48},{32,64},{48,80},{64,96},{80,112},{96,128},{112,144}... | collective-permute-start | bytes 786440 | tf_op jit(solution)/shard_map/ppermute | solution.py:27
  30.2 9.0 %collective-permute-start.2 = (f16[64,2048]{1,0:T(8,128)(2,1)S(1)}, f16[64,2048]{1,0:T(8,128)(2,1)S(1)}, u32[]{:S(2)}, u32[]{:S(2)}) collective-permute-start(f16[64,2048]{1,0:T(8,128)(2,1)S(1)} %get-tuple-element.67), channel_id=1, source_target_pairs={{0,224},{16,240},{32,0},{48,16},{64,32},{80,48},{96,64},{112,80},{... | collective-permute-start | bytes 786440 | tf_op jit(solution)/shard_map/ppermute | solution.py:27
  32.9 9.6 %collective-permute-start.1 = (f16[64,2048]{1,0:T(8,128)(2,1)S(1)}, f16[64,2048]{1,0:T(8,128)(2,1)S(1)}, u32[]{:S(2)}, u32[]{:S(2)}) collective-permute-start(f16[64,2048]{1,0:T(8,128)(2,1)S(1)} %get-tuple-element.68), channel_id=1, source_target_pairs={{0,32},{16,48},{32,64},{48,80},{64,96},{80,112},{96,128},{112,144}... | collective-permute-start | bytes 786440 | tf_op jit(solution)/shard_map/ppermute | solution.py:27
  36.8 11.3 %collective-permute-start.7 = (f16[64,2048]{1,0:T(8,128)(2,1)S(1)}, f16[64,2048]{1,0:T(8,128)(2,1)S(1)}, u32[]{:S(2)}, u32[]{:S(2)}) collective-permute-start(f16[64,2048]{1,0:T(8,128)(2,1)S(1)} %get-tuple-element.72), channel_id=1, source_target_pairs={{0,32},{16,48},{32,64},{48,80},{64,96},{80,112},{96,128},{112,144}... | collective-permute-start | bytes 786440 | tf_op jit(solution)/shard_map/ppermute | solution.py:27
  42.5 5.5 %collective-permute-start.8 = (f16[64,2048]{1,0:T(8,128)(2,1)S(1)}, f16[64,2048]{1,0:T(8,128)(2,1)S(1)}, u32[]{:S(2)}, u32[]{:S(2)}) collective-permute-start(f16[64,2048]{1,0:T(8,128)(2,1)S(1)} %get-tuple-element.71), channel_id=1, source_target_pairs={{0,224},{16,240},{32,0},{48,16},{64,32},{80,48},{96,64},{112,80},{... | collective-permute-start | bytes 786440 | tf_op jit(solution)/shard_map/ppermute | solution.py:27
  42.7 10.0 %collective-permute-start.6 = (f16[64,2048]{1,0:T(8,128)(2,1)S(1)}, f16[64,2048]{1,0:T(8,128)(2,1)S(1)}, u32[]{:S(2)}, u32[]{:S(2)}) collective-permute-start(f16[64,2048]{1,0:T(8,128)(2,1)S(1)} %get-tuple-element.65), channel_id=1, source_target_pairs={{0,224},{16,240},{32,0},{48,16},{64,32},{80,48},{96,64},{112,80},{... | collective-permute-start | bytes 786440 | tf_op jit(solution)/shard_map/ppermute | solution.py:27
  42.8 10.4 %collective-permute-start.5 = (f16[64,2048]{1,0:T(8,128)(2,1)S(1)}, f16[64,2048]{1,0:T(8,128)(2,1)S(1)}, u32[]{:S(2)}, u32[]{:S(2)}) collective-permute-start(f16[64,2048]{1,0:T(8,128)(2,1)S(1)} %get-tuple-element.66), channel_id=1, source_target_pairs={{0,32},{16,48},{32,64},{48,80},{64,96},{80,112},{96,128},{112,144}... | collective-permute-start | bytes 786440 | tf_op jit(solution)/shard_map/ppermute | solution.py:27
  48.3 10.9 %collective-permute-start.11 = (f16[64,2048]{1,0:T(8,128)(2,1)S(1)}, f16[64,2048]{1,0:T(8,128)(2,1)S(1)}, u32[]{:S(2)}, u32[]{:S(2)}) collective-permute-start(f16[64,2048]{1,0:T(8,128)(2,1)S(1)} %get-tuple-element.70), channel_id=1, source_target_pairs={{0,32},{16,48},{32,64},{48,80},{64,96},{80,112},{96,128},{112,144}... | collective-permute-start | bytes 786440 | tf_op jit(solution)/shard_map/ppermute | solution.py:27
  53.2 6.0 %collective-permute-start.12 = (f16[64,2048]{1,0:T(8,128)(2,1)S(1)}, f16[64,2048]{1,0:T(8,128)(2,1)S(1)}, u32[]{:S(2)}, u32[]{:S(2)}) collective-permute-start(f16[64,2048]{1,0:T(8,128)(2,1)S(1)} %get-tuple-element.69), channel_id=1, source_target_pairs={{0,224},{16,240},{32,0},{48,16},{64,32},{80,48},{96,64},{112,80},{... | collective-permute-start | bytes 786440 | tf_op jit(solution)/shard_map/ppermute | solution.py:27
  54.5 8.9 %collective-permute-start.10 = (f16[64,2048]{1,0:T(8,128)(2,1)S(1)}, f16[64,2048]{1,0:T(8,128)(2,1)S(1)}, u32[]{:S(2)}, u32[]{:S(2)}) collective-permute-start(f16[64,2048]{1,0:T(8,128)(2,1)S(1)} %get-tuple-element.63), channel_id=1, source_target_pairs={{0,224},{16,240},{32,0},{48,16},{64,32},{80,48},{96,64},{112,80},{... | collective-permute-start | bytes 786440 | tf_op jit(solution)/shard_map/ppermute | solution.py:27
  54.6 9.3 %collective-permute-start.9 = (f16[64,2048]{1,0:T(8,128)(2,1)S(1)}, f16[64,2048]{1,0:T(8,128)(2,1)S(1)}, u32[]{:S(2)}, u32[]{:S(2)}) collective-permute-start(f16[64,2048]{1,0:T(8,128)(2,1)S(1)} %get-tuple-element.64), channel_id=1, source_target_pairs={{0,32},{16,48},{32,64},{48,80},{64,96},{80,112},{96,128},{112,144}... | collective-permute-start | bytes 786440 | tf_op jit(solution)/shard_map/ppermute | solution.py:27
  59.4 10.2 %collective-permute-start.15 = (f16[64,2048]{1,0:T(8,128)(2,1)S(1)}, f16[64,2048]{1,0:T(8,128)(2,1)S(1)}, u32[]{:S(2)}, u32[]{:S(2)}) collective-permute-start(f16[64,2048]{1,0:T(8,128)(2,1)S(1)} %fusion.5), channel_id=1, source_target_pairs={{0,32},{16,48},{32,64},{48,80},{64,96},{80,112},{96,128},{112,144}... | collective-permute-start | bytes 786440 | tf_op jit(solution)/shard_map/ppermute | solution.py:27
  64.0 8.4 %collective-permute-start.13 = (f16[64,2048]{1,0:T(8,128)(2,1)S(1)}, f16[64,2048]{1,0:T(8,128)(2,1)S(1)}, u32[]{:S(2)}, u32[]{:S(2)}) collective-permute-start(f16[64,2048]{1,0:T(8,128)(2,1)S(1)} %fusion.3), channel_id=1, source_target_pairs={{0,224},{16,240},{32,0},{48,16},{64,32},{80,48},{96,64},{112,80},{... | collective-permute-start | bytes 786440 | tf_op jit(solution)/shard_map/ppermute | solution.py:27
  69.7 6.8 %collective-permute-start.16 = (f16[64,2048]{1,0:T(8,128)(2,1)S(1)}, f16[64,2048]{1,0:T(8,128)(2,1)S(1)}, u32[]{:S(2)}, u32[]{:S(2)}) collective-permute-start(f16[64,2048]{1,0:T(8,128)(2,1)S(1)} %fusion.2), channel_id=1, source_target_pairs={{0,16},{16,0},{32,48},{48,32},{64,80},{80,64},{96,112},{112,96},{1... | collective-permute-start | bytes 786440 | tf_op jit(solution)/shard_map/ppermute | solution.py:31
  72.5 8.8 %collective-permute-start.14 = (f16[64,2048]{1,0:T(8,128)(2,1)S(1)}, f16[64,2048]{1,0:T(8,128)(2,1)S(1)}, u32[]{:S(2)}, u32[]{:S(2)}) collective-permute-start(f16[64,2048]{1,0:T(8,128)(2,1)S(1)} %fusion.14), channel_id=1, source_target_pairs={{0,16},{16,0},{32,48},{48,32},{64,80},{80,64},{96,112},{112,96},{1... | collective-permute-start | bytes 786440 | tf_op jit(solution)/shard_map/ppermute | solution.py:31
  81.7 6.5 %collective-permute-start.17 = (bf16[64,2048]{1,0:T(8,128)(2,1)S(1)}, bf16[64,2048]{1,0:T(8,128)(2,1)S(1)}, u32[]{:S(2)}, u32[]{:S(2)}) collective-permute-start(bf16[64,2048]{1,0:T(8,128)(2,1)S(1)} %get-tuple-element.62), channel_id=1, source_target_pairs={{0,32},{16,48},{32,64},{48,80},{64,96},{80,112},{96,128},{112,144}... | collective-permute-start | bytes 786440 | tf_op jit(solution)/shard_map/ppermute | solution.py:27
  81.8 6.4 %collective-permute-start.18 = (bf16[64,2048]{1,0:T(8,128)(2,1)S(1)}, bf16[64,2048]{1,0:T(8,128)(2,1)S(1)}, u32[]{:S(2)}, u32[]{:S(2)}) collective-permute-start(bf16[64,2048]{1,0:T(8,128)(2,1)S(1)} %get-tuple-element.62), channel_id=1, source_target_pairs={{0,224},{16,240},{32,0},{48,16},{64,32},{80,48},{96,64},{112,80},{... | collective-permute-start | bytes 786440 | tf_op jit(solution)/shard_map/ppermute | solution.py:27
  85.5 7.4 %collective-permute-start.25 = (bf16[64,2048]{1,0:T(8,128)(2,1)S(1)}, bf16[64,2048]{1,0:T(8,128)(2,1)S(1)}, u32[]{:S(2)}, u32[]{:S(2)}) collective-permute-start(bf16[64,2048]{1,0:T(8,128)(2,1)S(1)} %get-tuple-element.52), channel_id=1, source_target_pairs={{0,224},{16,240},{32,0},{48,16},{64,32},{80,48},{96,64},{112,80},{... | collective-permute-start | bytes 786440 | tf_op jit(solution)/shard_map/ppermute | solution.py:27
  85.6 8.8 %collective-permute-start.24 = (bf16[64,2048]{1,0:T(8,128)(2,1)S(1)}, bf16[64,2048]{1,0:T(8,128)(2,1)S(1)}, u32[]{:S(2)}, u32[]{:S(2)}) collective-permute-start(bf16[64,2048]{1,0:T(8,128)(2,1)S(1)} %get-tuple-element.52), channel_id=1, source_target_pairs={{0,32},{16,48},{32,64},{48,80},{64,96},{80,112},{96,128},{112,144}... | collective-permute-start | bytes 786440 | tf_op jit(solution)/shard_map/ppermute | solution.py:27
  88.2 10.3 %collective-permute-start.20 = (bf16[64,2048]{1,0:T(8,128)(2,1)S(1)}, bf16[64,2048]{1,0:T(8,128)(2,1)S(1)}, u32[]{:S(2)}, u32[]{:S(2)}) collective-permute-start(bf16[64,2048]{1,0:T(8,128)(2,1)S(1)} %collective-permute-done.18), channel_id=1, source_target_pairs={{0,224},{16,240},{32,0},{48,16},{64,32},{80,48},{96,64},{112,80},{... | collective-permute-start | bytes 786440 | tf_op jit(solution)/shard_map/ppermute | solution.py:27
  90.9 9.7 %collective-permute-start.19 = (bf16[64,2048]{1,0:T(8,128)(2,1)S(1)}, bf16[64,2048]{1,0:T(8,128)(2,1)S(1)}, u32[]{:S(2)}, u32[]{:S(2)}) collective-permute-start(bf16[64,2048]{1,0:T(8,128)(2,1)S(1)} %collective-permute-done.17), channel_id=1, source_target_pairs={{0,32},{16,48},{32,64},{48,80},{64,96},{80,112},{96,128},{112,144}... | collective-permute-start | bytes 786440 | tf_op jit(solution)/shard_map/ppermute | solution.py:27
  94.4 9.7 %collective-permute-start.26 = (bf16[64,2048]{1,0:T(8,128)(2,1)S(1)}, bf16[64,2048]{1,0:T(8,128)(2,1)S(1)}, u32[]{:S(2)}, u32[]{:S(2)}) collective-permute-start(bf16[64,2048]{1,0:T(8,128)(2,1)S(1)} %collective-permute-done.25), channel_id=1, source_target_pairs={{0,224},{16,240},{32,0},{48,16},{64,32},{80,48},{96,64},{112,80},{... | collective-permute-start | bytes 786440 | tf_op jit(solution)/shard_map/ppermute | solution.py:27
  94.4 9.7 %collective-permute-start.27 = (bf16[64,2048]{1,0:T(8,128)(2,1)S(1)}, bf16[64,2048]{1,0:T(8,128)(2,1)S(1)}, u32[]{:S(2)}, u32[]{:S(2)}) collective-permute-start(bf16[64,2048]{1,0:T(8,128)(2,1)S(1)} %collective-permute-done.24), channel_id=1, source_target_pairs={{0,32},{16,48},{32,64},{48,80},{64,96},{80,112},{96,128},{112,144}... | collective-permute-start | bytes 786440 | tf_op jit(solution)/shard_map/ppermute | solution.py:27
  100.6 9.2 %collective-permute-start.22 = (bf16[64,2048]{1,0:T(8,128)(2,1)S(1)}, bf16[64,2048]{1,0:T(8,128)(2,1)S(1)}, u32[]{:S(2)}, u32[]{:S(2)}) collective-permute-start(bf16[64,2048]{1,0:T(8,128)(2,1)S(1)} %collective-permute-done.20), channel_id=1, source_target_pairs={{0,224},{16,240},{32,0},{48,16},{64,32},{80,48},{96,64},{112,80},{... | collective-permute-start | bytes 786440 | tf_op jit(solution)/shard_map/ppermute | solution.py:27
  100.6 19.5 %copy-start.1 = (bf16[512,2048]{1,0:T(8,128)(2,1)S(1)}, bf16[512,2048]{1,0:T(8,128)(2,1)}, u32[]{:S(2)}) copy-start(bf16[512,2048]{1,0:T(8,128)(2,1)} %copy-done) | copy-start | bytes 6291460
  100.6 9.1 %collective-permute-start.21 = (bf16[64,2048]{1,0:T(8,128)(2,1)S(1)}, bf16[64,2048]{1,0:T(8,128)(2,1)S(1)}, u32[]{:S(2)}, u32[]{:S(2)}) collective-permute-start(bf16[64,2048]{1,0:T(8,128)(2,1)S(1)} %collective-permute-done.19), channel_id=1, source_target_pairs={{0,32},{16,48},{32,64},{48,80},{64,96},{80,112},{96,128},{112,144}... | collective-permute-start | bytes 786440 | tf_op jit(solution)/shard_map/ppermute | solution.py:27
  104.1 10.6 %collective-permute-start.28 = (bf16[64,2048]{1,0:T(8,128)(2,1)S(1)}, bf16[64,2048]{1,0:T(8,128)(2,1)S(1)}, u32[]{:S(2)}, u32[]{:S(2)}) collective-permute-start(bf16[64,2048]{1,0:T(8,128)(2,1)S(1)} %collective-permute-done.26), channel_id=1, source_target_pairs={{0,224},{16,240},{32,0},{48,16},{64,32},{80,48},{96,64},{112,80},{... | collective-permute-start | bytes 786440 | tf_op jit(solution)/shard_map/ppermute | solution.py:27
  106.0 8.8 %collective-permute-start.29 = (bf16[64,2048]{1,0:T(8,128)(2,1)S(1)}, bf16[64,2048]{1,0:T(8,128)(2,1)S(1)}, u32[]{:S(2)}, u32[]{:S(2)}) collective-permute-start(bf16[64,2048]{1,0:T(8,128)(2,1)S(1)} %collective-permute-done.27), channel_id=1, source_target_pairs={{0,32},{16,48},{32,64},{48,80},{64,96},{80,112},{96,128},{112,144}... | collective-permute-start | bytes 786440 | tf_op jit(solution)/shard_map/ppermute | solution.py:27
  109.7 10.4 %collective-permute-start.23 = (bf16[64,2048]{1,0:T(8,128)(2,1)S(1)}, bf16[64,2048]{1,0:T(8,128)(2,1)S(1)}, u32[]{:S(2)}, u32[]{:S(2)}) collective-permute-start(bf16[64,2048]{1,0:T(8,128)(2,1)S(1)} %collective-permute-done.22), channel_id=1, source_target_pairs={{0,224},{16,240},{32,0},{48,16},{64,32},{80,48},{96,64},{112,80},{... | collective-permute-start | bytes 786440 | tf_op jit(solution)/shard_map/ppermute | solution.py:27
  114.8 21.1 %collective-permute-start.30 = (bf16[64,2048]{1,0:T(8,128)(2,1)S(1)}, bf16[64,2048]{1,0:T(8,128)(2,1)}, u32[]{:S(2)}, u32[]{:S(2)}) collective-permute-start(bf16[64,2048]{1,0:T(8,128)(2,1)S(1)} %collective-permute-done.29), channel_id=1, source_target_pairs={{0,32},{16,48},{32,64},{48,80},{64,96},{80,112},{96,128},{112,144}... | collective-permute-start | bytes 786440 | tf_op jit(solution)/shard_map/ppermute | solution.py:27
  120.1 2.1 %copy-start.3 = (bf16[8,64,2048]{2,1,0:T(8,128)(2,1)}, bf16[8,64,2048]{2,1,0:T(8,128)(2,1)S(1)}, u32[]{:S(2)}) copy-start(bf16[8,64,2048]{2,1,0:T(8,128)(2,1)S(1)} %bitcast_dynamic-update-slice_fusion.7) | copy-start | bytes 6291460
  122.2 19.3 %all-to-all-start.1 = ((bf16[16,32,512]{2,1,0:T(8,128)(2,1)}), bf16[16,32,512]{2,1,0:T(8,128)(2,1)S(1)}, u32[]{:S(2)}, u32[]{:S(2)}) async-start(bf16[16,32,512]{2,1,0:T(8,128)(2,1)} %bitcast.145), calls=%async_computation.1 | async-start | bytes 1048576 | tf_op jit(solution)/shard_map/all_to_all | solution.py:152

commit v4 on v3

--- a/solution.py
+++ b/solution.py
@@ -98,7 +98,6 @@
     )
     pre_part = pre_part.reshape(depth, tokens // depth, -1)
     act_part = act_part.reshape(depth, tokens // depth, -1)
-    inputs_all, cotangent_all = together(inputs_all, cotangent_all)
 
     def p(d):
         return chunk_of(pre_part, z + d) * PRE_SCALE
@@ -117,6 +116,7 @@
         if step < far - 1:
             gu = (g(far - 1 - step) + gu.astype(F32)).astype(F16)
         gd = (g(-far + step) + gd.astype(F32)).astype(F16)
+    inputs_all, cotangent_all, _ = together(inputs_all, cotangent_all, pu)
     pu = send(pu, 1, rows)
     gd = send(gd, -1, rows)
     pre = (p(0) + pu.astype(F32) + pd.astype(F32)).astype(F16)

time: 143 us -> 143 us (level)
  no operation moved by 1% of the time
where the time goes in v4:
time: 143 us; the launch traced here: 142 us
  waiting for transfers between devices  69 us (48%)
  starting transfers between devices  48 us (34%)
  matrix products  7.96 us (6%)
  local copies, waits for them, and re-layouts  6.42 us (4%)
  other arithmetic  5.65 us (4%)
  Pallas kernels  4.21 us (3%)
    ppermute x28, waiting for transfers between devices, send(): return lax.ppermute(value, 'row', ring(shift, rows))  52.5 us
    ppermute x28, starting transfers between devices, send(): return lax.ppermute(value, 'row', ring(shift, rows))  28.3 us
    all_to_all x1, starting transfers between devices, shards(): pieces = lax.all_to_all(pieces, 'col', 0, 0)  9.44 us
    all_to_all x1, waiting for transfers between devices, shards(): mine = lax.all_to_all(mine, 'col', 0, 0, axis_index_groups=same_core)  7.76 us
    ppermute x2, waiting for transfers between devices, swap(): return lax.ppermute(value, 'row', [(r, r ^ 1) for r in range(rows)])  7.69 us
    all_to_all x1, starting transfers between devices, shards(): mine = lax.all_to_all(mine, 'col', 0, 0, axis_index_groups=same_core)  5.86 us
    pallas_call x1, Pallas kernels, grad_of_weight_in(): pl.pallas_call(weight_in_kernel, out_shape=jax.ShapeDtypeStruct((features...  4.21 us
    ppermute x2, starting transfers between devices, swap(): return lax.ppermute(value, 'row', [(r, r ^ 1) for r in range(rows)])  3.53 us
  transfers between devices with their start and end apart: 33, of which 27 were waited for; matrix products, arithmetic and copies ran while one was open for 10% of the time, Pallas kernels for 3%

profile of v4, /device:TPU:1, one launch (start us, length us, event | category | flops | bytes accessed | tf_op | source)
XLA Modules:
  0.0 142.2 jit_solution(4711140559143218493)
XLA Ops:
  0.7 0.8 pad_maximum_fusion.1
  1.4 0.9 broadcast_in_dim.59
  2.3 5.9 %all-to-all-start = ((bf16[8,32,1024]{2,1,0:T(8,128)(2,1)}), bf16[8,32,1024]{2,1,0:T(8,128)(2,1)S(1)}, u32[]{:S(2)}, u32[]{:S(2)}) async-start(bf16[8,32,1024]{2,1,0:T(8,128)(2,1)} %broadcast_in_dim.59), calls=%async_computation | async-start | bytes 1048576 | tf_op jit(solution)/shard_map/all_to_all | solution.py:86
  8.4 0.6 mul.145
  9.0 1.6 %bitcast_multiply_fusion.2 = bf16[2048,512]{1,0:T(8,128)(2,1)} fusion(bf16[2048,512]{1,0:T(8,128)(2,1)S(1)} %copy-done.4, bf16[256,8,4,128]{3,2,1,0:T(4,128)(2,1)S(1)} %bitcast.138), kind=kLoop, calls=%fused_computation.2 | loop fusion | flops 1048576 | bytes 6291456 | tf_op jit(solution)/shard_map/mul | solution.py:18
  10.6 7.8 %all-to-all-done = bf16[8,32,1024]{2,1,0:T(8,128)(2,1)S(1)} async-done(((bf16[8,32,1024]{2,1,0:T(8,128)(2,1)}), bf16[8,32,1024]{2,1,0:T(8,128)(2,1)S(1)}, u32[]{:S(2)}, u32[]{:S(2)}) %all-to-all-start) | async-done | bytes 524320 | tf_op jit(solution)/shard_map/all_to_all | solution.py:86
  18.4 0.8 collective-permute-start
  19.2 0.3 mul.156
  19.5 0.4 copy-done.5
  19.9 0.5 bitcast_multiply_fusion.1
  20.5 0.3 collective-permute-done
  20.9 0.8 copy-done
  21.7 1.3 fusion.19
  23.1 5.7 %collective-permute-start.4 = (f16[64,2048]{1,0:T(8,128)(2,1)S(1)}, f16[64,2048]{1,0:T(8,128)(2,1)S(1)}, u32[]{:S(2)}, u32[]{:S(2)}) collective-permute-start(f16[64,2048]{1,0:T(8,128)(2,1)S(1)} %get-tuple-element.73), channel_id=1, source_target_pairs={{0,224},{16,240},{32,0},{48,16},{64,32},{80,48},{96,64},{112,80},{... | collective-permute-start | bytes 786440 | tf_op jit(solution)/shard_map/ppermute | solution.py:27
  28.8 1.3 fusion.21
  30.2 2.7 %collective-permute-start.2 = (f16[64,2048]{1,0:T(8,128)(2,1)S(1)}, f16[64,2048]{1,0:T(8,128)(2,1)S(1)}, u32[]{:S(2)}, u32[]{:S(2)}) collective-permute-start(f16[64,2048]{1,0:T(8,128)(2,1)S(1)} %get-tuple-element.67), channel_id=1, source_target_pairs={{0,224},{16,240},{32,0},{48,16},{64,32},{80,48},{96,64},{112,80},{... | collective-permute-start | bytes 786440 | tf_op jit(solution)/shard_map/ppermute | solution.py:27
  32.9 0.6 collective-permute-done.4
  33.5 3.1 %collective-permute-done.3 = f16[64,2048]{1,0:T(8,128)(2,1)S(1)} collective-permute-done((f16[64,2048]{1,0:T(8,128)(2,1)S(1)}, f16[64,2048]{1,0:T(8,128)(2,1)S(1)}, u32[]{:S(2)}, u32[]{:S(2)}) %collective-permute-start.3) | collective-permute-done | bytes 262176 | tf_op jit(solution)/shard_map/ppermute | solution.py:27
  36.9 2.3 %collective-permute-done.2 = f16[64,2048]{1,0:T(8,128)(2,1)S(1)} collective-permute-done((f16[64,2048]{1,0:T(8,128)(2,1)S(1)}, f16[64,2048]{1,0:T(8,128)(2,1)S(1)}, u32[]{:S(2)}, u32[]{:S(2)}) %collective-permute-start.2) | collective-permute-done | bytes 262176 | tf_op jit(solution)/shard_map/ppermute | solution.py:27
  39.2 3.4 %collective-permute-done.1 = f16[64,2048]{1,0:T(8,128)(2,1)S(1)} collective-permute-done((f16[64,2048]{1,0:T(8,128)(2,1)S(1)}, f16[64,2048]{1,0:T(8,128)(2,1)S(1)}, u32[]{:S(2)}, u32[]{:S(2)}) %collective-permute-start.1) | collective-permute-done | bytes 262176 | tf_op jit(solution)/shard_map/ppermute | solution.py:27
  42.8 1.5 %collective-permute-start.5 = (f16[64,2048]{1,0:T(8,128)(2,1)S(1)}, f16[64,2048]{1,0:T(8,128)(2,1)S(1)}, u32[]{:S(2)}, u32[]{:S(2)}) collective-permute-start(f16[64,2048]{1,0:T(8,128)(2,1)S(1)} %get-tuple-element.66), channel_id=1, source_target_pairs={{0,32},{16,48},{32,64},{48,80},{64,96},{80,112},{96,128},{112,144}... | collective-permute-start | bytes 786440 | tf_op jit(solution)/shard_map/ppermute | solution.py:27
  44.3 3.7 %collective-permute-done.8 = f16[64,2048]{1,0:T(8,128)(2,1)S(1)} collective-permute-done((f16[64,2048]{1,0:T(8,128)(2,1)S(1)}, f16[64,2048]{1,0:T(8,128)(2,1)S(1)}, u32[]{:S(2)}, u32[]{:S(2)}) %collective-permute-start.8) | collective-permute-done | bytes 262176 | tf_op jit(solution)/shard_map/ppermute | solution.py:27
  48.3 0.3 collective-permute-start.11
  48.6 4.1 %collective-permute-done.6 = f16[64,2048]{1,0:T(8,128)(2,1)S(1)} collective-permute-done((f16[64,2048]{1,0:T(8,128)(2,1)S(1)}, f16[64,2048]{1,0:T(8,128)(2,1)S(1)}, u32[]{:S(2)}, u32[]{:S(2)}) %collective-permute-start.6) | collective-permute-done | bytes 262176 | tf_op jit(solution)/shard_map/ppermute | solution.py:27
  52.7 0.5 collective-permute-done.5
  53.2 1.1 collective-permute-start.12
  54.6 1.5 %collective-permute-start.9 = (f16[64,2048]{1,0:T(8,128)(2,1)S(1)}, f16[64,2048]{1,0:T(8,128)(2,1)S(1)}, u32[]{:S(2)}, u32[]{:S(2)}) collective-permute-start(f16[64,2048]{1,0:T(8,128)(2,1)S(1)} %get-tuple-element.64), channel_id=1, source_target_pairs={{0,32},{16,48},{32,64},{48,80},{64,96},{80,112},{96,128},{112,144}... | collective-permute-start | bytes 786440 | tf_op jit(solution)/shard_map/ppermute | solution.py:27
  56.0 3.2 %collective-permute-done.12 = f16[64,2048]{1,0:T(8,128)(2,1)S(1)} collective-permute-done((f16[64,2048]{1,0:T(8,128)(2,1)S(1)}, f16[64,2048]{1,0:T(8,128)(2,1)S(1)}, u32[]{:S(2)}, u32[]{:S(2)}) %collective-permute-start.12) | collective-permute-done | bytes 262176 | tf_op jit(solution)/shard_map/ppermute | solution.py:27
  59.5 4.0 %collective-permute-done.10 = f16[64,2048]{1,0:T(8,128)(2,1)S(1)} collective-permute-done((f16[64,2048]{1,0:T(8,128)(2,1)S(1)}, f16[64,2048]{1,0:T(8,128)(2,1)S(1)}, u32[]{:S(2)}, u32[]{:S(2)}) %collective-permute-start.10) | collective-permute-done | bytes 262176 | tf_op jit(solution)/shard_map/ppermute | solution.py:27
  63.4 0.5 collective-permute-done.9
  64.0 1.3 collective-permute-start.13
  65.3 4.2 %collective-permute-done.15 = f16[64,2048]{1,0:T(8,128)(2,1)S(1)} collective-permute-done((f16[64,2048]{1,0:T(8,128)(2,1)S(1)}, f16[64,2048]{1,0:T(8,128)(2,1)S(1)}, u32[]{:S(2)}, u32[]{:S(2)}) %collective-permute-start.15) | collective-permute-done | bytes 262176 | tf_op jit(solution)/shard_map/ppermute | solution.py:27
  69.7 2.7 %collective-permute-start.16 = (f16[64,2048]{1,0:T(8,128)(2,1)S(1)}, f16[64,2048]{1,0:T(8,128)(2,1)S(1)}, u32[]{:S(2)}, u32[]{:S(2)}) collective-permute-start(f16[64,2048]{1,0:T(8,128)(2,1)S(1)} %fusion.2), channel_id=1, source_target_pairs={{0,16},{16,0},{32,48},{48,32},{64,80},{80,64},{96,112},{112,96},{1... | collective-permute-start | bytes 786440 | tf_op jit(solution)/shard_map/ppermute | solution.py:31
  72.5 0.8 collective-permute-start.14
  73.3 3.1 %collective-permute-done.16 = f16[64,2048]{1,0:T(8,128)(2,1)S(1)} collective-permute-done((f16[64,2048]{1,0:T(8,128)(2,1)S(1)}, f16[64,2048]{1,0:T(8,128)(2,1)S(1)}, u32[]{:S(2)}, u32[]{:S(2)}) %collective-permute-start.16) | collective-permute-done | bytes 262176 | tf_op jit(solution)/shard_map/ppermute | solution.py:31
  76.5 0.3 add_multiply_fusion
  76.7 4.5 %collective-permute-done.14 = f16[64,2048]{1,0:T(8,128)(2,1)S(1)} collective-permute-done((f16[64,2048]{1,0:T(8,128)(2,1)S(1)}, f16[64,2048]{1,0:T(8,128)(2,1)S(1)}, u32[]{:S(2)}, u32[]{:S(2)}) %collective-permute-start.14) | collective-permute-done | bytes 262176 | tf_op jit(solution)/shard_map/ppermute | solution.py:31
  81.3 0.2 broadcast.53
  81.8 2.7 %collective-permute-start.18 = (bf16[64,2048]{1,0:T(8,128)(2,1)S(1)}, bf16[64,2048]{1,0:T(8,128)(2,1)S(1)}, u32[]{:S(2)}, u32[]{:S(2)}) collective-permute-start(bf16[64,2048]{1,0:T(8,128)(2,1)S(1)} %get-tuple-element.62), channel_id=1, source_target_pairs={{0,224},{16,240},{32,0},{48,16},{64,32},{80,48},{96,64},{112,80},{... | collective-permute-start | bytes 786440 | tf_op jit(solution)/shard_map/ppermute | solution.py:27
  84.4 0.9 fusion.23
  85.6 1.5 %collective-permute-start.24 = (bf16[64,2048]{1,0:T(8,128)(2,1)S(1)}, bf16[64,2048]{1,0:T(8,128)(2,1)S(1)}, u32[]{:S(2)}, u32[]{:S(2)}) collective-permute-start(bf16[64,2048]{1,0:T(8,128)(2,1)S(1)} %get-tuple-element.52), channel_id=1, source_target_pairs={{0,32},{16,48},{32,64},{48,80},{64,96},{80,112},{96,128},{112,144}... | collective-permute-start | bytes 786440 | tf_op jit(solution)/shard_map/ppermute | solution.py:27
  87.1 0.2 dynamic_update_slice.58
  87.3 0.9 collective-permute-done.17
  88.2 2.7 %collective-permute-start.20 = (bf16[64,2048]{1,0:T(8,128)(2,1)S(1)}, bf16[64,2048]{1,0:T(8,128)(2,1)S(1)}, u32[]{:S(2)}, u32[]{:S(2)}) collective-permute-start(bf16[64,2048]{1,0:T(8,128)(2,1)S(1)} %collective-permute-done.18), channel_id=1, source_target_pairs={{0,224},{16,240},{32,0},{48,16},{64,32},{80,48},{96,64},{112,80},{... | collective-permute-start | bytes 786440 | tf_op jit(solution)/shard_map/ppermute | solution.py:27
  91.0 1.9 %collective-permute-done.25 = bf16[64,2048]{1,0:T(8,128)(2,1)S(1)} collective-permute-done((bf16[64,2048]{1,0:T(8,128)(2,1)S(1)}, bf16[64,2048]{1,0:T(8,128)(2,1)S(1)}, u32[]{:S(2)}, u32[]{:S(2)}) %collective-permute-start.25) | collective-permute-done | bytes 262176 | tf_op jit(solution)/shard_map/ppermute | solution.py:27
  92.9 1.5 %collective-permute-done.24 = bf16[64,2048]{1,0:T(8,128)(2,1)S(1)} collective-permute-done((bf16[64,2048]{1,0:T(8,128)(2,1)S(1)}, bf16[64,2048]{1,0:T(8,128)(2,1)S(1)}, u32[]{:S(2)}, u32[]{:S(2)}) %collective-permute-start.24) | collective-permute-done | bytes 262176 | tf_op jit(solution)/shard_map/ppermute | solution.py:27
  94.4 1.4 collective-permute-start.27
  95.9 2.6 %collective-permute-done.20 = bf16[64,2048]{1,0:T(8,128)(2,1)S(1)} collective-permute-done((bf16[64,2048]{1,0:T(8,128)(2,1)S(1)}, bf16[64,2048]{1,0:T(8,128)(2,1)S(1)}, u32[]{:S(2)}, u32[]{:S(2)}) %collective-permute-start.20) | collective-permute-done | bytes 262176 | tf_op jit(solution)/shard_map/ppermute | solution.py:27
  98.5 2.1 %collective-permute-done.19 = bf16[64,2048]{1,0:T(8,128)(2,1)S(1)} collective-permute-done((bf16[64,2048]{1,0:T(8,128)(2,1)S(1)}, bf16[64,2048]{1,0:T(8,128)(2,1)S(1)}, u32[]{:S(2)}, u32[]{:S(2)}) %collective-permute-start.19) | collective-permute-done | bytes 262176 | tf_op jit(solution)/shard_map/ppermute | solution.py:27
  100.6 1.5 %collective-permute-start.21 = (bf16[64,2048]{1,0:T(8,128)(2,1)S(1)}, bf16[64,2048]{1,0:T(8,128)(2,1)S(1)}, u32[]{:S(2)}, u32[]{:S(2)}) collective-permute-start(bf16[64,2048]{1,0:T(8,128)(2,1)S(1)} %collective-permute-done.19), channel_id=1, source_target_pairs={{0,32},{16,48},{32,64},{48,80},{64,96},{80,112},{96,128},{112,144}... | collective-permute-start | bytes 786440 | tf_op jit(solution)/shard_map/ppermute | solution.py:27
  102.2 1.9 %collective-permute-done.26 = bf16[64,2048]{1,0:T(8,128)(2,1)S(1)} collective-permute-done((bf16[64,2048]{1,0:T(8,128)(2,1)S(1)}, bf16[64,2048]{1,0:T(8,128)(2,1)S(1)}, u32[]{:S(2)}, u32[]{:S(2)}) %collective-permute-start.26) | collective-permute-done | bytes 262176 | tf_op jit(solution)/shard_map/ppermute | solution.py:27
  104.1 1.9 %collective-permute-start.28 = (bf16[64,2048]{1,0:T(8,128)(2,1)S(1)}, bf16[64,2048]{1,0:T(8,128)(2,1)S(1)}, u32[]{:S(2)}, u32[]{:S(2)}) collective-permute-start(bf16[64,2048]{1,0:T(8,128)(2,1)S(1)} %collective-permute-done.26), channel_id=1, source_target_pairs={{0,224},{16,240},{32,0},{48,16},{64,32},{80,48},{96,64},{112,80},{... | collective-permute-start | bytes 786440 | tf_op jit(solution)/shard_map/ppermute | solution.py:27
  106.1 3.6 %collective-permute-done.22 = bf16[64,2048]{1,0:T(8,128)(2,1)S(1)} collective-permute-done((bf16[64,2048]{1,0:T(8,128)(2,1)S(1)}, bf16[64,2048]{1,0:T(8,128)(2,1)S(1)}, u32[]{:S(2)}, u32[]{:S(2)}) %collective-permute-start.22) | collective-permute-done | bytes 262176 | tf_op jit(solution)/shard_map/ppermute | solution.py:27
  109.7 1.9 %collective-permute-start.23 = (bf16[64,2048]{1,0:T(8,128)(2,1)S(1)}, bf16[64,2048]{1,0:T(8,128)(2,1)S(1)}, u32[]{:S(2)}, u32[]{:S(2)}) collective-permute-start(bf16[64,2048]{1,0:T(8,128)(2,1)S(1)} %collective-permute-done.22), channel_id=1, source_target_pairs={{0,224},{16,240},{32,0},{48,16},{64,32},{80,48},{96,64},{112,80},{... | collective-permute-start | bytes 786440 | tf_op jit(solution)/shard_map/ppermute | solution.py:27
  111.7 3.0 %collective-permute-done.28 = bf16[64,2048]{1,0:T(8,128)(2,1)S(1)} collective-permute-done((bf16[64,2048]{1,0:T(8,128)(2,1)S(1)}, bf16[64,2048]{1,0:T(8,128)(2,1)S(1)}, u32[]{:S(2)}, u32[]{:S(2)}) %collective-permute-start.28) | collective-permute-done | bytes 262176 | tf_op jit(solution)/shard_map/ppermute | solution.py:27
  114.9 5.2 %collective-permute-done.23 = bf16[64,2048]{1,0:T(8,128)(2,1)S(1)} collective-permute-done((bf16[64,2048]{1,0:T(8,128)(2,1)S(1)}, bf16[64,2048]{1,0:T(8,128)(2,1)S(1)}, u32[]{:S(2)}, u32[]{:S(2)}) %collective-permute-start.23) | collective-permute-done | bytes 262176 | tf_op jit(solution)/shard_map/ppermute | solution.py:27
  120.1 2.1 %convolution_convert_fusion = bf16[512,512]{1,0:T(8,128)(2,1)} fusion(bf16[512,2048]{1,0:T(8,128)(2,1)S(1)} %bitcast.140, bf16[512,2048]{1,0:T(8,128)(2,1)S(1)} %copy-done.1), kind=kOutput, calls=%fused_computation.3 | convolution fusion | flops 1074003968 | bytes 4718592 | tf_op jit(solution)/shard_map/dot_general | solution.py:148
  122.2 9.4 %all-to-all-start.1 = ((bf16[16,32,512]{2,1,0:T(8,128)(2,1)}), bf16[16,32,512]{2,1,0:T(8,128)(2,1)S(1)}, u32[]{:S(2)}, u32[]{:S(2)}) async-start(bf16[16,32,512]{2,1,0:T(8,128)(2,1)} %bitcast.145), calls=%async_computation.1 | async-start | bytes 1048576 | tf_op jit(solution)/shard_map/all_to_all | solution.py:152
  131.7 4.2 %shard_map.85 = f32[512,2048]{1,0:T(8,128)} custom-call(s32[4,16]{1,0:T(4,128)} %mask.1, bf16[512,512]{1,0:T(8,128)(2,1)} %get-tuple-element.51.x, bf16[512,2048]{1,0:T(8,128)(2,1)} %bitcast.141), custom_call_target="tpu_custom_call" | custom-call | flops 1073741824 | bytes 8388608 | tf_op jit(solution)/shard_map/pallas_call | solution.py:57
  135.9 1.0 bitcast_dynamic-update-slice_fusion
  136.8 0.6 mul.187
  137.4 3.3 %bitcast_multiply_fusion = f32[2048,512]{1,0:T(8,128)} fusion(f32[256,8,4,128]{3,2,1,0:T(4,128)S(1)} %bitcast.123, bf16[512,2048]{1,0:T(8,128)(2,1)S(1)} %bitcast.134, bf16[512,512]{1,0:T(8,128)(2,1)S(1)} %bitcast.142), kind=kOutput, calls=%fused_computation | convolution fusion | flops 1074790400 | bytes 11010048 | tf_op jit(solution)/shard_map/dot_general | solution.py:161
  140.8 0.8 all-to-all-done.1
  141.5 0.7 convert_reduce_fusion
  (67 shorter events, 3.2 us)
Async XLA Ops:
  0.6 7.5 %copy-start.6 = (s32[4,16]{1,0:T(4,128)S(1)}, s32[4,16]{1,0:T(4,128)}, u32[]{:S(2)}) copy-start(s32[4,16]{1,0:T(4,128)} %mask.1) | copy-start | bytes 772
  0.6 7.5 %copy-start.7 = (s32[16,4]{0,1:T(4,128)S(1)}, s32[16,4]{0,1:T(4,128)}, u32[]{:S(2)}) copy-start(s32[16,4]{0,1:T(4,128)} %param.11) | copy-start | bytes 772
  1.4 7.6 %copy-start.4 = (bf16[2048,512]{1,0:T(8,128)(2,1)S(1)}, bf16[2048,512]{1,0:T(8,128)(2,1)}, u32[]{:S(2)}) copy-start(bf16[2048,512]{1,0:T(8,128)(2,1)} %param.9) | copy-start | bytes 6291460
  2.3 16.1 %all-to-all-start = ((bf16[8,32,1024]{2,1,0:T(8,128)(2,1)}), bf16[8,32,1024]{2,1,0:T(8,128)(2,1)S(1)}, u32[]{:S(2)}, u32[]{:S(2)}) async-start(bf16[8,32,1024]{2,1,0:T(8,128)(2,1)} %broadcast_in_dim.59), calls=%async_computation | async-start | bytes 1048576 | tf_op jit(solution)/shard_map/all_to_all | solution.py:86
  18.4 1.6 %copy-start.5 = (bf16[512,2048]{1,0:T(8,128)(2,1)S(1)}, bf16[512,2048]{1,0:T(8,128)(2,1)}, u32[]{:S(2)}) copy-start(bf16[512,2048]{1,0:T(8,128)(2,1)} %param.8) | copy-start | bytes 6291460
  18.4 2.4 %collective-permute-start = (bf16[8,32,1024]{2,1,0:T(8,128)(2,1)S(1)}, bf16[8,32,1024]{2,1,0:T(8,128)(2,1)S(1)}, u32[]{:S(2)}, u32[]{:S(2)}) collective-permute-start(bf16[8,32,1024]{2,1,0:T(8,128)(2,1)S(1)} %all-to-all-done), channel_id=1, source_target_pairs={{0,1},{1,0},{2,3},{3,2},{4,5},{5,4},{6,7},{7,6},{8,9},{9,8},{10,11... | collective-permute-start | bytes 1572872 | tf_op jit(solution)/shard_map/ppermute | solution.py:87
  20.4 1.3 copy-start
  21.7 7.0 %copy-start.2 = (bf16[2048,512]{1,0:T(8,128)(2,1)S(1)}, bf16[2048,512]{1,0:T(8,128)(2,1)}, u32[]{:S(2)}) copy-start(bf16[2048,512]{1,0:T(8,128)(2,1)} %bitcast_multiply_fusion.2) | copy-start | bytes 6291460
  23.1 10.4 %collective-permute-start.4 = (f16[64,2048]{1,0:T(8,128)(2,1)S(1)}, f16[64,2048]{1,0:T(8,128)(2,1)S(1)}, u32[]{:S(2)}, u32[]{:S(2)}) collective-permute-start(f16[64,2048]{1,0:T(8,128)(2,1)S(1)} %get-tuple-element.73), channel_id=1, source_target_pairs={{0,224},{16,240},{32,0},{48,16},{64,32},{80,48},{96,64},{112,80},{... | collective-permute-start | bytes 786440 | tf_op jit(solution)/shard_map/ppermute | solution.py:27
  28.8 7.9 %collective-permute-start.3 = (f16[64,2048]{1,0:T(8,128)(2,1)S(1)}, f16[64,2048]{1,0:T(8,128)(2,1)S(1)}, u32[]{:S(2)}, u32[]{:S(2)}) collective-permute-start(f16[64,2048]{1,0:T(8,128)(2,1)S(1)} %get-tuple-element.74), channel_id=1, source_target_pairs={{0,32},{16,48},{32,64},{48,80},{64,96},{80,112},{96,128},{112,144}... | collective-permute-start | bytes 786440 | tf_op jit(solution)/shard_map/ppermute | solution.py:27
  30.2 9.0 %collective-permute-start.2 = (f16[64,2048]{1,0:T(8,128)(2,1)S(1)}, f16[64,2048]{1,0:T(8,128)(2,1)S(1)}, u32[]{:S(2)}, u32[]{:S(2)}) collective-permute-start(f16[64,2048]{1,0:T(8,128)(2,1)S(1)} %get-tuple-element.67), channel_id=1, source_target_pairs={{0,224},{16,240},{32,0},{48,16},{64,32},{80,48},{96,64},{112,80},{... | collective-permute-start | bytes 786440 | tf_op jit(solution)/shard_map/ppermute | solution.py:27
  32.9 9.6 %collective-permute-start.1 = (f16[64,2048]{1,0:T(8,128)(2,1)S(1)}, f16[64,2048]{1,0:T(8,128)(2,1)S(1)}, u32[]{:S(2)}, u32[]{:S(2)}) collective-permute-start(f16[64,2048]{1,0:T(8,128)(2,1)S(1)} %get-tuple-element.68), channel_id=1, source_target_pairs={{0,32},{16,48},{32,64},{48,80},{64,96},{80,112},{96,128},{112,144}... | collective-permute-start | bytes 786440 | tf_op jit(solution)/shard_map/ppermute | solution.py:27
  36.8 11.3 %collective-permute-start.7 = (f16[64,2048]{1,0:T(8,128)(2,1)S(1)}, f16[64,2048]{1,0:T(8,128)(2,1)S(1)}, u32[]{:S(2)}, u32[]{:S(2)}) collective-permute-start(f16[64,2048]{1,0:T(8,128)(2,1)S(1)} %get-tuple-element.72), channel_id=1, source_target_pairs={{0,32},{16,48},{32,64},{48,80},{64,96},{80,112},{96,128},{112,144}... | collective-permute-start | bytes 786440 | tf_op jit(solution)/shard_map/ppermute | solution.py:27
  42.5 5.5 %collective-permute-start.8 = (f16[64,2048]{1,0:T(8,128)(2,1)S(1)}, f16[64,2048]{1,0:T(8,128)(2,1)S(1)}, u32[]{:S(2)}, u32[]{:S(2)}) collective-permute-start(f16[64,2048]{1,0:T(8,128)(2,1)S(1)} %get-tuple-element.71), channel_id=1, source_target_pairs={{0,224},{16,240},{32,0},{48,16},{64,32},{80,48},{96,64},{112,80},{... | collective-permute-start | bytes 786440 | tf_op jit(solution)/shard_map/ppermute | solution.py:27
  42.7 10.0 %collective-permute-start.6 = (f16[64,2048]{1,0:T(8,128)(2,1)S(1)}, f16[64,2048]{1,0:T(8,128)(2,1)S(1)}, u32[]{:S(2)}, u32[]{:S(2)}) collective-permute-start(f16[64,2048]{1,0:T(8,128)(2,1)S(1)} %get-tuple-element.65), channel_id=1, source_target_pairs={{0,224},{16,240},{32,0},{48,16},{64,32},{80,48},{96,64},{112,80},{... | collective-permute-start | bytes 786440 | tf_op jit(solution)/shard_map/ppermute | solution.py:27
  42.8 10.4 %collective-permute-start.5 = (f16[64,2048]{1,0:T(8,128)(2,1)S(1)}, f16[64,2048]{1,0:T(8,128)(2,1)S(1)}, u32[]{:S(2)}, u32[]{:S(2)}) collective-permute-start(f16[64,2048]{1,0:T(8,128)(2,1)S(1)} %get-tuple-element.66), channel_id=1, source_target_pairs={{0,32},{16,48},{32,64},{48,80},{64,96},{80,112},{96,128},{112,144}... | collective-permute-start | bytes 786440 | tf_op jit(solution)/shard_map/ppermute | solution.py:27
  48.3 10.9 %collective-permute-start.11 = (f16[64,2048]{1,0:T(8,128)(2,1)S(1)}, f16[64,2048]{1,0:T(8,128)(2,1)S(1)}, u32[]{:S(2)}, u32[]{:S(2)}) collective-permute-start(f16[64,2048]{1,0:T(8,128)(2,1)S(1)} %get-tuple-element.70), channel_id=1, source_target_pairs={{0,32},{16,48},{32,64},{48,80},{64,96},{80,112},{96,128},{112,144}... | collective-permute-start | bytes 786440 | tf_op jit(solution)/shard_map/ppermute | solution.py:27
  53.2 6.0 %collective-permute-start.12 = (f16[64,2048]{1,0:T(8,128)(2,1)S(1)}, f16[64,2048]{1,0:T(8,128)(2,1)S(1)}, u32[]{:S(2)}, u32[]{:S(2)}) collective-permute-start(f16[64,2048]{1,0:T(8,128)(2,1)S(1)} %get-tuple-element.69), channel_id=1, source_target_pairs={{0,224},{16,240},{32,0},{48,16},{64,32},{80,48},{96,64},{112,80},{... | collective-permute-start | bytes 786440 | tf_op jit(solution)/shard_map/ppermute | solution.py:27
  54.5 8.9 %collective-permute-start.10 = (f16[64,2048]{1,0:T(8,128)(2,1)S(1)}, f16[64,2048]{1,0:T(8,128)(2,1)S(1)}, u32[]{:S(2)}, u32[]{:S(2)}) collective-permute-start(f16[64,2048]{1,0:T(8,128)(2,1)S(1)} %get-tuple-element.63), channel_id=1, source_target_pairs={{0,224},{16,240},{32,0},{48,16},{64,32},{80,48},{96,64},{112,80},{... | collective-permute-start | bytes 786440 | tf_op jit(solution)/shard_map/ppermute | solution.py:27
  54.6 9.3 %collective-permute-start.9 = (f16[64,2048]{1,0:T(8,128)(2,1)S(1)}, f16[64,2048]{1,0:T(8,128)(2,1)S(1)}, u32[]{:S(2)}, u32[]{:S(2)}) collective-permute-start(f16[64,2048]{1,0:T(8,128)(2,1)S(1)} %get-tuple-element.64), channel_id=1, source_target_pairs={{0,32},{16,48},{32,64},{48,80},{64,96},{80,112},{96,128},{112,144}... | collective-permute-start | bytes 786440 | tf_op jit(solution)/shard_map/ppermute | solution.py:27
  59.4 10.2 %collective-permute-start.15 = (f16[64,2048]{1,0:T(8,128)(2,1)S(1)}, f16[64,2048]{1,0:T(8,128)(2,1)S(1)}, u32[]{:S(2)}, u32[]{:S(2)}) collective-permute-start(f16[64,2048]{1,0:T(8,128)(2,1)S(1)} %fusion.5), channel_id=1, source_target_pairs={{0,32},{16,48},{32,64},{48,80},{64,96},{80,112},{96,128},{112,144}... | collective-permute-start | bytes 786440 | tf_op jit(solution)/shard_map/ppermute | solution.py:27
  64.0 8.4 %collective-permute-start.13 = (f16[64,2048]{1,0:T(8,128)(2,1)S(1)}, f16[64,2048]{1,0:T(8,128)(2,1)S(1)}, u32[]{:S(2)}, u32[]{:S(2)}) collective-permute-start(f16[64,2048]{1,0:T(8,128)(2,1)S(1)} %fusion.3), channel_id=1, source_target_pairs={{0,224},{16,240},{32,0},{48,16},{64,32},{80,48},{96,64},{112,80},{... | collective-permute-start | bytes 786440 | tf_op jit(solution)/shard_map/ppermute | solution.py:27
  69.7 6.8 %collective-permute-start.16 = (f16[64,2048]{1,0:T(8,128)(2,1)S(1)}, f16[64,2048]{1,0:T(8,128)(2,1)S(1)}, u32[]{:S(2)}, u32[]{:S(2)}) collective-permute-start(f16[64,2048]{1,0:T(8,128)(2,1)S(1)} %fusion.2), channel_id=1, source_target_pairs={{0,16},{16,0},{32,48},{48,32},{64,80},{80,64},{96,112},{112,96},{1... | collective-permute-start | bytes 786440 | tf_op jit(solution)/shard_map/ppermute | solution.py:31
  72.5 8.8 %collective-permute-start.14 = (f16[64,2048]{1,0:T(8,128)(2,1)S(1)}, f16[64,2048]{1,0:T(8,128)(2,1)S(1)}, u32[]{:S(2)}, u32[]{:S(2)}) collective-permute-start(f16[64,2048]{1,0:T(8,128)(2,1)S(1)} %fusion.14), channel_id=1, source_target_pairs={{0,16},{16,0},{32,48},{48,32},{64,80},{80,64},{96,112},{112,96},{1... | collective-permute-start | bytes 786440 | tf_op jit(solution)/shard_map/ppermute | solution.py:31
  81.7 6.5 %collective-permute-start.17 = (bf16[64,2048]{1,0:T(8,128)(2,1)S(1)}, bf16[64,2048]{1,0:T(8,128)(2,1)S(1)}, u32[]{:S(2)}, u32[]{:S(2)}) collective-permute-start(bf16[64,2048]{1,0:T(8,128)(2,1)S(1)} %get-tuple-element.62), channel_id=1, source_target_pairs={{0,32},{16,48},{32,64},{48,80},{64,96},{80,112},{96,128},{112,144}... | collective-permute-start | bytes 786440 | tf_op jit(solution)/shard_map/ppermute | solution.py:27
  81.8 6.4 %collective-permute-start.18 = (bf16[64,2048]{1,0:T(8,128)(2,1)S(1)}, bf16[64,2048]{1,0:T(8,128)(2,1)S(1)}, u32[]{:S(2)}, u32[]{:S(2)}) collective-permute-start(bf16[64,2048]{1,0:T(8,128)(2,1)S(1)} %get-tuple-element.62), channel_id=1, source_target_pairs={{0,224},{16,240},{32,0},{48,16},{64,32},{80,48},{96,64},{112,80},{... | collective-permute-start | bytes 786440 | tf_op jit(solution)/shard_map/ppermute | solution.py:27
  85.5 7.4 %collective-permute-start.25 = (bf16[64,2048]{1,0:T(8,128)(2,1)S(1)}, bf16[64,2048]{1,0:T(8,128)(2,1)S(1)}, u32[]{:S(2)}, u32[]{:S(2)}) collective-permute-start(bf16[64,2048]{1,0:T(8,128)(2,1)S(1)} %get-tuple-element.52), channel_id=1, source_target_pairs={{0,224},{16,240},{32,0},{48,16},{64,32},{80,48},{96,64},{112,80},{... | collective-permute-start | bytes 786440 | tf_op jit(solution)/shard_map/ppermute | solution.py:27
  85.6 8.8 %collective-permute-start.24 = (bf16[64,2048]{1,0:T(8,128)(2,1)S(1)}, bf16[64,2048]{1,0:T(8,128)(2,1)S(1)}, u32[]{:S(2)}, u32[]{:S(2)}) collective-permute-start(bf16[64,2048]{1,0:T(8,128)(2,1)S(1)} %get-tuple-element.52), channel_id=1, source_target_pairs={{0,32},{16,48},{32,64},{48,80},{64,96},{80,112},{96,128},{112,144}... | collective-permute-start | bytes 786440 | tf_op jit(solution)/shard_map/ppermute | solution.py:27
  88.2 10.3 %collective-permute-start.20 = (bf16[64,2048]{1,0:T(8,128)(2,1)S(1)}, bf16[64,2048]{1,0:T(8,128)(2,1)S(1)}, u32[]{:S(2)}, u32[]{:S(2)}) collective-permute-start(bf16[64,2048]{1,0:T(8,128)(2,1)S(1)} %collective-permute-done.18), channel_id=1, source_target_pairs={{0,224},{16,240},{32,0},{48,16},{64,32},{80,48},{96,64},{112,80},{... | collective-permute-start | bytes 786440 | tf_op jit(solution)/shard_map/ppermute | solution.py:27
  90.9 9.7 %collective-permute-start.19 = (bf16[64,2048]{1,0:T(8,128)(2,1)S(1)}, bf16[64,2048]{1,0:T(8,128)(2,1)S(1)}, u32[]{:S(2)}, u32[]{:S(2)}) collective-permute-start(bf16[64,2048]{1,0:T(8,128)(2,1)S(1)} %collective-permute-done.17), channel_id=1, source_target_pairs={{0,32},{16,48},{32,64},{48,80},{64,96},{80,112},{96,128},{112,144}... | collective-permute-start | bytes 786440 | tf_op jit(solution)/shard_map/ppermute | solution.py:27
  94.4 9.7 %collective-permute-start.26 = (bf16[64,2048]{1,0:T(8,128)(2,1)S(1)}, bf16[64,2048]{1,0:T(8,128)(2,1)S(1)}, u32[]{:S(2)}, u32[]{:S(2)}) collective-permute-start(bf16[64,2048]{1,0:T(8,128)(2,1)S(1)} %collective-permute-done.25), channel_id=1, source_target_pairs={{0,224},{16,240},{32,0},{48,16},{64,32},{80,48},{96,64},{112,80},{... | collective-permute-start | bytes 786440 | tf_op jit(solution)/shard_map/ppermute | solution.py:27
  94.4 9.7 %collective-permute-start.27 = (bf16[64,2048]{1,0:T(8,128)(2,1)S(1)}, bf16[64,2048]{1,0:T(8,128)(2,1)S(1)}, u32[]{:S(2)}, u32[]{:S(2)}) collective-permute-start(bf16[64,2048]{1,0:T(8,128)(2,1)S(1)} %collective-permute-done.24), channel_id=1, source_target_pairs={{0,32},{16,48},{32,64},{48,80},{64,96},{80,112},{96,128},{112,144}... | collective-permute-start | bytes 786440 | tf_op jit(solution)/shard_map/ppermute | solution.py:27
  100.6 9.2 %collective-permute-start.22 = (bf16[64,2048]{1,0:T(8,128)(2,1)S(1)}, bf16[64,2048]{1,0:T(8,128)(2,1)S(1)}, u32[]{:S(2)}, u32[]{:S(2)}) collective-permute-start(bf16[64,2048]{1,0:T(8,128)(2,1)S(1)} %collective-permute-done.20), channel_id=1, source_target_pairs={{0,224},{16,240},{32,0},{48,16},{64,32},{80,48},{96,64},{112,80},{... | collective-permute-start | bytes 786440 | tf_op jit(solution)/shard_map/ppermute | solution.py:27
  100.6 19.5 %copy-start.1 = (bf16[512,2048]{1,0:T(8,128)(2,1)S(1)}, bf16[512,2048]{1,0:T(8,128)(2,1)}, u32[]{:S(2)}) copy-start(bf16[512,2048]{1,0:T(8,128)(2,1)} %copy-done) | copy-start | bytes 6291460
  100.6 9.1 %collective-permute-start.21 = (bf16[64,2048]{1,0:T(8,128)(2,1)S(1)}, bf16[64,2048]{1,0:T(8,128)(2,1)S(1)}, u32[]{:S(2)}, u32[]{:S(2)}) collective-permute-start(bf16[64,2048]{1,0:T(8,128)(2,1)S(1)} %collective-permute-done.19), channel_id=1, source_target_pairs={{0,32},{16,48},{32,64},{48,80},{64,96},{80,112},{96,128},{112,144}... | collective-permute-start | bytes 786440 | tf_op jit(solution)/shard_map/ppermute | solution.py:27
  104.1 10.6 %collective-permute-start.28 = (bf16[64,2048]{1,0:T(8,128)(2,1)S(1)}, bf16[64,2048]{1,0:T(8,128)(2,1)S(1)}, u32[]{:S(2)}, u32[]{:S(2)}) collective-permute-start(bf16[64,2048]{1,0:T(8,128)(2,1)S(1)} %collective-permute-done.26), channel_id=1, source_target_pairs={{0,224},{16,240},{32,0},{48,16},{64,32},{80,48},{96,64},{112,80},{... | collective-permute-start | bytes 786440 | tf_op jit(solution)/shard_map/ppermute | solution.py:27
  106.0 8.8 %collective-permute-start.29 = (bf16[64,2048]{1,0:T(8,128)(2,1)S(1)}, bf16[64,2048]{1,0:T(8,128)(2,1)S(1)}, u32[]{:S(2)}, u32[]{:S(2)}) collective-permute-start(bf16[64,2048]{1,0:T(8,128)(2,1)S(1)} %collective-permute-done.27), channel_id=1, source_target_pairs={{0,32},{16,48},{32,64},{48,80},{64,96},{80,112},{96,128},{112,144}... | collective-permute-start | bytes 786440 | tf_op jit(solution)/shard_map/ppermute | solution.py:27
  109.7 10.4 %collective-permute-start.23 = (bf16[64,2048]{1,0:T(8,128)(2,1)S(1)}, bf16[64,2048]{1,0:T(8,128)(2,1)S(1)}, u32[]{:S(2)}, u32[]{:S(2)}) collective-permute-start(bf16[64,2048]{1,0:T(8,128)(2,1)S(1)} %collective-permute-done.22), channel_id=1, source_target_pairs={{0,224},{16,240},{32,0},{48,16},{64,32},{80,48},{96,64},{112,80},{... | collective-permute-start | bytes 786440 | tf_op jit(solution)/shard_map/ppermute | solution.py:27
  114.8 21.1 %collective-permute-start.30 = (bf16[64,2048]{1,0:T(8,128)(2,1)S(1)}, bf16[64,2048]{1,0:T(8,128)(2,1)}, u32[]{:S(2)}, u32[]{:S(2)}) collective-permute-start(bf16[64,2048]{1,0:T(8,128)(2,1)S(1)} %collective-permute-done.29), channel_id=1, source_target_pairs={{0,32},{16,48},{32,64},{48,80},{64,96},{80,112},{96,128},{112,144}... | collective-permute-start | bytes 786440 | tf_op jit(solution)/shard_map/ppermute | solution.py:27
  120.1 2.1 %copy-start.3 = (bf16[8,64,2048]{2,1,0:T(8,128)(2,1)}, bf16[8,64,2048]{2,1,0:T(8,128)(2,1)S(1)}, u32[]{:S(2)}) copy-start(bf16[8,64,2048]{2,1,0:T(8,128)(2,1)S(1)} %bitcast_dynamic-update-slice_fusion.7) | copy-start | bytes 6291460
  122.2 19.3 %all-to-all-start.1 = ((bf16[16,32,512]{2,1,0:T(8,128)(2,1)}), bf16[16,32,512]{2,1,0:T(8,128)(2,1)S(1)}, u32[]{:S(2)}, u32[]{:S(2)}) async-start(bf16[16,32,512]{2,1,0:T(8,128)(2,1)} %bitcast.145), calls=%async_computation.1 | async-start | bytes 1048576 | tf_op jit(solution)/shard_map/all_to_all | solution.py:152
